TPU v7x, 32 devices: a whole 2x2x4 slice. The times are simulated.
32 devices in a mesh: outer: 4 (over y, x), inner: 8 (over z, core).
Axes of the slice: x: 2, y: 2, z: 4, core: 2. Of those that a mesh axis runs over, the one named last changes fastest.
Arguments:
- tokens: bfloat16 [4096, 4096], P('inner', 'outer'), may hold values from -6 to 6
- cotangent: bfloat16 [4096, 4096], P('inner', 'outer'), may hold values from -0.09375 to 0.09375
- weight_cache: bfloat16 [4096, 4096], P(None, 'outer'), may hold values from -0.09375 to 0.09375
- weight_delta: bfloat16 [4096, 4096], P('inner', 'outer'), may hold values from -0.078125 to 0.078125
- sign_bits: int32 [4096], P('outer'), may hold values from 0 to 1
- master: float32 [4096, 4096], P('inner', 'outer'), may hold values from -1.5 to 1.5
- moment: float32 [4096, 4096], P('inner', 'outer'), may hold values from -6 to 6
- variance: float32 [4096, 4096], P('inner', 'outer'), may hold values from 0.25 to 4
Outputs:
- activation: float32 [4096, 4096], P('inner', 'outer')
- new_master: float32 [4096, 4096], P('inner', 'outer')
- new_moment: float32 [4096, 4096], P('inner', 'outer')
- new_variance: float32 [4096, 4096], P('inner', 'outer')
- block_scales: float32 [4096, 32], P('inner', 'outer')
All inputs are finite; a program needn't handle non-finite values.
Results may differ from a plain program's by a relative error of at most 0.003.
Values may be sent and summed in bfloat16 or wider, within the bound.
No kernel may reach another device: no remote copies, remote signals or barrier semaphores. Data moves between devices by JAX's collectives and lax.ppermute only.
A program may use at most 128 MiB of HBM per device.

v0:
```python
import jax
import jax.numpy as jnp
from jax import lax
from jax.experimental import pallas as pl
from jax.sharding import PartitionSpec as P


BLOCK = 128
PARTS = 2


def sign_table(length):
    first = jnp.arange(length, dtype=jnp.int32)[:, None]
    second = jnp.arange(length, dtype=jnp.int32)[None, :]
    common = jnp.bitwise_and(first, second)
    parity = jnp.zeros((length, length), jnp.int32)
    for place in range(length.bit_length() - 1):
        parity = parity + jnp.bitwise_and(jnp.right_shift(common, place), 1)
    return 1 - 2 * (parity % 2)


def finish_kernel(signs, table, kept, own, first, second, master, moment, variance, *rest):
    new_master, new_moment, new_variance, scales = rest[-4:]
    step = pl.program_id(0)
    gradient = own[...]
    for line, received in enumerate((first, second)):
        wanted = kept[:, line : line + 1] > 0.0
        gradient = gradient + jnp.where(wanted, received[...].astype(jnp.float32), 0.0)
    first = 0.9 * moment[...] + 0.1 * gradient
    second = 0.95 * variance[...] + 0.05 * gradient * gradient
    corrected = first / (1.0 - 0.9**10)
    spread = jnp.sqrt(second / (1.0 - 0.95**10)) + 1e-08
    new_moment[...] = first
    new_variance[...] = second
    new_master[...] = master[...] - 0.01 * (corrected / spread + 0.1 * master[...])
    for place in range(gradient.shape[1] // BLOCK):
        columns = slice(place * BLOCK, (place + 1) * BLOCK)
        signed = gradient[:, columns] * signs[:, columns]
        high = signed.astype(jnp.bfloat16)
        low = (signed - high.astype(jnp.float32)).astype(jnp.bfloat16)
        mixed = sum(
            lax.dot_general(
                table[...], term, (((1,), (1,)), ((), ())), preferred_element_type=jnp.float32
            )
            for term in (high, low)
        )
        largest = jnp.max(jnp.abs(mixed), axis=0, keepdims=True)
        row = step * (gradient.shape[1] // BLOCK) + place
        scales[pl.ds(row, 1), :] = largest * (1.0 / BLOCK**0.5)


def finish(
    part, parts, signs, table, kept, own, first, second, master, moment, variance, before
):
    rows, width = master.shape
    size = rows // parts
    tile = min(width, 512)
    whole = pl.BlockSpec((size, tile), lambda k: (part, k))
    piece = pl.BlockSpec((size, tile), lambda k: (0, k))
    given = [
        pl.BlockSpec((1, tile), lambda k: (0, k)),
        pl.BlockSpec((BLOCK, BLOCK), lambda k: (0, 0)),
        pl.BlockSpec((1, 2), lambda k: (0, 0)),
        whole,
        piece,
        piece,
        whole,
        whole,
        whole,
    ]
    held = [pl.BlockSpec(memory_space=pl.ANY)] * len(before)
    return pl.pallas_call(
        finish_kernel,
        grid=(width // tile,),
        in_specs=given + held,
        out_specs=[
            whole,
            whole,
            whole,
            pl.BlockSpec((width // BLOCK, size), lambda k: (0, part)),
        ],
        out_shape=[jax.ShapeDtypeStruct(master.shape, jnp.float32)] * 3
        + [jax.ShapeDtypeStruct((width // BLOCK, rows), jnp.float32)],
        input_output_aliases={len(given) + k: k for k in range(len(before))},
    )(signs, table, kept, own, first, second, master, moment, variance, *before)


def gather_tokens(lows, highs, outer):
    parts = len(lows)
    if outer != 4:
        every = []
        for which, pieces in enumerate((lows, highs)):
            for part, piece in enumerate(pieces):
                whole = lax.all_gather(piece, "outer", axis=0, tiled=False)
                every += [(whole[k], which, part, k) for k in range(outer)]
        return every, None
    me = lax.axis_index("outer")
    even = (me == 0) | (me == 3)

    def across(value, distance):
        return lax.ppermute(value, "outer", [(k, k ^ distance) for k in range(outer)])

    near, far, corner = me ^ 1, me ^ 2, me ^ 3
    near_low = [across(lows[k], 1) for k in range(parts)]
    far_high = [across(highs[k], 2) for k in range(parts)]
    second_near = [across(jnp.where(even, highs[k], far_high[k]), 1) for k in range(parts)]
    second_far = [across(jnp.where(even, lows[k], near_low[k]), 2) for k in range(parts)]
    all_of = [jnp.concatenate(pieces, axis=1) for pieces in (lows, highs, near_low, far_high)]
    third_near = across(jnp.where(even, all_of[3], all_of[1]), 1)
    third_far = across(jnp.where(even, all_of[2], all_of[0]), 2)

    def end_block(owner, part):
        one = jnp.where(
            owner == me,
            lows[part],
            jnp.where(owner == near, near_low[part], second_far[part]),
        )
        two = jnp.where(
            owner == me,
            highs[part],
            jnp.where(owner == far, far_high[part], second_near[part]),
        )
        return one, two

    every = []
    for k in range(parts):
        every += [
            (lows[k], 0, k, me),
            (highs[k], 1, k, me),
            (near_low[k], 0, k, near),
            (far_high[k], 1, k, far),
            (second_near[k], 1, k, jnp.where(even, corner, near)),
            (second_far[k], 0, k, jnp.where(even, corner, far)),
        ]
    every += [
        (third_near, 1, 0, jnp.where(even, near, corner)),
        (third_far, 0, 0, jnp.where(even, far, corner)),
    ]
    return every, end_block


def contract(left, right):
    return lax.dot_general(
        left, right, (((0,), (0,)), ((), ())), preferred_element_type=jnp.float32
    )


def make_body(outer, inner):
    chips = inner // 2
    swap_pairs = [(k, k ^ 1) for k in range(inner)]
    up, down = [], []
    for z in range(chips - 1):
        up.append([(2 * z, 2 * z + 2), (2 * z + 1, 2 * z + 3)])
        down.append([(2 * z + 2, 2 * z), (2 * z + 3, 2 * z + 1)])
    top = 2 * chips - 2
    line_pairs = (
        [pair[0] for pair in up] + [pair[1] for pair in down] + [(top, top + 1), (1, 0)],
        [pair[1] for pair in up] + [pair[0] for pair in down] + [(top + 1, top), (0, 1)],
    )

    def swap(value):
        return lax.ppermute(value, "inner", swap_pairs)

    def along(line, value):
        return lax.ppermute(value, "inner", line_pairs[line])

    def body(tokens, cotangent, weight_cache, weight_delta, sign_bits, master, moment, variance):
        index = lax.axis_index("inner")
        chip, core = index // 2, index % 2
        rows, width = master.shape
        count, wide = tokens.shape
        group = wide // (2 * rows)
        signs = (1 - 2 * sign_bits).astype(jnp.float32)[None, :]
        table = sign_table(BLOCK).astype(jnp.bfloat16)
        upward = (core == 0, core == 1)

        def turned(line, position):
            return jnp.where(upward[line], position, chips - 1 - position)

        places = [turned(line, chip) for line in (0, 1)]

        parts = max(1, min(PARTS, rows // 128))
        size = rows // parts

        def columns_of(core_index, part):
            starts = [(2 * k + core_index) * rows + part * size for k in range(group)]
            return jnp.concatenate(
                [lax.dynamic_slice(tokens, (0, start), (count, size)) for start in starts],
                axis=1,
            )

        cut = [columns_of(which, part) for which in (core, 1 - core) for part in range(parts)]
        cut = lax.optimization_barrier(cut)
        lows = cut[:parts]
        highs = [swap(cut[parts + k]) for k in range(parts)]
        pieces, end_block = gather_tokens(lows, highs, outer)
        if chips != outer:
            end_block = None
        kept = [jnp.where(place == 0, 0.0, 1.0) for place in places]
        kept = jnp.stack(kept).astype(jnp.float32).reshape(1, 2)
        signs, table, kept, cotangent = lax.optimization_barrier((signs, table, kept, cotangent))
        cotangent_other = swap(cotangent)
        cotangents = jnp.concatenate([cotangent, cotangent_other], axis=0)
        held = jnp.zeros((outer, 2 * count, group, rows), tokens.dtype)
        for piece, which, part, owner in pieces:
            piece = piece.reshape(1, count, group, -1)
            held = lax.dynamic_update_slice(
                held, piece, (owner, which * count, 0, part * size)
            )
        held = held.reshape(outer, 2 * count, group * rows)

        def tokens_for(chip_index, which=None):
            first, size = (0, 2 * count) if which is None else (which * count, count)
            return lax.dynamic_slice(
                held,
                (chip_index // group, first, lax.rem(chip_index, group) * rows),
                (1, size, rows),
            )[0]

        def partial_sum(chip_index):
            return contract(tokens_for(chip_index), cotangents)

        def product(chip_index, delta, cache):
            cached = lax.dynamic_slice(cache, ((2 * chip_index + core) * rows, 0), (rows, width))
            weight = cached.astype(jnp.float32) + delta.astype(jnp.float32)
            weight = lax.optimization_barrier(weight.astype(jnp.bfloat16))
            return [
                jnp.dot(tokens_for(chip_index, which), weight, preferred_element_type=jnp.float32)
                for which in (0, 1)
            ]

        message = [[weight_delta], [weight_delta]]
        history = ([], [])
        cache = weight_cache
        caches = [cache]
        for turn in range(1, chips):
            terms = []
            for line in (0, 1):
                history[line].append([along(line, value) for value in message[line]])
                if turn > 1 or end_block is None:
                    target = turned(line, lax.rem(places[line] - turn + chips, chips))
                    term = partial_sum(target)
                    term = jnp.where(turn <= places[line], jnp.float32(0), term)
                    terms.append(lax.optimization_barrier(term))
            message = [[], []]
            for k in range(parts):
                rows_of = slice(k * size, (k + 1) * size)
                for line in (0, 1):
                    received, place = history[line][-1], places[line]
                    if terms:
                        term = terms[line][rows_of]
                    else:
                        one, two = end_block(turned(line, chips - 1), k)
                        term = contract(one, cotangent) + contract(two, cotangent_other)
                        term = jnp.where(turn <= place, jnp.float32(0), term)
                    before = received[0][rows_of] if len(received) == 1 else received[k]
                    before = jnp.where(place == 0, jnp.bfloat16(0), before)
                    value = (before.astype(jnp.float32) + term).astype(jnp.bfloat16)
                    cache, value, cotangent_other, *terms = lax.optimization_barrier(
                        (cache, value, cotangent_other, *terms)
                    )
                    message[line].append(value)
            caches.append(cache)

        last = [[along(line, message[line][k]) for line in (0, 1)] for k in range(parts)]
        own = lax.optimization_barrier(partial_sum(chip))

        mine, other = product(chip, weight_delta, caches[min(2, chips - 1)])
        order = sorted(range(1, chips), key=lambda t: max(t, chips - t))
        products = []
        for number, turn in enumerate(order, 1):
            passed = [history[0][turn - 1], history[1][chips - turn - 1]]
            most = max(len(value) for value in passed)
            for line in (0, 1):
                if len(passed[line]) < most:
                    whole = passed[line][0]
                    passed[line] = [
                        whole[k * size : (k + 1) * size] for k in range(most)
                    ]
            delta = jnp.concatenate(
                [jnp.where(turn <= places[0], one, two) for one, two in zip(*passed)], axis=0
            )
            source = turned(0, lax.rem(places[0] - turn + chips, chips))
            one, two = product(source, delta, caches[max(turn, chips - turn)])
            other = other + two
            products.append((number, one))
        theirs = swap(other)
        for number, one in products:
            mine = lax.optimization_barrier(mine)
            if number == chips - 1:
                mine = mine + theirs
            mine = mine + one
        output = mine

        done = []
        for k in range(parts):
            done = finish(
                k, parts, signs, table, kept, own, *last[k], master, moment, variance, done
            )
        new_master, new_moment, new_variance, scales = done
        return (output, new_master, new_moment, new_variance, scales.T)

    return body


def solution(mesh):
    placed = (
        P("inner", "outer"),
        P("inner", "outer"),
        P(None, "outer"),
        P("inner", "outer"),
        P("outer"),
        P("inner", "outer"),
        P("inner", "outer"),
        P("inner", "outer"),
    )
    return jax.shard_map(
        make_body(mesh.shape["outer"], mesh.shape["inner"]),
        mesh=mesh,
        in_specs=placed,
        out_specs=(
            P("inner", "outer"),
            P("inner", "outer"),
            P("inner", "outer"),
            P("inner", "outer"),
            P("inner", "outer"),
        ),
        check_vma=False,
    )
```

profile of v0, /device:TPU:0, one launch (start us, length us, event | category | flops | bytes accessed | tf_op | source)
XLA Modules:
  0.0 169.2 jit_solution(15675314849789961037)
XLA Ops:
  1.3 1.3 subtract_convert_fusion
  3.7 2.2 %constant_dynamic-slice_fusion = (bf16[512,256]{1,0:T(8,128)(2,1)}, bf16[512,256]{1,0:T(8,128)(2,1)}, bf16[512,256]{1,0:T(8,128)(2,1)}, bf16[512,256]{1,0:T(8,128)(2,1)}) fusion(bf16[512,1024]{1,0:T(8,128)(2,1)} %param.8, s32[]{:T(128)S(6)} %select_n.417, s32[]{:T(128)S(6)} %select_n.415, s32[]{:T(128)S(6)} %select_n.414, s32[]{:T(128)S(6)} %select_n.416), kind=kLoop, calls=%fused_computation.148 | loop fusion | bytes 2097168 | tf_op jit(solution)/shard_map/dynamic_slice | solution.py:188
  5.9 3.0 %collective-permute-start.1 = (bf16[512,256]{1,0:T(8,128)(2,1)}, bf16[512,256]{1,0:T(8,128)(2,1)}, u32[]{:S(2)}, u32[]{:S(2)}) collective-permute-start(bf16[512,256]{1,0:T(8,128)(2,1)} %get-tuple-element.58), channel_id=1, source_target_pairs={{0,8},{8,0},{16,24},{24,16},{1,9},{9,1},{17,25},{25,17},{2,10},{10... | collective-permute-start | bytes 786440 | tf_op jit(solution)/shard_map/ppermute | solution.py:101
  8.9 2.3 %reshape.100 = bf16[4,1024,512]{2,1,0:T(8,128)(2,1)} broadcast(bf16[]{:T(256)} %constant.161.clone.1), dimensions={} | broadcast | bytes 4194306 | tf_op jit(solution)/shard_map/reshape | solution.py:210
  11.2 1.7 bitcast_dynamic-update-slice_fusion.13
  13.2 3.1 %collective-permute-done.1 = bf16[512,256]{1,0:T(8,128)(2,1)} collective-permute-done((bf16[512,256]{1,0:T(8,128)(2,1)}, bf16[512,256]{1,0:T(8,128)(2,1)}, u32[]{:S(2)}, u32[]{:S(2)}) %collective-permute-start.1) | collective-permute-done | bytes 262176 | tf_op jit(solution)/shard_map/ppermute | solution.py:101
  16.3 2.1 %collective-permute-start.12 = (bf16[512,1024]{1,0:T(8,128)(2,1)}, bf16[512,1024]{1,0:T(8,128)(2,1)S(1)}, u32[]{:S(2)}, u32[]{:S(2)}) collective-permute-start(bf16[512,1024]{1,0:T(8,128)(2,1)} %param.11), channel_id=1, source_target_pairs={{0,2},{2,4},{4,6},{3,1},{5,3},{7,5},{6,7},{1,0},{8,10},{10,12},{12... | collective-permute-start | bytes 3145736 | tf_op jit(solution)/shard_map/ppermute | solution.py:165
  18.4 1.0 broadcast_select_fusion.8
  19.5 1.6 collective-permute-start.2
  21.2 1.8 %collective-permute-start.7 = (bf16[512,256]{1,0:T(8,128)(2,1)S(1)}, bf16[512,256]{1,0:T(8,128)(2,1)S(1)}, u32[]{:S(2)}, u32[]{:S(2)}) collective-permute-start(bf16[512,256]{1,0:T(8,128)(2,1)S(1)} %collective-permute-done.5), channel_id=1, source_target_pairs={{0,16},{8,24},{16,0},{24,8},{1,17},{9,25},{17,1},{25,9},{2,18},{10... | collective-permute-start | bytes 786440 | tf_op jit(solution)/shard_map/ppermute | solution.py:101
  23.0 1.0 broadcast_select_fusion.6
  24.0 1.7 bitcast_dynamic-update-slice_fusion.12
  25.7 1.7 bitcast_dynamic-update-slice_fusion.11
  27.4 1.3 maximum_select_fusion.1
  28.9 1.5 collective-permute-start.4
  30.4 1.0 broadcast_select_fusion.9
  31.4 2.9 %collective-permute-done.7 = bf16[512,256]{1,0:T(8,128)(2,1)S(1)} collective-permute-done((bf16[512,256]{1,0:T(8,128)(2,1)S(1)}, bf16[512,256]{1,0:T(8,128)(2,1)S(1)}, u32[]{:S(2)}, u32[]{:S(2)}) %collective-permute-start.7) | collective-permute-done | bytes 262176 | tf_op jit(solution)/shard_map/ppermute | solution.py:101
  34.3 1.7 collective-permute-start.3
  36.0 0.8 bitcast_dynamic-update-slice_fusion.10
  36.8 1.1 maximum_select_fusion
  37.9 2.9 %collective-permute-done.3 = bf16[512,256]{1,0:T(8,128)(2,1)S(1)} collective-permute-done((bf16[512,256]{1,0:T(8,128)(2,1)S(1)}, bf16[512,256]{1,0:T(8,128)(2,1)S(1)}, u32[]{:S(2)}, u32[]{:S(2)}) %collective-permute-start.3) | collective-permute-done | bytes 262176 | tf_op jit(solution)/shard_map/ppermute | solution.py:101
  40.7 3.2 %collective-permute-start.9 = (bf16[512,256]{1,0:T(8,128)(2,1)S(1)}, bf16[512,256]{1,0:T(8,128)(2,1)S(1)}, u32[]{:S(2)}, u32[]{:S(2)}) collective-permute-start(bf16[512,256]{1,0:T(8,128)(2,1)S(1)} %broadcast_select_fusion.6), channel_id=1, source_target_pairs={{0,16},{8,24},{16,0},{24,8},{1,17},{9,25},{17,1},{25,9},{2,18},{10... | collective-permute-start | bytes 786440 | tf_op jit(solution)/shard_map/ppermute | solution.py:101
  44.6 1.3 collective-permute-start.8
  46.6 1.7 %bitcast_dynamic-update-slice_fusion.7 = bf16[4,1024,512]{2,1,0:T(8,128)(2,1)} fusion(bf16[4,1024,512]{2,1,0:T(8,128)(2,1)} %bitcast_dynamic-update-slice_fusion.8, s32[]{:T(128)S(6)} %select_n.418, bf16[512,256]{1,0:T(8,128)(2,1)} %get-tuple-element.60), kind=kLoop, calls=%fused_computation.81 | loop fusion | bytes 524292 | tf_op jit(solution)/shard_map/dynamic_update_slice | solution.py:207
  49.1 1.7 bitcast_dynamic-update-slice_fusion.5
  51.5 2.1 %collective-permute-done.8 = bf16[512,256]{1,0:T(8,128)(2,1)S(1)} collective-permute-done((bf16[512,256]{1,0:T(8,128)(2,1)S(1)}, bf16[512,256]{1,0:T(8,128)(2,1)S(1)}, u32[]{:S(2)}, u32[]{:S(2)}) %collective-permute-start.8) | collective-permute-done | bytes 262176 | tf_op jit(solution)/shard_map/ppermute | solution.py:101
  53.6 0.7 bitcast_dynamic-update-slice_fusion.3
  54.4 1.3 collective-permute-start.10
  57.5 1.4 fusion.50
  58.9 1.5 add_convert_fusion.12
  61.4 2.7 %collective-permute-start.17 = (bf16[256,1024]{1,0:T(8,128)(2,1)S(1)}, bf16[256,1024]{1,0:T(8,128)(2,1)S(1)}, u32[]{:S(2)}, u32[]{:S(2)}) collective-permute-start(bf16[256,1024]{1,0:T(8,128)(2,1)S(1)} %add_convert_fusion.11), channel_id=1, source_target_pairs={{0,2},{2,4},{4,6},{3,1},{5,3},{7,5},{6,7},{1,0},{8,10},{10,12},{12... | collective-permute-start | bytes 1572872 | tf_op jit(solution)/shard_map/ppermute | solution.py:165
  64.6 1.5 add_convert_fusion.10
  66.1 2.0 %collective-permute-start.15 = (bf16[256,1024]{1,0:T(8,128)(2,1)S(1)}, bf16[256,1024]{1,0:T(8,128)(2,1)S(1)}, u32[]{:S(2)}, u32[]{:S(2)}) collective-permute-start(bf16[256,1024]{1,0:T(8,128)(2,1)S(1)} %add_convert_fusion.13), channel_id=1, source_target_pairs={{0,2},{2,4},{4,6},{3,1},{5,3},{7,5},{6,7},{1,0},{8,10},{10,12},{12... | collective-permute-start | bytes 1572872 | tf_op jit(solution)/shard_map/ppermute | solution.py:165
  68.2 0.8 bitcast_dynamic-update-slice_fusion.1
  69.1 0.8 bitcast_dynamic-update-slice_fusion
  69.9 2.5 %convolution_select_fusion.3 = f32[512,1024]{1,0:T(8,128)S(1)} fusion(bf16[1024,1024]{1,0:T(8,128)(2,1)S(1)} %constant_dynamic-update-slice_fusion, bf16[4,1024,512]{2,1,0:T(8,128)(2,1)} %bitcast_dynamic-update-slice_fusion, s32[]{:T(128)S(6)} %select_n.483, pred[]{:T(512)S(6)} %ge.28), kind=kOutput, calls=%fused_computation.11 | convolution fusion | flops 1074266112 | bytes 5242885 | tf_op jit(solution)/shard_map/dot_general | solution.py:143
  72.4 2.5 %convolution_select_fusion.2 = f32[512,1024]{1,0:T(8,128)S(1)} fusion(bf16[1024,1024]{1,0:T(8,128)(2,1)S(1)} %constant_dynamic-update-slice_fusion, bf16[4,1024,512]{2,1,0:T(8,128)(2,1)} %bitcast_dynamic-update-slice_fusion, s32[]{:T(128)S(6)} %select_n.487, pred[]{:T(512)S(6)} %ge.29), kind=kOutput, calls=%fused_computation.10 | convolution fusion | flops 1074266112 | bytes 5242885 | tf_op jit(solution)/shard_map/dot_general | solution.py:143
  74.9 2.5 %convolution_select_fusion.1 = f32[512,1024]{1,0:T(8,128)S(1)} fusion(bf16[1024,1024]{1,0:T(8,128)(2,1)S(1)} %constant_dynamic-update-slice_fusion, bf16[4,1024,512]{2,1,0:T(8,128)(2,1)} %bitcast_dynamic-update-slice_fusion, s32[]{:T(128)S(6)} %select_n.502, pred[]{:T(512)S(6)} %ge.30), kind=kOutput, calls=%fused_computation.9 | convolution fusion | flops 1074266112 | bytes 5242885 | tf_op jit(solution)/shard_map/dot_general | solution.py:143
  77.4 2.6 %convolution_select_fusion = f32[512,1024]{1,0:T(8,128)S(1)} fusion(bf16[1024,1024]{1,0:T(8,128)(2,1)S(1)} %constant_dynamic-update-slice_fusion, bf16[4,1024,512]{2,1,0:T(8,128)(2,1)} %bitcast_dynamic-update-slice_fusion, s32[]{:T(128)S(6)} %select_n.506, pred[]{:T(512)S(6)} %ge.31), kind=kOutput, calls=%fused_computation.8 | convolution fusion | flops 1074266112 | bytes 5242885 | tf_op jit(solution)/shard_map/dot_general | solution.py:143
  80.1 5.7 %collective-permute-done.15 = bf16[256,1024]{1,0:T(8,128)(2,1)S(1)} collective-permute-done((bf16[256,1024]{1,0:T(8,128)(2,1)S(1)}, bf16[256,1024]{1,0:T(8,128)(2,1)S(1)}, u32[]{:S(2)}, u32[]{:S(2)}) %collective-permute-start.15) | collective-permute-done | bytes 524320 | tf_op jit(solution)/shard_map/ppermute | solution.py:165
  86.6 1.5 slice-done.1
  88.6 1.0 add_convert_fusion.2
  89.6 2.5 %collective-permute-start.19 = (bf16[256,1024]{1,0:T(8,128)(2,1)S(1)}, bf16[256,1024]{1,0:T(8,128)(2,1)S(1)}, u32[]{:S(2)}, u32[]{:S(2)}) collective-permute-start(bf16[256,1024]{1,0:T(8,128)(2,1)S(1)} %fusion.5), channel_id=1, source_target_pairs={{0,2},{2,4},{4,6},{3,1},{5,3},{7,5},{6,7},{1,0},{8,10},{10,12},{12... | collective-permute-start | bytes 1572872 | tf_op jit(solution)/shard_map/ppermute | solution.py:165
  92.6 1.8 %fusion.24 = f32[512,1024]{1,0:T(8,128)S(1)} fusion(bf16[512,1024]{1,0:T(8,128)(2,1)S(1)} %get-tuple-element.113, bf16[4,1024,512]{2,1,0:T(8,128)(2,1)} %bitcast_dynamic-update-slice_fusion, s32[]{:T(128)S(6)} %select_n.483), kind=kOutput, calls=%fused_computation.52 | convolution fusion | flops 536870912 | bytes 3670020 | tf_op jit(solution)/shard_map/dot_general | solution.py:228
  94.3 1.9 %fusion.26 = f32[512,1024]{1,0:T(8,128)S(1)} fusion(bf16[512,1024]{1,0:T(8,128)(2,1)S(1)} %get-tuple-element.114, bf16[4,1024,512]{2,1,0:T(8,128)(2,1)} %bitcast_dynamic-update-slice_fusion, s32[]{:T(128)S(6)} %select_n.438), kind=kOutput, calls=%fused_computation.54 | convolution fusion | flops 536870912 | bytes 3670020 | tf_op jit(solution)/shard_map/dot_general | solution.py:228
  96.3 8.1 %collective-permute-done.19 = bf16[256,1024]{1,0:T(8,128)(2,1)S(1)} collective-permute-done((bf16[256,1024]{1,0:T(8,128)(2,1)S(1)}, bf16[256,1024]{1,0:T(8,128)(2,1)S(1)}, u32[]{:S(2)}, u32[]{:S(2)}) %collective-permute-start.19) | collective-permute-done | bytes 524320 | tf_op jit(solution)/shard_map/ppermute | solution.py:165
  104.5 2.3 %collective-permute-done.20 = bf16[256,1024]{1,0:T(8,128)(2,1)S(1)} collective-permute-done((bf16[256,1024]{1,0:T(8,128)(2,1)S(1)}, bf16[256,1024]{1,0:T(8,128)(2,1)S(1)}, u32[]{:S(2)}, u32[]{:S(2)}) %collective-permute-start.20) | collective-permute-done | bytes 524320 | tf_op jit(solution)/shard_map/ppermute | solution.py:165
  107.0 8.4 %collective-permute-done.21 = bf16[256,1024]{1,0:T(8,128)(2,1)S(1)} collective-permute-done((bf16[256,1024]{1,0:T(8,128)(2,1)S(1)}, bf16[256,1024]{1,0:T(8,128)(2,1)S(1)}, u32[]{:S(2)}, u32[]{:S(2)}) %collective-permute-start.21) | collective-permute-done | bytes 524320 | tf_op jit(solution)/shard_map/ppermute | solution.py:165
  115.4 1.0 add_convert_fusion.5
  116.4 1.0 add_convert_fusion.4
  117.7 1.0 add_convert_fusion
  118.7 1.8 %fusion.22 = f32[512,1024]{1,0:T(8,128)S(1)} fusion(bf16[512,1024]{1,0:T(8,128)(2,1)S(1)} %get-tuple-element.112, bf16[4,1024,512]{2,1,0:T(8,128)(2,1)} %bitcast_dynamic-update-slice_fusion, s32[]{:T(128)S(6)} %select_n.498), kind=kOutput, calls=%fused_computation.50 | convolution fusion | flops 536870912 | bytes 3670020 | tf_op jit(solution)/shard_map/dot_general | solution.py:228
  120.5 3.1 %add_add_fusion.1 = f32[512,1024]{1,0:T(8,128)} fusion(f32[512,1024]{1,0:T(8,128)S(1)} %fusion.22, f32[512,1024]{1,0:T(8,128)S(1)} %fusion.26, f32[512,1024]{1,0:T(8,128)S(1)} %fusion.24, bf16[512,1024]{1,0:T(8,128)(2,1)S(1)} %get-tuple-element.111, bf16[4,1024,512]{2,1,0:T(8,128)(2,1)} %bitcast_dynamic-update-slice_fusion, s32[]{:T(128)S(6)} %select_n.502), kind=kOutput, calls=%fused_computation.2 | convolution fusion | flops 538443776 | bytes 9961476 | tf_op jit(solution)/shard_map/dot_general | solution.py:228
  123.6 3.9 %fusion.6.own = f32[512,1024]{1,0:T(8,128)} fusion(bf16[1024,1024]{1,0:T(8,128)(2,1)S(1)} %constant_dynamic-update-slice_fusion, bf16[4,1024,512]{2,1,0:T(8,128)(2,1)} %bitcast_dynamic-update-slice_fusion, s32[]{:T(128)S(6)} %select_n.438), kind=kOutput, calls=%fused_computation.24 | convolution fusion | flops 1073741824 | bytes 5242884 | tf_op jit(solution)/shard_map/dot_general | solution.py:143
  127.5 1.8 %fusion.30 = f32[512,1024]{1,0:T(8,128)S(1)} fusion(bf16[512,1024]{1,0:T(8,128)(2,1)S(1)} %get-tuple-element.114, bf16[4,1024,512]{2,1,0:T(8,128)(2,1)} %bitcast_dynamic-update-slice_fusion, s32[]{:T(128)S(6)} %select_n.438), kind=kOutput, calls=%fused_computation.58 | convolution fusion | flops 536870912 | bytes 3670020 | tf_op jit(solution)/shard_map/dot_general | solution.py:228
  129.2 2.5 %collective-permute-start.24 = (bf16[256,1024]{1,0:T(8,128)(2,1)}, bf16[256,1024]{1,0:T(8,128)(2,1)}, u32[]{:S(2)}, u32[]{:S(2)}) collective-permute-start(bf16[256,1024]{1,0:T(8,128)(2,1)} %add_convert_fusion.5), channel_id=1, source_target_pairs={{0,2},{2,4},{4,6},{3,1},{5,3},{7,5},{6,7},{1,0},{8,10},{10,12},{12... | collective-permute-start | bytes 1572872 | tf_op jit(solution)/shard_map/ppermute | solution.py:165
  131.7 2.0 %collective-permute-start.26 = (bf16[256,1024]{1,0:T(8,128)(2,1)S(1)}, bf16[256,1024]{1,0:T(8,128)(2,1)S(1)}, u32[]{:S(2)}, u32[]{:S(2)}) collective-permute-start(bf16[256,1024]{1,0:T(8,128)(2,1)S(1)} %fusion.4), channel_id=1, source_target_pairs={{0,2},{2,4},{4,6},{3,1},{5,3},{7,5},{6,7},{1,0},{8,10},{10,12},{12... | collective-permute-start | bytes 1572872 | tf_op jit(solution)/shard_map/ppermute | solution.py:165
  133.8 1.8 %convolution_add_fusion.1 = f32[512,1024]{1,0:T(8,128)S(1)} fusion(f32[512,1024]{1,0:T(8,128)S(1)} %fusion.30, bf16[512,1024]{1,0:T(8,128)(2,1)S(1)} %get-tuple-element.113, bf16[4,1024,512]{2,1,0:T(8,128)(2,1)} %bitcast_dynamic-update-slice_fusion, s32[]{:T(128)S(6)} %select_n.483), kind=kOutput, calls=%fused_computation.7 | convolution fusion | flops 537395200 | bytes 5767172 | tf_op jit(solution)/shard_map/dot_general | solution.py:228
  135.6 1.8 %convolution_add_fusion = f32[512,1024]{1,0:T(8,128)S(1)} fusion(f32[512,1024]{1,0:T(8,128)S(1)} %convolution_add_fusion.1, bf16[512,1024]{1,0:T(8,128)(2,1)S(1)} %get-tuple-element.112, bf16[4,1024,512]{2,1,0:T(8,128)(2,1)} %bitcast_dynamic-update-slice_fusion, s32[]{:T(128)S(6)} %select_n.498), kind=kOutput, calls=%fused_computation.6 | convolution fusion | flops 537395200 | bytes 5767172 | tf_op jit(solution)/shard_map/dot_general | solution.py:228
  137.4 17.7 %collective-permute-done.26.first = bf16[256,1024]{1,0:T(8,128)(2,1)S(1)} collective-permute-done((bf16[256,1024]{1,0:T(8,128)(2,1)S(1)}, bf16[256,1024]{1,0:T(8,128)(2,1)S(1)}, u32[]{:S(2)}, u32[]{:S(2)}) %collective-permute-start.26) | collective-permute-done | bytes 524320 | tf_op jit(solution)/shard_map/ppermute | solution.py:165
  155.1 0.8 copy-done.3
  155.9 4.7 %shard_map.119 = (f32[512,1024]{1,0:T(8,128)}, f32[512,1024]{1,0:T(8,128)}, f32[512,1024]{1,0:T(8,128)}, f32[8,512]{1,0:T(8,128)}) custom-call(f32[1,1024]{1,0:T(1,128)} %bitcast.98, bf16[128,128]{1,0:T(8,128)(2,1)} %fusion.79.table, f32[1,2]{1,0:T(1,128)} %maximum_bitcast_fusion.kept, f32[512,1024]{1,0:T(8,128)} %fusion.6.own, bf16[256,1024]{1,0:T(8,128)(2,1)} %copy-done.3, ...), custom_call_target="tpu_custom_call" | custom-call | tf_op jit(solution)/shard_map/pallas_call | solution.py:72
  160.6 4.7 %shard_map.120 = (f32[512,1024]{1,0:T(8,128)}, f32[512,1024]{1,0:T(8,128)}, f32[512,1024]{1,0:T(8,128)}, f32[8,512]{1,0:T(8,128)}) custom-call(f32[1,1024]{1,0:T(1,128)} %bitcast.99, bf16[128,128]{1,0:T(8,128)(2,1)} %fusion.79.table, f32[1,2]{1,0:T(1,128)} %maximum_bitcast_fusion.kept, ...), custom_call_target="tpu_custom_call", output_to_operand_aliasing={{0}: (9, {}), {1}: (10, {}), {2}: (11, {}), {3}: (12, {})} | custom-call | tf_op jit(solution)/shard_map/pallas_call | solution.py:72
  165.4 3.8 %add_add_fusion = f32[512,1024]{1,0:T(8,128)} fusion(f32[512,1024]{1,0:T(8,128)S(1)} %convolution_add_fusion, f32[512,1024]{1,0:T(8,128)} %collective-permute-done.23, bf16[512,1024]{1,0:T(8,128)(2,1)S(1)} %get-tuple-element.111, bf16[4,1024,512]{2,1,0:T(8,128)(2,1)} %bitcast_dynamic-update-slice_fusion, s32[]{:T(128)S(6)} %select_n.502), kind=kOutput, calls=%fused_computation | convolution fusion | flops 537919488 | bytes 7864324 | tf_op jit(solution)/shard_map/dot_general | solution.py:228
  (69 shorter events, 11.0 us)
Async XLA Ops:
  3.2 53.3 %collective-permute-start.13 = (bf16[512,1024]{1,0:T(8,128)(2,1)}, bf16[512,1024]{1,0:T(8,128)(2,1)S(1)}, u32[]{:S(2)}, u32[]{:S(2)}) collective-permute-start(bf16[512,1024]{1,0:T(8,128)(2,1)} %param.9), channel_id=1, source_target_pairs={{0,1},{1,0},{2,3},{3,2},{4,5},{5,4},{6,7},{7,6},{8,9},{9,8},{10,11... | collective-permute-start | bytes 3145736 | tf_op jit(solution)/shard_map/ppermute | solution.py:162
  5.8 13.6 %collective-permute-start = (bf16[512,256]{1,0:T(8,128)(2,1)}, bf16[512,256]{1,0:T(8,128)(2,1)}, u32[]{:S(2)}, u32[]{:S(2)}) collective-permute-start(bf16[512,256]{1,0:T(8,128)(2,1)} %get-tuple-element.59), channel_id=1, source_target_pairs={{0,1},{1,0},{2,3},{3,2},{4,5},{5,4},{6,7},{7,6},{8,9},{9,8},{10,11... | collective-permute-start | bytes 786440 | tf_op jit(solution)/shard_map/ppermute | solution.py:162
  5.9 10.4 %collective-permute-start.1 = (bf16[512,256]{1,0:T(8,128)(2,1)}, bf16[512,256]{1,0:T(8,128)(2,1)}, u32[]{:S(2)}, u32[]{:S(2)}) collective-permute-start(bf16[512,256]{1,0:T(8,128)(2,1)} %get-tuple-element.58), channel_id=1, source_target_pairs={{0,8},{8,0},{16,24},{24,16},{1,9},{9,1},{17,25},{25,17},{2,10},{10... | collective-permute-start | bytes 786440 | tf_op jit(solution)/shard_map/ppermute | solution.py:101
  8.8 10.6 %collective-permute-start.5 = (bf16[512,256]{1,0:T(8,128)(2,1)}, bf16[512,256]{1,0:T(8,128)(2,1)S(1)}, u32[]{:S(2)}, u32[]{:S(2)}) collective-permute-start(bf16[512,256]{1,0:T(8,128)(2,1)} %get-tuple-element.61), channel_id=1, source_target_pairs={{0,1},{1,0},{2,3},{3,2},{4,5},{5,4},{6,7},{7,6},{8,9},{9,8},{10,11... | collective-permute-start | bytes 786440 | tf_op jit(solution)/shard_map/ppermute | solution.py:162
  8.8 12.4 %collective-permute-start.6 = (bf16[512,256]{1,0:T(8,128)(2,1)}, bf16[512,256]{1,0:T(8,128)(2,1)}, u32[]{:S(2)}, u32[]{:S(2)}) collective-permute-start(bf16[512,256]{1,0:T(8,128)(2,1)} %get-tuple-element.60), channel_id=1, source_target_pairs={{0,8},{8,0},{16,24},{24,16},{1,9},{9,1},{17,25},{25,17},{2,10},{10... | collective-permute-start | bytes 786440 | tf_op jit(solution)/shard_map/ppermute | solution.py:101
  8.9 4.0 %copy-start = (bf16[512,1024]{1,0:T(8,128)(2,1)S(1)}, bf16[512,1024]{1,0:T(8,128)(2,1)}, u32[]{:S(2)}) copy-start(bf16[512,1024]{1,0:T(8,128)(2,1)} %param.9) | copy-start | bytes 3145732
  16.3 40.6 %collective-permute-start.12 = (bf16[512,1024]{1,0:T(8,128)(2,1)}, bf16[512,1024]{1,0:T(8,128)(2,1)S(1)}, u32[]{:S(2)}, u32[]{:S(2)}) collective-permute-start(bf16[512,1024]{1,0:T(8,128)(2,1)} %param.11), channel_id=1, source_target_pairs={{0,2},{2,4},{4,6},{3,1},{5,3},{7,5},{6,7},{1,0},{8,10},{10,12},{12... | collective-permute-start | bytes 3145736 | tf_op jit(solution)/shard_map/ppermute | solution.py:165
  19.4 39.5 %collective-permute-start.14 = (bf16[512,1024]{1,0:T(8,128)(2,1)}, bf16[512,1024]{1,0:T(8,128)(2,1)S(1)}, u32[]{:S(2)}, u32[]{:S(2)}) collective-permute-start(bf16[512,1024]{1,0:T(8,128)(2,1)} %param.11), channel_id=1, source_target_pairs={{1,3},{3,5},{5,7},{2,0},{4,2},{6,4},{7,6},{0,1},{9,11},{11,13},{13... | collective-permute-start | bytes 3145736 | tf_op jit(solution)/shard_map/ppermute | solution.py:165
  19.5 9.5 %collective-permute-start.2 = (bf16[512,256]{1,0:T(8,128)(2,1)}, bf16[512,256]{1,0:T(8,128)(2,1)S(1)}, u32[]{:S(2)}, u32[]{:S(2)}) collective-permute-start(bf16[512,256]{1,0:T(8,128)(2,1)} %collective-permute-done), channel_id=1, source_target_pairs={{0,16},{8,24},{16,0},{24,8},{1,17},{9,25},{17,1},{25,9},{2,18},{10... | collective-permute-start | bytes 786440 | tf_op jit(solution)/shard_map/ppermute | solution.py:101
  21.2 13.1 %collective-permute-start.7 = (bf16[512,256]{1,0:T(8,128)(2,1)S(1)}, bf16[512,256]{1,0:T(8,128)(2,1)S(1)}, u32[]{:S(2)}, u32[]{:S(2)}) collective-permute-start(bf16[512,256]{1,0:T(8,128)(2,1)S(1)} %collective-permute-done.5), channel_id=1, source_target_pairs={{0,16},{8,24},{16,0},{24,8},{1,17},{9,25},{17,1},{25,9},{2,18},{10... | collective-permute-start | bytes 786440 | tf_op jit(solution)/shard_map/ppermute | solution.py:101
  28.9 15.7 %collective-permute-start.4 = (bf16[512,256]{1,0:T(8,128)(2,1)S(1)}, bf16[512,256]{1,0:T(8,128)(2,1)S(1)}, u32[]{:S(2)}, u32[]{:S(2)}) collective-permute-start(bf16[512,256]{1,0:T(8,128)(2,1)S(1)} %broadcast_select_fusion.8), channel_id=1, source_target_pairs={{0,16},{8,24},{16,0},{24,8},{1,17},{9,25},{17,1},{25,9},{2,18},{10... | collective-permute-start | bytes 786440 | tf_op jit(solution)/shard_map/ppermute | solution.py:101
  34.3 6.4 %collective-permute-start.3 = (bf16[512,256]{1,0:T(8,128)(2,1)S(1)}, bf16[512,256]{1,0:T(8,128)(2,1)S(1)}, u32[]{:S(2)}, u32[]{:S(2)}) collective-permute-start(bf16[512,256]{1,0:T(8,128)(2,1)S(1)} %broadcast_select_fusion.9), channel_id=1, source_target_pairs={{0,8},{8,0},{16,24},{24,16},{1,9},{9,1},{17,25},{25,17},{2,10},{10... | collective-permute-start | bytes 786440 | tf_op jit(solution)/shard_map/ppermute | solution.py:101
  40.7 13.6 %collective-permute-start.9 = (bf16[512,256]{1,0:T(8,128)(2,1)S(1)}, bf16[512,256]{1,0:T(8,128)(2,1)S(1)}, u32[]{:S(2)}, u32[]{:S(2)}) collective-permute-start(bf16[512,256]{1,0:T(8,128)(2,1)S(1)} %broadcast_select_fusion.6), channel_id=1, source_target_pairs={{0,16},{8,24},{16,0},{24,8},{1,17},{9,25},{17,1},{25,9},{2,18},{10... | collective-permute-start | bytes 786440 | tf_op jit(solution)/shard_map/ppermute | solution.py:101
  44.6 9.0 %collective-permute-start.8 = (bf16[512,256]{1,0:T(8,128)(2,1)S(1)}, bf16[512,256]{1,0:T(8,128)(2,1)S(1)}, u32[]{:S(2)}, u32[]{:S(2)}) collective-permute-start(bf16[512,256]{1,0:T(8,128)(2,1)S(1)} %broadcast_select_fusion.7), channel_id=1, source_target_pairs={{0,8},{8,0},{16,24},{24,16},{1,9},{9,1},{17,25},{25,17},{2,10},{10... | collective-permute-start | bytes 786440 | tf_op jit(solution)/shard_map/ppermute | solution.py:101
  51.5 5.5 %copy-start.1 = (bf16[512,1024]{1,0:T(8,128)(2,1)S(1)}, bf16[512,1024]{1,0:T(8,128)(2,1)}, u32[]{:S(2)}) copy-start(bf16[512,1024]{1,0:T(8,128)(2,1)} %param.9) | copy-start | bytes 3145732
  53.6 15.5 %collective-permute-start.11 = (bf16[512,512]{1,0:T(8,128)(2,1)S(1)}, bf16[512,512]{1,0:T(8,128)(2,1)S(1)}, u32[]{:S(2)}, u32[]{:S(2)}) collective-permute-start(bf16[512,512]{1,0:T(8,128)(2,1)S(1)} %maximum_select_fusion.1), channel_id=1, source_target_pairs={{0,16},{8,24},{16,0},{24,8},{1,17},{9,25},{17,1},{25,9},{2,18},{10... | collective-permute-start | bytes 1572872 | tf_op jit(solution)/shard_map/ppermute | solution.py:101
  54.4 13.8 %collective-permute-start.10 = (bf16[512,512]{1,0:T(8,128)(2,1)S(1)}, bf16[512,512]{1,0:T(8,128)(2,1)S(1)}, u32[]{:S(2)}, u32[]{:S(2)}) collective-permute-start(bf16[512,512]{1,0:T(8,128)(2,1)S(1)} %maximum_select_fusion), channel_id=1, source_target_pairs={{0,8},{8,0},{16,24},{24,16},{1,9},{9,1},{17,25},{25,17},{2,10},{10... | collective-permute-start | bytes 1572872 | tf_op jit(solution)/shard_map/ppermute | solution.py:101
  61.4 24.8 %collective-permute-start.17 = (bf16[256,1024]{1,0:T(8,128)(2,1)S(1)}, bf16[256,1024]{1,0:T(8,128)(2,1)S(1)}, u32[]{:S(2)}, u32[]{:S(2)}) collective-permute-start(bf16[256,1024]{1,0:T(8,128)(2,1)S(1)} %add_convert_fusion.11), channel_id=1, source_target_pairs={{0,2},{2,4},{4,6},{3,1},{5,3},{7,5},{6,7},{1,0},{8,10},{10,12},{12... | collective-permute-start | bytes 1572872 | tf_op jit(solution)/shard_map/ppermute | solution.py:165
  66.1 20.2 %collective-permute-start.18 = (bf16[256,1024]{1,0:T(8,128)(2,1)S(1)}, bf16[256,1024]{1,0:T(8,128)(2,1)S(1)}, u32[]{:S(2)}, u32[]{:S(2)}) collective-permute-start(bf16[256,1024]{1,0:T(8,128)(2,1)S(1)} %add_convert_fusion.10), channel_id=1, source_target_pairs={{1,3},{3,5},{5,7},{2,0},{4,2},{6,4},{7,6},{0,1},{9,11},{11,13},{13... | collective-permute-start | bytes 1572872 | tf_op jit(solution)/shard_map/ppermute | solution.py:165
  66.1 19.7 %collective-permute-start.15 = (bf16[256,1024]{1,0:T(8,128)(2,1)S(1)}, bf16[256,1024]{1,0:T(8,128)(2,1)S(1)}, u32[]{:S(2)}, u32[]{:S(2)}) collective-permute-start(bf16[256,1024]{1,0:T(8,128)(2,1)S(1)} %add_convert_fusion.13), channel_id=1, source_target_pairs={{0,2},{2,4},{4,6},{3,1},{5,3},{7,5},{6,7},{1,0},{8,10},{10,12},{12... | collective-permute-start | bytes 1572872 | tf_op jit(solution)/shard_map/ppermute | solution.py:165
  68.2 17.8 %collective-permute-start.16 = (bf16[256,1024]{1,0:T(8,128)(2,1)S(1)}, bf16[256,1024]{1,0:T(8,128)(2,1)S(1)}, u32[]{:S(2)}, u32[]{:S(2)}) collective-permute-start(bf16[256,1024]{1,0:T(8,128)(2,1)S(1)} %add_convert_fusion.12), channel_id=1, source_target_pairs={{1,3},{3,5},{5,7},{2,0},{4,2},{6,4},{7,6},{0,1},{9,11},{11,13},{13... | collective-permute-start | bytes 1572872 | tf_op jit(solution)/shard_map/ppermute | solution.py:165
  77.4 9.2 %slice-start = ((s8[8388608]{0:T(1024)(128)(4,1)}), s8[4194304]{0:T(1024)(128)(4,1)S(1)}, s32[]{:S(2)}) async-start(s8[8388608]{0:T(1024)(128)(4,1)} %bitcast.96), calls=%async_computation | async-start | bytes 8388608
  85.9 2.2 %slice-start.1 = ((s8[8388608]{0:T(1024)(128)(4,1)}), s8[4194304]{0:T(1024)(128)(4,1)S(1)}, s32[]{:S(2)}) async-start(s8[8388608]{0:T(1024)(128)(4,1)} %bitcast.96), calls=%async_computation.1 | async-start | bytes 8388608
  86.5 2.1 %copy-start.2 = (bf16[512,1024]{1,0:T(8,128)(2,1)S(1)}, bf16[512,1024]{1,0:T(8,128)(2,1)}, u32[]{:S(2)}) copy-start(bf16[512,1024]{1,0:T(8,128)(2,1)} %param.11) | copy-start | bytes 3145732
  89.6 14.8 %collective-permute-start.19 = (bf16[256,1024]{1,0:T(8,128)(2,1)S(1)}, bf16[256,1024]{1,0:T(8,128)(2,1)S(1)}, u32[]{:S(2)}, u32[]{:S(2)}) collective-permute-start(bf16[256,1024]{1,0:T(8,128)(2,1)S(1)} %fusion.5), channel_id=1, source_target_pairs={{0,2},{2,4},{4,6},{3,1},{5,3},{7,5},{6,7},{1,0},{8,10},{10,12},{12... | collective-permute-start | bytes 1572872 | tf_op jit(solution)/shard_map/ppermute | solution.py:165
  92.1 23.4 %collective-permute-start.21 = (bf16[256,1024]{1,0:T(8,128)(2,1)S(1)}, bf16[256,1024]{1,0:T(8,128)(2,1)S(1)}, u32[]{:S(2)}, u32[]{:S(2)}) collective-permute-start(bf16[256,1024]{1,0:T(8,128)(2,1)S(1)} %add_convert_fusion.8), channel_id=1, source_target_pairs={{0,2},{2,4},{4,6},{3,1},{5,3},{7,5},{6,7},{1,0},{8,10},{10,12},{12... | collective-permute-start | bytes 1572872 | tf_op jit(solution)/shard_map/ppermute | solution.py:165
  92.1 14.8 %collective-permute-start.20 = (bf16[256,1024]{1,0:T(8,128)(2,1)S(1)}, bf16[256,1024]{1,0:T(8,128)(2,1)S(1)}, u32[]{:S(2)}, u32[]{:S(2)}) collective-permute-start(bf16[256,1024]{1,0:T(8,128)(2,1)S(1)} %add_convert_fusion.9), channel_id=1, source_target_pairs={{1,3},{3,5},{5,7},{2,0},{4,2},{6,4},{7,6},{0,1},{9,11},{11,13},{13... | collective-permute-start | bytes 1572872 | tf_op jit(solution)/shard_map/ppermute | solution.py:165
  92.6 23.8 %collective-permute-start.22 = (bf16[256,1024]{1,0:T(8,128)(2,1)S(1)}, bf16[256,1024]{1,0:T(8,128)(2,1)S(1)}, u32[]{:S(2)}, u32[]{:S(2)}) collective-permute-start(bf16[256,1024]{1,0:T(8,128)(2,1)S(1)} %add_convert_fusion.7), channel_id=1, source_target_pairs={{1,3},{3,5},{5,7},{2,0},{4,2},{6,4},{7,6},{0,1},{9,11},{11,13},{13... | collective-permute-start | bytes 1572872 | tf_op jit(solution)/shard_map/ppermute | solution.py:165
  123.6 41.8 %collective-permute-start.23 = (f32[512,1024]{1,0:T(8,128)}, f32[512,1024]{1,0:T(8,128)}, u32[]{:S(2)}, u32[]{:S(2)}) collective-permute-start(f32[512,1024]{1,0:T(8,128)} %add_add_fusion.1), channel_id=1, source_target_pairs={{0,1},{1,0},{2,3},{3,2},{4,5},{5,4},{6,7},{7,6},{8,9},{9,8},{10,11... | collective-permute-start | bytes 6291464 | tf_op jit(solution)/shard_map/ppermute | solution.py:162
  129.2 31.4 %collective-permute-start.24 = (bf16[256,1024]{1,0:T(8,128)(2,1)}, bf16[256,1024]{1,0:T(8,128)(2,1)}, u32[]{:S(2)}, u32[]{:S(2)}) collective-permute-start(bf16[256,1024]{1,0:T(8,128)(2,1)} %add_convert_fusion.5), channel_id=1, source_target_pairs={{0,2},{2,4},{4,6},{3,1},{5,3},{7,5},{6,7},{1,0},{8,10},{10,12},{12... | collective-permute-start | bytes 1572872 | tf_op jit(solution)/shard_map/ppermute | solution.py:165
  131.7 28.9 %collective-permute-start.25 = (bf16[256,1024]{1,0:T(8,128)(2,1)}, bf16[256,1024]{1,0:T(8,128)(2,1)}, u32[]{:S(2)}, u32[]{:S(2)}) collective-permute-start(bf16[256,1024]{1,0:T(8,128)(2,1)} %add_convert_fusion.4), channel_id=1, source_target_pairs={{1,3},{3,5},{5,7},{2,0},{4,2},{6,4},{7,6},{0,1},{9,11},{11,13},{13... | collective-permute-start | bytes 1572872 | tf_op jit(solution)/shard_map/ppermute | solution.py:165
  131.7 23.3 %collective-permute-start.26 = (bf16[256,1024]{1,0:T(8,128)(2,1)S(1)}, bf16[256,1024]{1,0:T(8,128)(2,1)S(1)}, u32[]{:S(2)}, u32[]{:S(2)}) collective-permute-start(bf16[256,1024]{1,0:T(8,128)(2,1)S(1)} %fusion.4), channel_id=1, source_target_pairs={{0,2},{2,4},{4,6},{3,1},{5,3},{7,5},{6,7},{1,0},{8,10},{10,12},{12... | collective-permute-start | bytes 1572872 | tf_op jit(solution)/shard_map/ppermute | solution.py:165
  133.8 22.1 %collective-permute-start.27 = (bf16[256,1024]{1,0:T(8,128)(2,1)S(1)}, bf16[256,1024]{1,0:T(8,128)(2,1)}, u32[]{:S(2)}, u32[]{:S(2)}) collective-permute-start(bf16[256,1024]{1,0:T(8,128)(2,1)S(1)} %add_convert_fusion.6), channel_id=1, source_target_pairs={{1,3},{3,5},{5,7},{2,0},{4,2},{6,4},{7,6},{0,1},{9,11},{11,13},{13... | collective-permute-start | bytes 1572872 | tf_op jit(solution)/shard_map/ppermute | solution.py:165
  155.1 0.8 copy-start.3
where the time goes:
time: 171 us; the launch traced here: 169 us
  waiting for transfers between devices  53.8 us (31%)
  matrix products  38.5 us (23%)
  starting transfers between devices  30.4 us (18%)
  local copies, waits for them, and re-layouts  22.6 us (13%)
  other arithmetic  13.2 us (8%)
  Pallas kernels  9.42 us (6%)
    ppermute x14, waiting for transfers between devices, along(): return lax.ppermute(value, 'inner', line_pairs[line])  42.3 us
    dot_general x13, matrix products, contract(): lax.dot_general(left, right, (((0,), (0,)), ((), ())), preferred_element_...  20.8 us
    dot_general x8, matrix products, product(): jnp.dot(tokens_for(chip_index, which), weight, preferred_element_type=jnp...  17.7 us
    ppermute x10, starting transfers between devices, across(): lax.ppermute(value, 'outer', [(k, k ^ distance) for k in range(outer)])  15.4 us
    dynamic_update_slice x14, local copies, waits for them, and re-layouts, body(): lax.dynamic_update_slice(held, piece, (owner, which * count, 0, part * si...  15.3 us
    ppermute x14, starting transfers between devices, along(): return lax.ppermute(value, 'inner', line_pairs[line])  14.5 us
    ppermute x10, waiting for transfers between devices, across(): lax.ppermute(value, 'outer', [(k, k ^ distance) for k in range(outer)])  11.5 us
    pallas_call x2, Pallas kernels, finish(): pl.pallas_call(finish_kernel, grid=(width // tile,), in_specs=given + hel...  9.42 us
  transfers between devices with their start and end apart: 28, of which 11 were waited for; matrix products, arithmetic and copies ran while one was open for 34% of the time, Pallas kernels for 6%

commit v1 on v0

--- a/solution.py
+++ b/solution.py
@@ -198,9 +198,7 @@
             end_block = None
         kept = [jnp.where(place == 0, 0.0, 1.0) for place in places]
         kept = jnp.stack(kept).astype(jnp.float32).reshape(1, 2)
-        signs, table, kept, cotangent = lax.optimization_barrier((signs, table, kept, cotangent))
         cotangent_other = swap(cotangent)
-        cotangents = jnp.concatenate([cotangent, cotangent_other], axis=0)
         held = jnp.zeros((outer, 2 * count, group, rows), tokens.dtype)
         for piece, which, part, owner in pieces:
             piece = piece.reshape(1, count, group, -1)
@@ -209,27 +207,38 @@
             )
         held = held.reshape(outer, 2 * count, group * rows)
 
-        def tokens_for(chip_index, which=None):
-            first, size = (0, 2 * count) if which is None else (which * count, count)
+        def tokens_for(chip_index, which):
+            column = lax.rem(chip_index, group) * rows
             return lax.dynamic_slice(
-                held,
-                (chip_index // group, first, lax.rem(chip_index, group) * rows),
-                (1, size, rows),
+                held, (chip_index // group, which * count, column), (1, count, rows)
             )[0]
 
         def partial_sum(chip_index):
-            return contract(tokens_for(chip_index), cotangents)
-
-        def product(chip_index, delta, cache):
-            cached = lax.dynamic_slice(cache, ((2 * chip_index + core) * rows, 0), (rows, width))
-            weight = cached.astype(jnp.float32) + delta.astype(jnp.float32)
-            weight = lax.optimization_barrier(weight.astype(jnp.bfloat16))
+            one, two = tokens_for(chip_index, 0), tokens_for(chip_index, 1)
+            return contract(one, cotangent) + contract(two, cotangent_other)
+
+        def products(chip_index, deltas, cache):
+            weights = []
+            height = rows // len(deltas)
+            for part, delta in enumerate(deltas):
+                first = (2 * chip_index + core) * rows + part * height
+                cached = lax.dynamic_slice(cache, (first, 0), (height, width))
+                weight = cached.astype(jnp.float32) + delta.astype(jnp.float32)
+                weights.append(lax.optimization_barrier(weight.astype(jnp.bfloat16)))
             return [
-                jnp.dot(tokens_for(chip_index, which), weight, preferred_element_type=jnp.float32)
+                [
+                    jnp.dot(
+                        tokens_for(chip_index, which)[:, part * height :][:, :height],
+                        weight,
+                        preferred_element_type=jnp.float32,
+                    )
+                    for part, weight in enumerate(weights)
+                ]
                 for which in (0, 1)
             ]
 
-        message = [[weight_delta], [weight_delta]]
+        halves = [weight_delta[k * size : (k + 1) * size] for k in range(parts)]
+        message = [halves, halves]
         history = ([], [])
         cache = weight_cache
         caches = [cache]
@@ -242,6 +251,8 @@
                     term = partial_sum(target)
                     term = jnp.where(turn <= places[line], jnp.float32(0), term)
                     terms.append(lax.optimization_barrier(term))
+            if turn == min(2, chips - 1):
+                own = lax.optimization_barrier(partial_sum(chip))
             message = [[], []]
             for k in range(parts):
                 rows_of = slice(k * size, (k + 1) * size)
@@ -253,8 +264,7 @@
                         one, two = end_block(turned(line, chips - 1), k)
                         term = contract(one, cotangent) + contract(two, cotangent_other)
                         term = jnp.where(turn <= place, jnp.float32(0), term)
-                    before = received[0][rows_of] if len(received) == 1 else received[k]
-                    before = jnp.where(place == 0, jnp.bfloat16(0), before)
+                    before = jnp.where(place == 0, jnp.bfloat16(0), received[k])
                     value = (before.astype(jnp.float32) + term).astype(jnp.bfloat16)
                     cache, value, cotangent_other, *terms = lax.optimization_barrier(
                         (cache, value, cotangent_other, *terms)
@@ -263,33 +273,25 @@
             caches.append(cache)
 
         last = [[along(line, message[line][k]) for line in (0, 1)] for k in range(parts)]
-        own = lax.optimization_barrier(partial_sum(chip))
-
-        mine, other = product(chip, weight_delta, caches[min(2, chips - 1)])
+        mine, other = products(chip, [weight_delta], caches[1])
+        mine, other = mine[0], other[0]
         order = sorted(range(1, chips), key=lambda t: max(t, chips - t))
-        products = []
+        later = []
         for number, turn in enumerate(order, 1):
             passed = [history[0][turn - 1], history[1][chips - turn - 1]]
-            most = max(len(value) for value in passed)
-            for line in (0, 1):
-                if len(passed[line]) < most:
-                    whole = passed[line][0]
-                    passed[line] = [
-                        whole[k * size : (k + 1) * size] for k in range(most)
-                    ]
-            delta = jnp.concatenate(
-                [jnp.where(turn <= places[0], one, two) for one, two in zip(*passed)], axis=0
-            )
+            deltas = [jnp.where(turn <= places[0], one, two) for one, two in zip(*passed)]
             source = turned(0, lax.rem(places[0] - turn + chips, chips))
-            one, two = product(source, delta, caches[max(turn, chips - turn)])
-            other = other + two
-            products.append((number, one))
+            ones, twos = products(source, deltas, caches[max(turn, chips - turn)])
+            for two in twos:
+                other = other + two
+            later.append((number, ones))
         theirs = swap(other)
-        for number, one in products:
-            mine = lax.optimization_barrier(mine)
-            if number == chips - 1:
-                mine = mine + theirs
-            mine = mine + one
+        for number, ones in later:
+            for k, one in enumerate(ones):
+                mine = lax.optimization_barrier(mine)
+                if number == chips - 1 and k == len(ones) - 1:
+                    mine = mine + theirs
+                mine = mine + one
         output = mine
 
         done = []

time: 171 us -> 173 us (1.012)
  waiting for transfers between devices: 53.8 us -> 68.6 us
  matrix products: 38.5 us -> 32.4 us
  other arithmetic: 13.2 us -> 8.7 us
  local copies, waits for them, and re-layouts: 22.6 us -> 20 us
    ppermute x14 -> x16, waiting for transfers between devices: 42.3 us -> 51.6 us  [along(): return lax.ppermute(value, 'inner', line_pairs[line])]
    ppermute x10, waiting for transfers between devices: 11.5 us -> 17 us  [across(): lax.ppermute(value, 'outer', [(k, k ^ distance) for k in range(outer)])]
    dot_general x8 -> x14, matrix products: 17.7 us -> 13.3 us  [products(): jnp.dot(tokens_for(chip_index, which)[:, part * height:][:, :height], wei...]
    dynamic_update_slice x14, local copies, waits for them, and re-layouts: 15.3 us -> 11.5 us  [body(): lax.dynamic_update_slice(held, piece, (owner, which * count, 0, part * si...]
    ppermute x4, starting transfers between devices: 0.52 us -> 2.75 us  [swap(): return lax.ppermute(value, 'inner', swap_pairs)]
    squeeze x0 -> x1, local copies, waits for them, and re-layouts: none -> 2.15 us  [tokens_for(): lax.dynamic_slice(held, (chip_index // group, which * count, column), (1,...]
    unnamed x13 -> x16, local copies, waits for them, and re-layouts: 2.82 us -> 0.92 us
    select_n x2, other arithmetic: 1.96 us -> 0.06 us  [gather_tokens(): jnp.where(even, lows[k], near_low[k])]
  transfers between devices with their start and end apart: 28 -> 30, of which waited for: 11 -> 13; matrix products, arithmetic and copies ran while one was open for 34% -> 25% of each run, Pallas kernels for 6% -> 5%
where the time goes in v1:
time: 173 us; the launch traced here: 172 us
  waiting for transfers between devices  68.6 us (40%)
  matrix products  32.4 us (19%)
  starting transfers between devices  31.7 us (18%)
  local copies, waits for them, and re-layouts  20 us (12%)
  Pallas kernels  9.38 us (5%)
  other arithmetic  8.7 us (5%)
    ppermute x16, waiting for transfers between devices, along(): return lax.ppermute(value, 'inner', line_pairs[line])  51.6 us
    dot_general x18, matrix products, contract(): lax.dot_general(left, right, (((0,), (0,)), ((), ())), preferred_element_...  19.1 us
    ppermute x10, waiting for transfers between devices, across(): lax.ppermute(value, 'outer', [(k, k ^ distance) for k in range(outer)])  17 us
    ppermute x16, starting transfers between devices, along(): return lax.ppermute(value, 'inner', line_pairs[line])  14.5 us
    ppermute x10, starting transfers between devices, across(): lax.ppermute(value, 'outer', [(k, k ^ distance) for k in range(outer)])  14.4 us
    dot_general x14, matrix products, products(): jnp.dot(tokens_for(chip_index, which)[:, part * height:][:, :height], wei...  13.3 us
    dynamic_update_slice x14, local copies, waits for them, and re-layouts, body(): lax.dynamic_update_slice(held, piece, (owner, which * count, 0, part * si...  11.5 us
    pallas_call x2, Pallas kernels, finish(): pl.pallas_call(finish_kernel, grid=(width // tile,), in_specs=given + hel...  9.38 us
  transfers between devices with their start and end apart: 30, of which 13 were waited for; matrix products, arithmetic and copies ran while one was open for 25% of the time, Pallas kernels for 5%

profile of v1, /device:TPU:0, one launch (start us, length us, event | category | flops | bytes accessed | tf_op | source)
XLA Modules:
  0.0 172.0 jit_solution(16897074243563085249)
XLA Ops:
  0.7 2.1 %constant_dynamic-slice_fusion = (bf16[512,256]{1,0:T(8,128)(2,1)}, bf16[512,256]{1,0:T(8,128)(2,1)S(1)}, bf16[512,256]{1,0:T(8,128)(2,1)S(1)}, bf16[512,256]{1,0:T(8,128)(2,1)}) fusion(bf16[512,1024]{1,0:T(8,128)(2,1)} %param.8, s32[]{:T(128)S(6)} %select_n.461, s32[]{:T(128)S(6)} %select_n.459, s32[]{:T(128)S(6)} %select_n.458, s32[]{:T(128)S(6)} %select_n.460), kind=kLoop, calls=%fused_computation.157 | loop fusion | bytes 2097168 | tf_op jit(solution)/shard_map/dynamic_slice | solution.py:188
  3.3 1.0 fusion.99
  4.4 2.6 %collective-permute-start.12 = (bf16[256,1024]{1,0:T(8,128)(2,1)}, bf16[256,1024]{1,0:T(8,128)(2,1)}, u32[]{:S(2)}, u32[]{:S(2)}) collective-permute-start(bf16[256,1024]{1,0:T(8,128)(2,1)} %get-tuple-element.126), channel_id=1, source_target_pairs={{0,2},{2,4},{4,6},{3,1},{5,3},{7,5},{6,7},{1,0},{8,10},{10,12},{12... | collective-permute-start | bytes 1572872 | tf_op jit(solution)/shard_map/ppermute | solution.py:165
  6.9 1.5 collective-permute-start.1
  8.9 2.3 %reshape.100 = bf16[4,1024,512]{2,1,0:T(8,128)(2,1)} broadcast(bf16[]{:T(256)} %constant.185.clone.1), dimensions={} | broadcast | bytes 4194306 | tf_op jit(solution)/shard_map/reshape | solution.py:208
  11.2 0.7 bitcast_dynamic-update-slice_fusion.13
  13.8 2.4 %collective-permute-done.1 = bf16[512,256]{1,0:T(8,128)(2,1)} collective-permute-done((bf16[512,256]{1,0:T(8,128)(2,1)S(1)}, bf16[512,256]{1,0:T(8,128)(2,1)}, u32[]{:S(2)}, u32[]{:S(2)}) %collective-permute-start.1) | collective-permute-done | bytes 262176 | tf_op jit(solution)/shard_map/ppermute | solution.py:101
  16.4 2.5 %collective-permute-start.2 = (bf16[512,256]{1,0:T(8,128)(2,1)S(1)}, bf16[512,256]{1,0:T(8,128)(2,1)S(1)}, u32[]{:S(2)}, u32[]{:S(2)}) collective-permute-start(bf16[512,256]{1,0:T(8,128)(2,1)S(1)} %collective-permute-done), channel_id=1, source_target_pairs={{0,16},{8,24},{16,0},{24,8},{1,17},{9,25},{17,1},{25,9},{2,18},{10... | collective-permute-start | bytes 786440 | tf_op jit(solution)/shard_map/ppermute | solution.py:101
  19.4 1.8 %collective-permute-start.7 = (bf16[512,256]{1,0:T(8,128)(2,1)S(1)}, bf16[512,256]{1,0:T(8,128)(2,1)S(1)}, u32[]{:S(2)}, u32[]{:S(2)}) collective-permute-start(bf16[512,256]{1,0:T(8,128)(2,1)S(1)} %collective-permute-done.5), channel_id=1, source_target_pairs={{0,16},{8,24},{16,0},{24,8},{1,17},{9,25},{17,1},{25,9},{2,18},{10... | collective-permute-start | bytes 786440 | tf_op jit(solution)/shard_map/ppermute | solution.py:101
  21.2 0.7 bitcast_dynamic-update-slice_fusion.12
  22.0 1.7 bitcast_dynamic-update-slice_fusion.11
  23.6 1.1 maximum_select_fusion.1
  24.7 1.3 collective-permute-done.2
  26.0 2.0 %collective-permute-start.4 = (bf16[512,256]{1,0:T(8,128)(2,1)S(1)}, bf16[512,256]{1,0:T(8,128)(2,1)S(1)}, u32[]{:S(2)}, u32[]{:S(2)}) collective-permute-start(bf16[512,256]{1,0:T(8,128)(2,1)S(1)} %broadcast_select_fusion.2), channel_id=1, source_target_pairs={{0,16},{8,24},{16,0},{24,8},{1,17},{9,25},{17,1},{25,9},{2,18},{10... | collective-permute-start | bytes 786440 | tf_op jit(solution)/shard_map/ppermute | solution.py:101
  28.1 3.6 %collective-permute-done.7 = bf16[512,256]{1,0:T(8,128)(2,1)S(1)} collective-permute-done((bf16[512,256]{1,0:T(8,128)(2,1)S(1)}, bf16[512,256]{1,0:T(8,128)(2,1)S(1)}, u32[]{:S(2)}, u32[]{:S(2)}) %collective-permute-start.7) | collective-permute-done | bytes 262176 | tf_op jit(solution)/shard_map/ppermute | solution.py:101
  31.7 2.0 %collective-permute-start.3 = (bf16[512,256]{1,0:T(8,128)(2,1)S(1)}, bf16[512,256]{1,0:T(8,128)(2,1)S(1)}, u32[]{:S(2)}, u32[]{:S(2)}) collective-permute-start(bf16[512,256]{1,0:T(8,128)(2,1)S(1)} %broadcast_select_fusion.3), channel_id=1, source_target_pairs={{0,8},{8,0},{16,24},{24,16},{1,9},{9,1},{17,25},{25,17},{2,10},{10... | collective-permute-start | bytes 786440 | tf_op jit(solution)/shard_map/ppermute | solution.py:101
  33.7 0.7 bitcast_dynamic-update-slice_fusion.10
  34.6 4.9 %collective-permute-done.3 = bf16[512,256]{1,0:T(8,128)(2,1)S(1)} collective-permute-done((bf16[512,256]{1,0:T(8,128)(2,1)S(1)}, bf16[512,256]{1,0:T(8,128)(2,1)S(1)}, u32[]{:S(2)}, u32[]{:S(2)}) %collective-permute-start.3) | collective-permute-done | bytes 262176 | tf_op jit(solution)/shard_map/ppermute | solution.py:101
  39.5 1.5 collective-permute-start.9
  40.9 0.7 bitcast_dynamic-update-slice_fusion.9
  42.2 0.7 bitcast_dynamic-update-slice_fusion.8
  42.9 0.8 bitcast_dynamic-update-slice_fusion.7
  43.7 0.7 bitcast_dynamic-update-slice_fusion.6
  44.4 0.7 bitcast_dynamic-update-slice_fusion.5
  45.2 0.7 bitcast_dynamic-update-slice_fusion.4
  45.9 2.1 %collective-permute-done.8 = bf16[512,256]{1,0:T(8,128)(2,1)S(1)} collective-permute-done((bf16[512,256]{1,0:T(8,128)(2,1)S(1)}, bf16[512,256]{1,0:T(8,128)(2,1)S(1)}, u32[]{:S(2)}, u32[]{:S(2)}) %collective-permute-start.8) | collective-permute-done | bytes 262176 | tf_op jit(solution)/shard_map/ppermute | solution.py:101
  48.0 2.0 %collective-permute-start.15 = (bf16[256,1024]{1,0:T(8,128)(2,1)S(1)}, bf16[256,1024]{1,0:T(8,128)(2,1)S(1)}, u32[]{:S(2)}, u32[]{:S(2)}) collective-permute-start(bf16[256,1024]{1,0:T(8,128)(2,1)S(1)} %copy-done.4), channel_id=1, source_target_pairs={{0,2},{2,4},{4,6},{3,1},{5,3},{7,5},{6,7},{1,0},{8,10},{10,12},{12... | collective-permute-start | bytes 1572872 | tf_op jit(solution)/shard_map/ppermute | solution.py:165
  50.0 0.7 bitcast_dynamic-update-slice_fusion.3
  50.8 0.8 bitcast_dynamic-update-slice_fusion.2
  51.5 0.9 collective-permute-start.11
  52.9 1.2 collective-permute-start.10
  56.1 4.8 %collective-permute-done.15 = bf16[256,1024]{1,0:T(8,128)(2,1)S(1)} collective-permute-done((bf16[256,1024]{1,0:T(8,128)(2,1)S(1)}, bf16[256,1024]{1,0:T(8,128)(2,1)S(1)}, u32[]{:S(2)}, u32[]{:S(2)}) %collective-permute-start.15) | collective-permute-done | bytes 524320 | tf_op jit(solution)/shard_map/ppermute | solution.py:165
  62.8 2.2 %collective-permute-done.10 = bf16[512,512]{1,0:T(8,128)(2,1)S(1)} collective-permute-done((bf16[512,512]{1,0:T(8,128)(2,1)S(1)}, bf16[512,512]{1,0:T(8,128)(2,1)S(1)}, u32[]{:S(2)}, u32[]{:S(2)}) %collective-permute-start.10) | collective-permute-done | bytes 524320 | tf_op jit(solution)/shard_map/ppermute | solution.py:101
  65.0 0.8 bitcast_dynamic-update-slice_fusion.1
  65.8 0.8 bitcast_dynamic-update-slice_fusion
  66.7 1.8 %fusion.16 = f32[512,1024]{1,0:T(8,128)S(1)} fusion(bf16[512,1024]{1,0:T(8,128)(2,1)S(1)} %add_convert_fusion, bf16[4,1024,512]{2,1,0:T(8,128)(2,1)} %bitcast_dynamic-update-slice_fusion, s32[]{:T(128)S(6)} %select_n.482), kind=kOutput, calls=%fused_computation.53 | convolution fusion | flops 536870912 | bytes 3670020 | tf_op jit(solution)/shard_map/dot_general | solution.py:230
  69.0 2.1 %dynamic-slice_bitcast_fusion = (bf16[512,512]{1,0:T(8,128)(2,1)S(1)}, bf16[512,512]{1,0:T(8,128)(2,1)S(1)}, bf16[512,512]{1,0:T(8,128)(2,1)S(1)}, bf16[512,512]...) fusion(bf16[4,1024,512]{2,1,0:T(8,128)(2,1)} %bitcast_dynamic-update-slice_fusion, ...), kind=kLoop, calls=%fused_computation.57 | loop fusion | bytes 6291468 | tf_op jit(solution)/shard_map/squeeze | solution.py:212
  71.2 0.7 fusion.100
  71.9 0.7 add_select_fusion.3
  72.7 2.0 %collective-permute-start.17 = (bf16[256,1024]{1,0:T(8,128)(2,1)S(1)}, bf16[256,1024]{1,0:T(8,128)(2,1)S(1)}, u32[]{:S(2)}, u32[]{:S(2)}) collective-permute-start(bf16[256,1024]{1,0:T(8,128)(2,1)S(1)} %add_convert_fusion.16), channel_id=1, source_target_pairs={{0,2},{2,4},{4,6},{3,1},{5,3},{7,5},{6,7},{1,0},{8,10},{10,12},{12... | collective-permute-start | bytes 1572872 | tf_op jit(solution)/shard_map/ppermute | solution.py:165
  74.7 1.8 %fusion.12 = f32[512,1024]{1,0:T(8,128)S(1)} fusion(bf16[512,1024]{1,0:T(8,128)(2,1)S(1)} %collective-permute-done.13, bf16[4,1024,512]{2,1,0:T(8,128)(2,1)} %bitcast_dynamic-update-slice_fusion, s32[]{:T(128)S(6)} %select_n.529), kind=kOutput, calls=%fused_computation.49 | convolution fusion | flops 536870912 | bytes 3670020 | tf_op jit(solution)/shard_map/dot_general | solution.py:143
  76.5 1.8 %add_select_fusion.2 = f32[512,1024]{1,0:T(8,128)S(1)} fusion(f32[512,1024]{1,0:T(8,128)S(1)} %fusion.12, bf16[512,1024]{1,0:T(8,128)(2,1)S(1)} %copy-done, pred[]{:T(512)S(6)} %ge.29, bf16[4,1024,512]{2,1,0:T(8,128)(2,1)} %bitcast_dynamic-update-slice_fusion, s32[]{:T(128)S(6)} %select_n.529), kind=kOutput, calls=%fused_computation.4 | convolution fusion | flops 537919488 | bytes 5767173 | tf_op jit(solution)/shard_map/dot_general | solution.py:143
  78.3 1.8 %fusion.6 = f32[512,1024]{1,0:T(8,128)S(1)} fusion(bf16[512,1024]{1,0:T(8,128)(2,1)S(1)} %collective-permute-done.13, bf16[4,1024,512]{2,1,0:T(8,128)(2,1)} %bitcast_dynamic-update-slice_fusion, s32[]{:T(128)S(6)} %select_n.482), kind=kOutput, calls=%fused_computation.43 | convolution fusion | flops 536870912 | bytes 3670020 | tf_op jit(solution)/shard_map/dot_general | solution.py:143
  80.1 11.7 %collective-permute-done.17 = bf16[256,1024]{1,0:T(8,128)(2,1)S(1)} collective-permute-done((bf16[256,1024]{1,0:T(8,128)(2,1)S(1)}, bf16[256,1024]{1,0:T(8,128)(2,1)S(1)}, u32[]{:S(2)}, u32[]{:S(2)}) %collective-permute-start.17) | collective-permute-done | bytes 524320 | tf_op jit(solution)/shard_map/ppermute | solution.py:165
  93.2 2.5 %collective-permute-start.23 = (bf16[256,1024]{1,0:T(8,128)(2,1)S(1)}, bf16[256,1024]{1,0:T(8,128)(2,1)S(1)}, u32[]{:S(2)}, u32[]{:S(2)}) collective-permute-start(bf16[256,1024]{1,0:T(8,128)(2,1)S(1)} %add_convert_fusion.11), channel_id=1, source_target_pairs={{0,2},{2,4},{4,6},{3,1},{5,3},{7,5},{6,7},{1,0},{8,10},{10,12},{12... | collective-permute-start | bytes 1572872 | tf_op jit(solution)/shard_map/ppermute | solution.py:165
  95.7 0.7 fusion.101
  96.4 0.9 add_select_fusion.1
  97.4 1.8 %fusion.9 = f32[512,1024]{1,0:T(8,128)S(1)} fusion(bf16[512,1024]{1,0:T(8,128)(2,1)S(1)} %collective-permute-done.13, bf16[4,1024,512]{2,1,0:T(8,128)(2,1)} %bitcast_dynamic-update-slice_fusion, s32[]{:T(128)S(6)} %select_n.548), kind=kOutput, calls=%fused_computation.46 | convolution fusion | flops 536870912 | bytes 3670020 | tf_op jit(solution)/shard_map/dot_general | solution.py:143
  99.2 1.8 %add_select_fusion = f32[512,1024]{1,0:T(8,128)S(1)} fusion(f32[512,1024]{1,0:T(8,128)S(1)} %fusion.9, bf16[512,1024]{1,0:T(8,128)(2,1)S(1)} %copy-done, pred[]{:T(512)S(6)} %ge.31, bf16[4,1024,512]{2,1,0:T(8,128)(2,1)} %bitcast_dynamic-update-slice_fusion, s32[]{:T(128)S(6)} %select_n.548), kind=kOutput, calls=%fused_computation.2 | convolution fusion | flops 537919488 | bytes 5767173 | tf_op jit(solution)/shard_map/dot_general | solution.py:143
  102.4 11.7 %collective-permute-done.21 = bf16[256,1024]{1,0:T(8,128)(2,1)S(1)} collective-permute-done((bf16[256,1024]{1,0:T(8,128)(2,1)S(1)}, bf16[256,1024]{1,0:T(8,128)(2,1)S(1)}, u32[]{:S(2)}, u32[]{:S(2)}) %collective-permute-start.21) | collective-permute-done | bytes 524320 | tf_op jit(solution)/shard_map/ppermute | solution.py:165
  114.5 1.0 add_convert_fusion.6
  115.5 2.7 %collective-permute-done.24 = bf16[256,1024]{1,0:T(8,128)(2,1)S(1)} collective-permute-done((bf16[256,1024]{1,0:T(8,128)(2,1)S(1)}, bf16[256,1024]{1,0:T(8,128)(2,1)S(1)}, u32[]{:S(2)}, u32[]{:S(2)}) %collective-permute-start.24) | collective-permute-done | bytes 524320 | tf_op jit(solution)/shard_map/ppermute | solution.py:165
  118.2 1.0 add_convert_fusion.5
  119.2 1.5 add_convert_fusion.1
  122.5 3.4 %add_add_fusion.1 = f32[512,1024]{1,0:T(8,128)} fusion(f32[512,1024]{1,0:T(8,128)S(1)} %fusion.30, f32[512,1024]{1,0:T(8,128)S(1)} %fusion.32, f32[512,1024]{1,0:T(8,128)S(1)} %fusion.34, f32[512,1024]{1,0:T(8,128)S(1)} %fusion.36, f32[512,1024]{1,0:T(8,128)S(1)} %fusion.38, f32[512,1024]{1,0:T(8,128)S(1)} %fusion.40, ...), kind=kOutput, calls=%fused_computation.1 | convolution fusion | flops 540016640 | bytes 16252932 | tf_op jit(solution)/shard_map/dot_general | solution.py:230
  125.9 2.2 %collective-permute-start.25 = (f32[512,1024]{1,0:T(8,128)}, f32[512,1024]{1,0:T(8,128)}, u32[]{:S(2)}, u32[]{:S(2)}) collective-permute-start(f32[512,1024]{1,0:T(8,128)} %add_add_fusion.1), channel_id=1, source_target_pairs={{0,1},{1,0},{2,3},{3,2},{4,5},{5,4},{6,7},{7,6},{8,9},{9,8},{10,11... | collective-permute-start | bytes 6291464 | tf_op jit(solution)/shard_map/ppermute | solution.py:162
  128.1 3.2 %convolution_add_fusion.own = f32[512,1024]{1,0:T(8,128)} fusion(f32[512,1024]{1,0:T(8,128)S(1)} %fusion.6, bf16[512,1024]{1,0:T(8,128)(2,1)S(1)} %copy-done, bf16[4,1024,512]{2,1,0:T(8,128)(2,1)} %bitcast_dynamic-update-slice_fusion, s32[]{:T(128)S(6)} %select_n.482), kind=kOutput, calls=%fused_computation.7 | convolution fusion | flops 537395200 | bytes 5767172 | tf_op jit(solution)/shard_map/dot_general | solution.py:143
  132.6 2.2 %collective-permute-start.26 = (bf16[256,1024]{1,0:T(8,128)(2,1)}, bf16[256,1024]{1,0:T(8,128)(2,1)}, u32[]{:S(2)}, u32[]{:S(2)}) collective-permute-start(bf16[256,1024]{1,0:T(8,128)(2,1)} %add_convert_fusion.6), channel_id=1, source_target_pairs={{0,2},{2,4},{4,6},{3,1},{5,3},{7,5},{6,7},{1,0},{8,10},{10,12},{12... | collective-permute-start | bytes 1572872 | tf_op jit(solution)/shard_map/ppermute | solution.py:165
  134.8 2.0 %collective-permute-start.28 = (bf16[256,1024]{1,0:T(8,128)(2,1)S(1)}, bf16[256,1024]{1,0:T(8,128)(2,1)S(1)}, u32[]{:S(2)}, u32[]{:S(2)}) collective-permute-start(bf16[256,1024]{1,0:T(8,128)(2,1)S(1)} %fusion.4), channel_id=1, source_target_pairs={{0,2},{2,4},{4,6},{3,1},{5,3},{7,5},{6,7},{1,0},{8,10},{10,12},{12... | collective-permute-start | bytes 1572872 | tf_op jit(solution)/shard_map/ppermute | solution.py:165
  137.7 19.9 %collective-permute-done.28.first = bf16[256,1024]{1,0:T(8,128)(2,1)S(1)} collective-permute-done((bf16[256,1024]{1,0:T(8,128)(2,1)S(1)}, bf16[256,1024]{1,0:T(8,128)(2,1)S(1)}, u32[]{:S(2)}, u32[]{:S(2)}) %collective-permute-start.28) | collective-permute-done | bytes 524320 | tf_op jit(solution)/shard_map/ppermute | solution.py:165
  158.4 0.8 copy-done.3
  159.2 4.7 %shard_map.119 = (f32[512,1024]{1,0:T(8,128)}, f32[512,1024]{1,0:T(8,128)}, f32[512,1024]{1,0:T(8,128)}, f32[8,512]{1,0:T(8,128)}) custom-call(f32[1,1024]{1,0:T(1,128)} %bitcast.106, bf16[128,128]{1,0:T(8,128)(2,1)} %fusion.86.table, f32[1,2]{1,0:T(1,128)} %maximum_bitcast_fusion.kept, f32[512,1024]{1,0:T(8,128)} %convolution_add_fusion.own, ...), custom_call_target="tpu_custom_call" | custom-call | tf_op jit(solution)/shard_map/pallas_call | solution.py:72
  163.9 4.7 %shard_map.120 = (f32[512,1024]{1,0:T(8,128)}, f32[512,1024]{1,0:T(8,128)}, f32[512,1024]{1,0:T(8,128)}, f32[8,512]{1,0:T(8,128)}) custom-call(f32[1,1024]{1,0:T(1,128)} %bitcast.107, bf16[128,128]{1,0:T(8,128)(2,1)} %fusion.86.table, f32[1,2]{1,0:T(1,128)} %maximum_bitcast_fusion.kept, ...), custom_call_target="tpu_custom_call", output_to_operand_aliasing={{0}: (9, {}), {1}: (10, {}), {2}: (11, {}), {3}: (12, {})} | custom-call | tf_op jit(solution)/shard_map/pallas_call | solution.py:72
  168.6 3.4 %add_add_fusion = f32[512,1024]{1,0:T(8,128)} fusion(f32[512,1024]{1,0:T(8,128)S(1)} %convolution_add_fusion.1, f32[512,1024]{1,0:T(8,128)} %collective-permute-done.25, bf16[256,1024]{1,0:T(8,128)(2,1)S(1)} %get-tuple-element.113, bf16[512,512]{1,0:T(8,128)(2,1)S(1)} %get-tuple-element.121), kind=kOutput, calls=%fused_computation | convolution fusion | flops 269484032 | bytes 7077888 | tf_op jit(solution)/shard_map/dot_general | solution.py:230
  (85 shorter events, 17.1 us)
Async XLA Ops:
  0.6 2.7 %copy-start.1 = (bf16[512,1024]{1,0:T(8,128)(2,1)S(1)}, bf16[512,1024]{1,0:T(8,128)(2,1)}, u32[]{:S(2)}) copy-start(bf16[512,1024]{1,0:T(8,128)(2,1)} %param.11) | copy-start | bytes 3145732
  2.8 13.4 %collective-permute-start = (bf16[512,256]{1,0:T(8,128)(2,1)}, bf16[512,256]{1,0:T(8,128)(2,1)S(1)}, u32[]{:S(2)}, u32[]{:S(2)}) collective-permute-start(bf16[512,256]{1,0:T(8,128)(2,1)} %get-tuple-element.60), channel_id=1, source_target_pairs={{0,1},{1,0},{2,3},{3,2},{4,5},{5,4},{6,7},{7,6},{8,9},{9,8},{10,11... | collective-permute-start | bytes 786440 | tf_op jit(solution)/shard_map/ppermute | solution.py:162
  4.4 48.5 %collective-permute-start.12 = (bf16[256,1024]{1,0:T(8,128)(2,1)}, bf16[256,1024]{1,0:T(8,128)(2,1)}, u32[]{:S(2)}, u32[]{:S(2)}) collective-permute-start(bf16[256,1024]{1,0:T(8,128)(2,1)} %get-tuple-element.126), channel_id=1, source_target_pairs={{0,2},{2,4},{4,6},{3,1},{5,3},{7,5},{6,7},{1,0},{8,10},{10,12},{12... | collective-permute-start | bytes 1572872 | tf_op jit(solution)/shard_map/ppermute | solution.py:165
  6.9 9.3 %collective-permute-start.1 = (bf16[512,256]{1,0:T(8,128)(2,1)S(1)}, bf16[512,256]{1,0:T(8,128)(2,1)}, u32[]{:S(2)}, u32[]{:S(2)}) collective-permute-start(bf16[512,256]{1,0:T(8,128)(2,1)S(1)} %get-tuple-element.59), channel_id=1, source_target_pairs={{0,8},{8,0},{16,24},{24,16},{1,9},{9,1},{17,25},{25,17},{2,10},{10... | collective-permute-start | bytes 786440 | tf_op jit(solution)/shard_map/ppermute | solution.py:101
  8.4 7.9 %collective-permute-start.5 = (bf16[512,256]{1,0:T(8,128)(2,1)}, bf16[512,256]{1,0:T(8,128)(2,1)S(1)}, u32[]{:S(2)}, u32[]{:S(2)}) collective-permute-start(bf16[512,256]{1,0:T(8,128)(2,1)} %get-tuple-element.62), channel_id=1, source_target_pairs={{0,1},{1,0},{2,3},{3,2},{4,5},{5,4},{6,7},{7,6},{8,9},{9,8},{10,11... | collective-permute-start | bytes 786440 | tf_op jit(solution)/shard_map/ppermute | solution.py:162
  8.4 11.0 %collective-permute-start.6 = (bf16[512,256]{1,0:T(8,128)(2,1)S(1)}, bf16[512,256]{1,0:T(8,128)(2,1)S(1)}, u32[]{:S(2)}, u32[]{:S(2)}) collective-permute-start(bf16[512,256]{1,0:T(8,128)(2,1)S(1)} %get-tuple-element.61), channel_id=1, source_target_pairs={{0,8},{8,0},{16,24},{24,16},{1,9},{9,1},{17,25},{25,17},{2,10},{10... | collective-permute-start | bytes 786440 | tf_op jit(solution)/shard_map/ppermute | solution.py:101
  8.9 3.0 %copy-start.5 = (s32[1024]{0:T(1024)S(1)}, s32[1024]{0:T(1024)}, u32[]{:S(2)}) copy-start(s32[1024]{0:T(1024)} %param.12) | copy-start | bytes 12292
  8.9 7.3 %copy-start = (bf16[512,1024]{1,0:T(8,128)(2,1)S(1)}, bf16[512,1024]{1,0:T(8,128)(2,1)}, u32[]{:S(2)}) copy-start(bf16[512,1024]{1,0:T(8,128)(2,1)} %param.9) | copy-start | bytes 3145732
  16.2 38.9 %collective-permute-start.14 = (bf16[256,1024]{1,0:T(8,128)(2,1)}, bf16[256,1024]{1,0:T(8,128)(2,1)S(1)}, u32[]{:S(2)}, u32[]{:S(2)}) collective-permute-start(bf16[256,1024]{1,0:T(8,128)(2,1)} %get-tuple-element.126), channel_id=1, source_target_pairs={{1,3},{3,5},{5,7},{2,0},{4,2},{6,4},{7,6},{0,1},{9,11},{11,13},{13... | collective-permute-start | bytes 1572872 | tf_op jit(solution)/shard_map/ppermute | solution.py:165
  16.3 35.3 %collective-permute-start.13 = (bf16[512,1024]{1,0:T(8,128)(2,1)S(1)}, bf16[512,1024]{1,0:T(8,128)(2,1)S(1)}, u32[]{:S(2)}, u32[]{:S(2)}) collective-permute-start(bf16[512,1024]{1,0:T(8,128)(2,1)S(1)} %copy-done), channel_id=1, source_target_pairs={{0,1},{1,0},{2,3},{3,2},{4,5},{5,4},{6,7},{7,6},{8,9},{9,8},{10,11... | collective-permute-start | bytes 3145736 | tf_op jit(solution)/shard_map/ppermute | solution.py:162
  16.4 9.7 %collective-permute-start.2 = (bf16[512,256]{1,0:T(8,128)(2,1)S(1)}, bf16[512,256]{1,0:T(8,128)(2,1)S(1)}, u32[]{:S(2)}, u32[]{:S(2)}) collective-permute-start(bf16[512,256]{1,0:T(8,128)(2,1)S(1)} %collective-permute-done), channel_id=1, source_target_pairs={{0,16},{8,24},{16,0},{24,8},{1,17},{9,25},{17,1},{25,9},{2,18},{10... | collective-permute-start | bytes 786440 | tf_op jit(solution)/shard_map/ppermute | solution.py:101
  19.4 12.2 %collective-permute-start.7 = (bf16[512,256]{1,0:T(8,128)(2,1)S(1)}, bf16[512,256]{1,0:T(8,128)(2,1)S(1)}, u32[]{:S(2)}, u32[]{:S(2)}) collective-permute-start(bf16[512,256]{1,0:T(8,128)(2,1)S(1)} %collective-permute-done.5), channel_id=1, source_target_pairs={{0,16},{8,24},{16,0},{24,8},{1,17},{9,25},{17,1},{25,9},{2,18},{10... | collective-permute-start | bytes 786440 | tf_op jit(solution)/shard_map/ppermute | solution.py:101
  26.0 15.6 %collective-permute-start.4 = (bf16[512,256]{1,0:T(8,128)(2,1)S(1)}, bf16[512,256]{1,0:T(8,128)(2,1)S(1)}, u32[]{:S(2)}, u32[]{:S(2)}) collective-permute-start(bf16[512,256]{1,0:T(8,128)(2,1)S(1)} %broadcast_select_fusion.2), channel_id=1, source_target_pairs={{0,16},{8,24},{16,0},{24,8},{1,17},{9,25},{17,1},{25,9},{2,18},{10... | collective-permute-start | bytes 786440 | tf_op jit(solution)/shard_map/ppermute | solution.py:101
  31.7 7.8 %collective-permute-start.3 = (bf16[512,256]{1,0:T(8,128)(2,1)S(1)}, bf16[512,256]{1,0:T(8,128)(2,1)S(1)}, u32[]{:S(2)}, u32[]{:S(2)}) collective-permute-start(bf16[512,256]{1,0:T(8,128)(2,1)S(1)} %broadcast_select_fusion.3), channel_id=1, source_target_pairs={{0,8},{8,0},{16,24},{24,16},{1,9},{9,1},{17,25},{25,17},{2,10},{10... | collective-permute-start | bytes 786440 | tf_op jit(solution)/shard_map/ppermute | solution.py:101
  34.4 13.6 %copy-start.4 = (bf16[256,1024]{1,0:T(8,128)(2,1)S(1)}, bf16[256,1024]{1,0:T(8,128)(2,1)}, u32[]{:S(2)}) copy-start(bf16[256,1024]{1,0:T(8,128)(2,1)} %get-tuple-element.125) | copy-start | bytes 1572868
  39.5 11.3 %collective-permute-start.9 = (bf16[512,256]{1,0:T(8,128)(2,1)S(1)}, bf16[512,256]{1,0:T(8,128)(2,1)S(1)}, u32[]{:S(2)}, u32[]{:S(2)}) collective-permute-start(bf16[512,256]{1,0:T(8,128)(2,1)S(1)} %broadcast_select_fusion), channel_id=1, source_target_pairs={{0,16},{8,24},{16,0},{24,8},{1,17},{9,25},{17,1},{25,9},{2,18},{10... | collective-permute-start | bytes 786440 | tf_op jit(solution)/shard_map/ppermute | solution.py:101
  41.6 6.4 %collective-permute-start.8 = (bf16[512,256]{1,0:T(8,128)(2,1)S(1)}, bf16[512,256]{1,0:T(8,128)(2,1)S(1)}, u32[]{:S(2)}, u32[]{:S(2)}) collective-permute-start(bf16[512,256]{1,0:T(8,128)(2,1)S(1)} %broadcast_select_fusion.1), channel_id=1, source_target_pairs={{0,8},{8,0},{16,24},{24,16},{1,9},{9,1},{17,25},{25,17},{2,10},{10... | collective-permute-start | bytes 786440 | tf_op jit(solution)/shard_map/ppermute | solution.py:101
  48.0 12.9 %collective-permute-start.15 = (bf16[256,1024]{1,0:T(8,128)(2,1)S(1)}, bf16[256,1024]{1,0:T(8,128)(2,1)S(1)}, u32[]{:S(2)}, u32[]{:S(2)}) collective-permute-start(bf16[256,1024]{1,0:T(8,128)(2,1)S(1)} %copy-done.4), channel_id=1, source_target_pairs={{0,2},{2,4},{4,6},{3,1},{5,3},{7,5},{6,7},{1,0},{8,10},{10,12},{12... | collective-permute-start | bytes 1572872 | tf_op jit(solution)/shard_map/ppermute | solution.py:165
  50.8 11.1 %collective-permute-start.16 = (bf16[256,1024]{1,0:T(8,128)(2,1)S(1)}, bf16[256,1024]{1,0:T(8,128)(2,1)S(1)}, u32[]{:S(2)}, u32[]{:S(2)}) collective-permute-start(bf16[256,1024]{1,0:T(8,128)(2,1)S(1)} %copy-done.4), channel_id=1, source_target_pairs={{1,3},{3,5},{5,7},{2,0},{4,2},{6,4},{7,6},{0,1},{9,11},{11,13},{13... | collective-permute-start | bytes 1572872 | tf_op jit(solution)/shard_map/ppermute | solution.py:165
  51.5 14.3 %collective-permute-start.11 = (bf16[512,512]{1,0:T(8,128)(2,1)S(1)}, bf16[512,512]{1,0:T(8,128)(2,1)S(1)}, u32[]{:S(2)}, u32[]{:S(2)}) collective-permute-start(bf16[512,512]{1,0:T(8,128)(2,1)S(1)} %maximum_select_fusion.1), channel_id=1, source_target_pairs={{0,16},{8,24},{16,0},{24,8},{1,17},{9,25},{17,1},{25,9},{2,18},{10... | collective-permute-start | bytes 1572872 | tf_op jit(solution)/shard_map/ppermute | solution.py:101
  52.9 12.1 %collective-permute-start.10 = (bf16[512,512]{1,0:T(8,128)(2,1)S(1)}, bf16[512,512]{1,0:T(8,128)(2,1)S(1)}, u32[]{:S(2)}, u32[]{:S(2)}) collective-permute-start(bf16[512,512]{1,0:T(8,128)(2,1)S(1)} %maximum_select_fusion), channel_id=1, source_target_pairs={{0,8},{8,0},{16,24},{24,16},{1,9},{9,1},{17,25},{25,17},{2,10},{10... | collective-permute-start | bytes 1572872 | tf_op jit(solution)/shard_map/ppermute | solution.py:101
  55.1 7.3 %slice-start = ((s8[8388608]{0:T(1024)(128)(4,1)}), s8[4194304]{0:T(1024)(128)(4,1)S(1)}, s32[]{:S(2)}) async-start(s8[8388608]{0:T(1024)(128)(4,1)} %bitcast.104), calls=%async_computation | async-start | bytes 8388608
  56.1 6.3 %slice-start.1 = ((s8[8388608]{0:T(1024)(128)(4,1)}), s8[4194304]{0:T(1024)(128)(4,1)S(1)}, s32[]{:S(2)}) async-start(s8[8388608]{0:T(1024)(128)(4,1)} %bitcast.104), calls=%async_computation.1 | async-start | bytes 8388608
  68.4 23.7 %collective-permute-start.19 = (bf16[256,1024]{1,0:T(8,128)(2,1)S(1)}, bf16[256,1024]{1,0:T(8,128)(2,1)S(1)}, u32[]{:S(2)}, u32[]{:S(2)}) collective-permute-start(bf16[256,1024]{1,0:T(8,128)(2,1)S(1)} %add_convert_fusion.14), channel_id=1, source_target_pairs={{0,2},{2,4},{4,6},{3,1},{5,3},{7,5},{6,7},{1,0},{8,10},{10,12},{12... | collective-permute-start | bytes 1572872 | tf_op jit(solution)/shard_map/ppermute | solution.py:165
  69.0 23.3 %collective-permute-start.20 = (bf16[256,1024]{1,0:T(8,128)(2,1)S(1)}, bf16[256,1024]{1,0:T(8,128)(2,1)S(1)}, u32[]{:S(2)}, u32[]{:S(2)}) collective-permute-start(bf16[256,1024]{1,0:T(8,128)(2,1)S(1)} %add_convert_fusion.13), channel_id=1, source_target_pairs={{1,3},{3,5},{5,7},{2,0},{4,2},{6,4},{7,6},{0,1},{9,11},{11,13},{13... | collective-permute-start | bytes 1572872 | tf_op jit(solution)/shard_map/ppermute | solution.py:165
  72.7 19.2 %collective-permute-start.17 = (bf16[256,1024]{1,0:T(8,128)(2,1)S(1)}, bf16[256,1024]{1,0:T(8,128)(2,1)S(1)}, u32[]{:S(2)}, u32[]{:S(2)}) collective-permute-start(bf16[256,1024]{1,0:T(8,128)(2,1)S(1)} %add_convert_fusion.16), channel_id=1, source_target_pairs={{0,2},{2,4},{4,6},{3,1},{5,3},{7,5},{6,7},{1,0},{8,10},{10,12},{12... | collective-permute-start | bytes 1572872 | tf_op jit(solution)/shard_map/ppermute | solution.py:165
  78.3 13.7 %collective-permute-start.18 = (bf16[256,1024]{1,0:T(8,128)(2,1)S(1)}, bf16[256,1024]{1,0:T(8,128)(2,1)S(1)}, u32[]{:S(2)}, u32[]{:S(2)}) collective-permute-start(bf16[256,1024]{1,0:T(8,128)(2,1)S(1)} %add_convert_fusion.15), channel_id=1, source_target_pairs={{1,3},{3,5},{5,7},{2,0},{4,2},{6,4},{7,6},{0,1},{9,11},{11,13},{13... | collective-permute-start | bytes 1572872 | tf_op jit(solution)/shard_map/ppermute | solution.py:165
  93.2 21.3 %collective-permute-start.23 = (bf16[256,1024]{1,0:T(8,128)(2,1)S(1)}, bf16[256,1024]{1,0:T(8,128)(2,1)S(1)}, u32[]{:S(2)}, u32[]{:S(2)}) collective-permute-start(bf16[256,1024]{1,0:T(8,128)(2,1)S(1)} %add_convert_fusion.11), channel_id=1, source_target_pairs={{0,2},{2,4},{4,6},{3,1},{5,3},{7,5},{6,7},{1,0},{8,10},{10,12},{12... | collective-permute-start | bytes 1572872 | tf_op jit(solution)/shard_map/ppermute | solution.py:165
  97.4 16.7 %collective-permute-start.21 = (bf16[256,1024]{1,0:T(8,128)(2,1)S(1)}, bf16[256,1024]{1,0:T(8,128)(2,1)S(1)}, u32[]{:S(2)}, u32[]{:S(2)}) collective-permute-start(bf16[256,1024]{1,0:T(8,128)(2,1)S(1)} %fusion.5), channel_id=1, source_target_pairs={{0,2},{2,4},{4,6},{3,1},{5,3},{7,5},{6,7},{1,0},{8,10},{10,12},{12... | collective-permute-start | bytes 1572872 | tf_op jit(solution)/shard_map/ppermute | solution.py:165
  101.0 13.3 %collective-permute-start.22 = (bf16[256,1024]{1,0:T(8,128)(2,1)S(1)}, bf16[256,1024]{1,0:T(8,128)(2,1)S(1)}, u32[]{:S(2)}, u32[]{:S(2)}) collective-permute-start(bf16[256,1024]{1,0:T(8,128)(2,1)S(1)} %add_convert_fusion.12), channel_id=1, source_target_pairs={{1,3},{3,5},{5,7},{2,0},{4,2},{6,4},{7,6},{0,1},{9,11},{11,13},{13... | collective-permute-start | bytes 1572872 | tf_op jit(solution)/shard_map/ppermute | solution.py:165
  101.5 16.7 %collective-permute-start.24 = (bf16[256,1024]{1,0:T(8,128)(2,1)S(1)}, bf16[256,1024]{1,0:T(8,128)(2,1)S(1)}, u32[]{:S(2)}, u32[]{:S(2)}) collective-permute-start(bf16[256,1024]{1,0:T(8,128)(2,1)S(1)} %add_convert_fusion.10), channel_id=1, source_target_pairs={{1,3},{3,5},{5,7},{2,0},{4,2},{6,4},{7,6},{0,1},{9,11},{11,13},{13... | collective-permute-start | bytes 1572872 | tf_op jit(solution)/shard_map/ppermute | solution.py:165
  125.9 42.7 %collective-permute-start.25 = (f32[512,1024]{1,0:T(8,128)}, f32[512,1024]{1,0:T(8,128)}, u32[]{:S(2)}, u32[]{:S(2)}) collective-permute-start(f32[512,1024]{1,0:T(8,128)} %add_add_fusion.1), channel_id=1, source_target_pairs={{0,1},{1,0},{2,3},{3,2},{4,5},{5,4},{6,7},{7,6},{8,9},{9,8},{10,11... | collective-permute-start | bytes 6291464 | tf_op jit(solution)/shard_map/ppermute | solution.py:162
  132.6 31.3 %collective-permute-start.26 = (bf16[256,1024]{1,0:T(8,128)(2,1)}, bf16[256,1024]{1,0:T(8,128)(2,1)}, u32[]{:S(2)}, u32[]{:S(2)}) collective-permute-start(bf16[256,1024]{1,0:T(8,128)(2,1)} %add_convert_fusion.6), channel_id=1, source_target_pairs={{0,2},{2,4},{4,6},{3,1},{5,3},{7,5},{6,7},{1,0},{8,10},{10,12},{12... | collective-permute-start | bytes 1572872 | tf_op jit(solution)/shard_map/ppermute | solution.py:165
  134.8 29.1 %collective-permute-start.27 = (bf16[256,1024]{1,0:T(8,128)(2,1)}, bf16[256,1024]{1,0:T(8,128)(2,1)}, u32[]{:S(2)}, u32[]{:S(2)}) collective-permute-start(bf16[256,1024]{1,0:T(8,128)(2,1)} %add_convert_fusion.5), channel_id=1, source_target_pairs={{1,3},{3,5},{5,7},{2,0},{4,2},{6,4},{7,6},{0,1},{9,11},{11,13},{13... | collective-permute-start | bytes 1572872 | tf_op jit(solution)/shard_map/ppermute | solution.py:165
  134.8 22.8 %collective-permute-start.28 = (bf16[256,1024]{1,0:T(8,128)(2,1)S(1)}, bf16[256,1024]{1,0:T(8,128)(2,1)S(1)}, u32[]{:S(2)}, u32[]{:S(2)}) collective-permute-start(bf16[256,1024]{1,0:T(8,128)(2,1)S(1)} %fusion.4), channel_id=1, source_target_pairs={{0,2},{2,4},{4,6},{3,1},{5,3},{7,5},{6,7},{1,0},{8,10},{10,12},{12... | collective-permute-start | bytes 1572872 | tf_op jit(solution)/shard_map/ppermute | solution.py:165
  136.8 21.5 %collective-permute-start.29 = (bf16[256,1024]{1,0:T(8,128)(2,1)S(1)}, bf16[256,1024]{1,0:T(8,128)(2,1)S(1)}, u32[]{:S(2)}, u32[]{:S(2)}) collective-permute-start(bf16[256,1024]{1,0:T(8,128)(2,1)S(1)} %add_convert_fusion.7), channel_id=1, source_target_pairs={{1,3},{3,5},{5,7},{2,0},{4,2},{6,4},{7,6},{0,1},{9,11},{11,13},{13... | collective-permute-start | bytes 1572872 | tf_op jit(solution)/shard_map/ppermute | solution.py:165
  157.6 0.8 copy-start.2
  158.4 0.8 copy-start.3

commit v2 on v1

--- a/solution.py
+++ b/solution.py
@@ -1,7 +1,10 @@
+import functools
+
 import jax
 import jax.numpy as jnp
 from jax import lax
 from jax.experimental import pallas as pl
+from jax.experimental.pallas import tpu as pltpu
 from jax.sharding import PartitionSpec as P
 
 
@@ -19,20 +22,23 @@
     return 1 - 2 * (parity % 2)
 
 
-def finish_kernel(signs, table, kept, own, first, second, master, moment, variance, *rest):
+def finish_kernel(start, signs, table, kept, own, first, second, master, moment, variance, *rest):
     new_master, new_moment, new_variance, scales = rest[-4:]
-    step = pl.program_id(0)
-    gradient = own[...]
+    tile = new_master.shape[0]
+    near = pl.ds(pl.multiple_of(pl.program_id(0) * tile, tile), tile)
+    far = pl.ds(pl.multiple_of(start + pl.program_id(0) * tile, tile), tile)
+    gradient = own[far, :]
     for line, received in enumerate((first, second)):
         wanted = kept[:, line : line + 1] > 0.0
-        gradient = gradient + jnp.where(wanted, received[...].astype(jnp.float32), 0.0)
-    first = 0.9 * moment[...] + 0.1 * gradient
-    second = 0.95 * variance[...] + 0.05 * gradient * gradient
-    corrected = first / (1.0 - 0.9**10)
-    spread = jnp.sqrt(second / (1.0 - 0.95**10)) + 1e-08
-    new_moment[...] = first
-    new_variance[...] = second
-    new_master[...] = master[...] - 0.01 * (corrected / spread + 0.1 * master[...])
+        gradient = gradient + jnp.where(wanted, received[near, :].astype(jnp.float32), 0.0)
+    first_moment = 0.9 * moment[far, :] + 0.1 * gradient
+    second_moment = 0.95 * variance[far, :] + 0.05 * gradient * gradient
+    corrected = first_moment / (1.0 - 0.9**10)
+    spread = jnp.sqrt(second_moment / (1.0 - 0.95**10)) + 1e-08
+    new_moment[...] = first_moment
+    new_variance[...] = second_moment
+    given = master[far, :]
+    new_master[...] = given - 0.01 * (corrected / spread + 0.1 * given)
     for place in range(gradient.shape[1] // BLOCK):
         columns = slice(place * BLOCK, (place + 1) * BLOCK)
         signed = gradient[:, columns] * signs[:, columns]
@@ -45,47 +51,35 @@
             for term in (high, low)
         )
         largest = jnp.max(jnp.abs(mixed), axis=0, keepdims=True)
-        row = step * (gradient.shape[1] // BLOCK) + place
-        scales[pl.ds(row, 1), :] = largest * (1.0 / BLOCK**0.5)
-
-
-def finish(
-    part, parts, signs, table, kept, own, first, second, master, moment, variance, before
-):
-    rows, width = master.shape
-    size = rows // parts
-    tile = min(width, 512)
-    whole = pl.BlockSpec((size, tile), lambda k: (part, k))
-    piece = pl.BlockSpec((size, tile), lambda k: (0, k))
-    given = [
-        pl.BlockSpec((1, tile), lambda k: (0, k)),
-        pl.BlockSpec((BLOCK, BLOCK), lambda k: (0, 0)),
-        pl.BlockSpec((1, 2), lambda k: (0, 0)),
-        whole,
-        piece,
-        piece,
-        whole,
-        whole,
-        whole,
-    ]
-    held = [pl.BlockSpec(memory_space=pl.ANY)] * len(before)
+        scales[place : place + 1, :] = largest * (1.0 / BLOCK**0.5)
+
+
+def finish(start, given, before):
+    rows, width = given[-1].shape
+    size = given[4].shape[0]
+    tile = min(size, 128)
+    first = start // tile
+    whole = pl.BlockSpec((tile, width), lambda k: (first + k, 0))
+    given = [pltpu.with_memory_space_constraint(value, pltpu.VMEM) for value in given]
     return pl.pallas_call(
-        finish_kernel,
-        grid=(width // tile,),
-        in_specs=given + held,
+        functools.partial(finish_kernel, start),
+        grid=(size // tile,),
+        in_specs=[pl.BlockSpec(memory_space=pltpu.VMEM)] * len(given)
+        + [pl.BlockSpec(memory_space=pl.ANY)] * len(before),
         out_specs=[
             whole,
             whole,
             whole,
-            pl.BlockSpec((width // BLOCK, size), lambda k: (0, part)),
+            pl.BlockSpec((width // BLOCK, tile), lambda k: (0, first + k)),
         ],
-        out_shape=[jax.ShapeDtypeStruct(master.shape, jnp.float32)] * 3
+        out_shape=[jax.ShapeDtypeStruct((rows, width), jnp.float32)] * 3
         + [jax.ShapeDtypeStruct((width // BLOCK, rows), jnp.float32)],
         input_output_aliases={len(given) + k: k for k in range(len(before))},
-    )(signs, table, kept, own, first, second, master, moment, variance, *before)
-
-
-def gather_tokens(lows, highs, outer):
+        compiler_params=pltpu.CompilerParams(vmem_limit_bytes=16 * tile * width * 4),
+    )(*given, *before)
+
+
+def gather_tokens(lows, highs, outer, inner):
     parts = len(lows)
     if outer != 4:
         every = []
@@ -95,46 +89,50 @@
                 every += [(whole[k], which, part, k) for k in range(outer)]
         return every, None
     me = lax.axis_index("outer")
+    core = lax.axis_index("inner") % 2
     even = (me == 0) | (me == 3)
-
-    def across(value, distance):
-        return lax.ppermute(value, "outer", [(k, k ^ distance) for k in range(outer)])
-
-    near, far, corner = me ^ 1, me ^ 2, me ^ 3
-    near_low = [across(lows[k], 1) for k in range(parts)]
-    far_high = [across(highs[k], 2) for k in range(parts)]
-    second_near = [across(jnp.where(even, highs[k], far_high[k]), 1) for k in range(parts)]
-    second_far = [across(jnp.where(even, lows[k], near_low[k]), 2) for k in range(parts)]
-    all_of = [jnp.concatenate(pieces, axis=1) for pieces in (lows, highs, near_low, far_high)]
-    third_near = across(jnp.where(even, all_of[3], all_of[1]), 1)
-    third_far = across(jnp.where(even, all_of[2], all_of[0]), 2)
+    distances = ((1, 2), (2, 1))
+
+    def across(value, turn):
+        pairs = []
+        for place in range(outer):
+            for index in range(inner):
+                other = place ^ distances[index % 2][turn]
+                pairs.append((place * inner + index, other * inner + index))
+        return lax.ppermute(value, ("outer", "inner"), pairs)
+
+    one = me ^ jnp.where(core == 0, 1, 2)
+    two = me ^ jnp.where(core == 0, 2, 1)
+    corner = me ^ 3
+    low_of_one = [across(lows[k], 0) for k in range(parts)]
+    high_of_two = [across(highs[k], 1) for k in range(parts)]
+    second_low = [across(jnp.where(even, lows[k], low_of_one[k]), 1) for k in range(parts)]
+    second_high = [across(jnp.where(even, highs[k], high_of_two[k]), 0) for k in range(parts)]
+    every = [jnp.concatenate(pieces, axis=1) for pieces in (lows, highs, low_of_one, high_of_two)]
+    third_low = across(jnp.where(even, every[2], every[0]), 1)
+    third_high = across(jnp.where(even, every[3], every[1]), 0)
 
     def end_block(owner, part):
-        one = jnp.where(
-            owner == me,
-            lows[part],
-            jnp.where(owner == near, near_low[part], second_far[part]),
+        low = jnp.where(owner == one, low_of_one[part], second_low[part])
+        high = jnp.where(owner == two, high_of_two[part], second_high[part])
+        return (
+            jnp.where(owner == me, lows[part], low),
+            jnp.where(owner == me, highs[part], high),
         )
-        two = jnp.where(
-            owner == me,
-            highs[part],
-            jnp.where(owner == far, far_high[part], second_near[part]),
-        )
-        return one, two
 
     every = []
     for k in range(parts):
         every += [
             (lows[k], 0, k, me),
             (highs[k], 1, k, me),
-            (near_low[k], 0, k, near),
-            (far_high[k], 1, k, far),
-            (second_near[k], 1, k, jnp.where(even, corner, near)),
-            (second_far[k], 0, k, jnp.where(even, corner, far)),
+            (low_of_one[k], 0, k, one),
+            (high_of_two[k], 1, k, two),
+            (second_high[k], 1, k, jnp.where(even, corner, one)),
+            (second_low[k], 0, k, jnp.where(even, corner, two)),
         ]
     every += [
-        (third_near, 1, 0, jnp.where(even, near, corner)),
-        (third_far, 0, 0, jnp.where(even, far, corner)),
+        (third_high, 1, 0, jnp.where(even, one, corner)),
+        (third_low, 0, 0, jnp.where(even, two, corner)),
     ]
     return every, end_block
 
@@ -189,11 +187,14 @@
                 axis=1,
             )
 
-        cut = [columns_of(which, part) for which in (core, 1 - core) for part in range(parts)]
-        cut = lax.optimization_barrier(cut)
-        lows = cut[:parts]
-        highs = [swap(cut[parts + k]) for k in range(parts)]
-        pieces, end_block = gather_tokens(lows, highs, outer)
+        lows, highs = [], []
+        for part in range(parts):
+            low, high = lax.optimization_barrier(
+                (columns_of(core, part), columns_of(1 - core, part))
+            )
+            lows.append(low)
+            highs.append(swap(high))
+        pieces, end_block = gather_tokens(lows, highs, outer, inner)
         if chips != outer:
             end_block = None
         kept = [jnp.where(place == 0, 0.0, 1.0) for place in places]
@@ -237,8 +238,14 @@
                 for which in (0, 1)
             ]
 
-        halves = [weight_delta[k * size : (k + 1) * size] for k in range(parts)]
-        message = [halves, halves]
+        def pieces_of(turn):
+            found = [(k, 0, size) for k in range(parts)]
+            if turn == chips and size % 256 == 0:
+                half = size // 2
+                found[-1:] = [(parts - 1, 0, half), (parts - 1, half, half)]
+            return found
+
+        message = [[weight_delta], [weight_delta]]
         history = ([], [])
         cache = weight_cache
         caches = [cache]
@@ -254,17 +261,21 @@
             if turn == min(2, chips - 1):
                 own = lax.optimization_barrier(partial_sum(chip))
             message = [[], []]
-            for k in range(parts):
-                rows_of = slice(k * size, (k + 1) * size)
+            for k, offset, height in pieces_of(turn + 1):
+                rows_of = slice(k * size + offset, k * size + offset + height)
+                inside = slice(offset, offset + height)
                 for line in (0, 1):
                     received, place = history[line][-1], places[line]
                     if terms:
                         term = terms[line][rows_of]
                     else:
                         one, two = end_block(turned(line, chips - 1), k)
-                        term = contract(one, cotangent) + contract(two, cotangent_other)
+                        term = contract(one[:, inside], cotangent)
+                        term = term + contract(two[:, inside], cotangent_other)
                         term = jnp.where(turn <= place, jnp.float32(0), term)
-                    before = jnp.where(place == 0, jnp.bfloat16(0), received[k])
+                    whole = len(received) == 1
+                    before = received[0][rows_of] if whole else received[k][inside]
+                    before = jnp.where(place == 0, jnp.bfloat16(0), before)
                     value = (before.astype(jnp.float32) + term).astype(jnp.bfloat16)
                     cache, value, cotangent_other, *terms = lax.optimization_barrier(
                         (cache, value, cotangent_other, *terms)
@@ -272,13 +283,19 @@
                     message[line].append(value)
             caches.append(cache)
 
-        last = [[along(line, message[line][k]) for line in (0, 1)] for k in range(parts)]
+        last = [[along(line, message[line][k]) for line in (0, 1)] for k in range(len(message[0]))]
+
+        def cut(values):
+            if len(values) == parts:
+                return values
+            return [values[0][k * size : (k + 1) * size] for k in range(parts)]
+
         mine, other = products(chip, [weight_delta], caches[1])
         mine, other = mine[0], other[0]
         order = sorted(range(1, chips), key=lambda t: max(t, chips - t))
         later = []
         for number, turn in enumerate(order, 1):
-            passed = [history[0][turn - 1], history[1][chips - turn - 1]]
+            passed = [cut(history[0][turn - 1]), cut(history[1][chips - turn - 1])]
             deltas = [jnp.where(turn <= places[0], one, two) for one, two in zip(*passed)]
             source = turned(0, lax.rem(places[0] - turn + chips, chips))
             ones, twos = products(source, deltas, caches[max(turn, chips - turn)])
@@ -295,10 +312,9 @@
         output = mine
 
         done = []
-        for k in range(parts):
-            done = finish(
-                k, parts, signs, table, kept, own, *last[k], master, moment, variance, done
-            )
+        for number, (k, offset, _) in enumerate(pieces_of(chips)):
+            given = [signs, table, kept, own, *last[number], master, moment, variance]
+            done = finish(k * size + offset, given, done)
         new_master, new_moment, new_variance, scales = done
         return (output, new_master, new_moment, new_variance, scales.T)
 

time: 173 us -> 148 us (0.86)
  waiting for transfers between devices: 68.6 us -> 59.2 us
  starting transfers between devices: 31.7 us -> 26.9 us
  local copies, waits for them, and re-layouts: 20 us -> 16.4 us
  Pallas kernels: 9.38 us -> 6.5 us
  other arithmetic: 8.7 us -> 6.87 us
  matrix products: 32.4 us -> 30.6 us
    ppermute x16, waiting for transfers between devices: 51.6 us -> 42.3 us  [along(): return lax.ppermute(value, 'inner', line_pairs[line])]
    ppermute x10, starting transfers between devices: 14.4 us -> 8.07 us  [across(): return lax.ppermute(value, ('outer', 'inner'), pairs)]
    pallas_call x2 -> x3, Pallas kernels: 9.38 us -> 6.5 us  [finish(): pl.pallas_call(functools.partial(finish_kernel, start), grid=(size // til...]
    dot_general x14, matrix products: 13.3 us -> 10.5 us  [products(): jnp.dot(tokens_for(chip_index, which)[:, part * height:][:, :height], wei...]
    convert_element_type x3, other arithmetic: 2.54 us -> 4.98 us  [products(): weights.append(lax.optimization_barrier(weight.astype(jnp.bfloat16)))]
  transfers between devices with their start and end apart: 30 -> 30, of which waited for: 13 -> 14; matrix products, arithmetic and copies ran while one was open for 25% -> 27% of each run, Pallas kernels for 5% -> 4%
where the time goes in v2:
time: 148 us
  waiting for transfers between devices  59.2 us (40%)
  matrix products  30.6 us (21%)
  starting transfers between devices  26.9 us (18%)
  local copies, waits for them, and re-layouts  16.4 us (11%)
  other arithmetic  6.87 us (5%)
  Pallas kernels  6.5 us (4%)
    ppermute x16, waiting for transfers between devices, along(): return lax.ppermute(value, 'inner', line_pairs[line])  42.3 us
    dot_general x18, matrix products, contract(): lax.dot_general(left, right, (((0,), (0,)), ((), ())), preferred_element_...  20.1 us
    ppermute x10, waiting for transfers between devices, across(): return lax.ppermute(value, ('outer', 'inner'), pairs)  16.9 us
    ppermute x16, starting transfers between devices, along(): return lax.ppermute(value, 'inner', line_pairs[line])  15.8 us
    dynamic_update_slice x14, local copies, waits for them, and re-layouts, body(): lax.dynamic_update_slice(held, piece, (owner, which * count, 0, part * si...  10.5 us
    dot_general x14, matrix products, products(): jnp.dot(tokens_for(chip_index, which)[:, part * height:][:, :height], wei...  10.5 us
    ppermute x10, starting transfers between devices, across(): return lax.ppermute(value, ('outer', 'inner'), pairs)  8.07 us
    pallas_call x3, Pallas kernels, finish(): pl.pallas_call(functools.partial(finish_kernel, start), grid=(size // til...  6.5 us
  transfers between devices with their start and end apart: 30, of which 14 were waited for; matrix products, arithmetic and copies ran while one was open for 27% of the time, Pallas kernels for 4%

profile of v2, /device:TPU:0, one launch (start us, length us, event | category | flops | bytes accessed | tf_op | source)
XLA Modules:
  0.0 147.8 jit_solution(10349013405912461601)
XLA Ops:
  0.7 1.3 constant_dynamic-slice_fusion
  2.5 2.6 %collective-permute-start.12 = (bf16[512,1024]{1,0:T(8,128)(2,1)}, bf16[512,1024]{1,0:T(8,128)(2,1)}, u32[]{:S(2)}, u32[]{:S(2)}) collective-permute-start(bf16[512,1024]{1,0:T(8,128)(2,1)} %param.11), channel_id=1, source_target_pairs={{0,2},{2,4},{4,6},{3,1},{5,3},{7,5},{6,7},{1,0},{8,10},{10,12},{12... | collective-permute-start | bytes 3145736 | tf_op jit(solution)/shard_map/ppermute | solution.py:163
  5.1 1.5 %collective-permute-start.1 = (bf16[512,256]{1,0:T(8,128)(2,1)S(1)}, bf16[512,256]{1,0:T(8,128)(2,1)S(1)}, u32[]{:S(2)}, u32[]{:S(2)}) collective-permute-start(bf16[512,256]{1,0:T(8,128)(2,1)S(1)} %get-tuple-element.71), channel_id=1, source_target_pairs={{0,8},{1,17},{2,10},{3,19},{4,12},{5,21},{6,14},{7,23},{8,0},{9,25... | collective-permute-start | bytes 786440 | tf_op jit(solution)/shard_map/ppermute | solution.py:102
  7.1 2.3 %reshape.100 = bf16[4,1024,512]{2,1,0:T(8,128)(2,1)} broadcast(bf16[]{:T(256)} %constant.187.clone.1), dimensions={} | broadcast | bytes 4194306 | tf_op jit(solution)/shard_map/reshape | solution.py:209
  9.4 0.7 bitcast_dynamic-update-slice_fusion.13
  10.5 0.9 collective-permute-done.1
  11.8 1.4 collective-permute-start.13
  14.3 1.5 %collective-permute-start.7 = (bf16[512,256]{1,0:T(8,128)(2,1)S(1)}, bf16[512,256]{1,0:T(8,128)(2,1)S(1)}, u32[]{:S(2)}, u32[]{:S(2)}) collective-permute-start(bf16[512,256]{1,0:T(8,128)(2,1)S(1)} %collective-permute-done.5), channel_id=1, source_target_pairs={{0,16},{1,9},{2,18},{3,11},{4,20},{5,13},{6,22},{7,15},{8,24},{9,1... | collective-permute-start | bytes 786440 | tf_op jit(solution)/shard_map/ppermute | solution.py:102
  15.8 0.7 bitcast_dynamic-update-slice_fusion.12
  16.6 0.7 bitcast_dynamic-update-slice_fusion.11
  17.4 2.1 %collective-permute-done.2 = bf16[512,256]{1,0:T(8,128)(2,1)S(1)} collective-permute-done((bf16[512,256]{1,0:T(8,128)(2,1)S(1)}, bf16[512,256]{1,0:T(8,128)(2,1)S(1)}, u32[]{:S(2)}, u32[]{:S(2)}) %collective-permute-start.2) | collective-permute-done | bytes 262176 | tf_op jit(solution)/shard_map/ppermute | solution.py:102
  20.1 2.3 %collective-permute-done.7 = bf16[512,256]{1,0:T(8,128)(2,1)S(1)} collective-permute-done((bf16[512,256]{1,0:T(8,128)(2,1)S(1)}, bf16[512,256]{1,0:T(8,128)(2,1)S(1)}, u32[]{:S(2)}, u32[]{:S(2)}) %collective-permute-start.7) | collective-permute-done | bytes 262176 | tf_op jit(solution)/shard_map/ppermute | solution.py:102
  22.9 0.7 bitcast_dynamic-update-slice_fusion.10
  23.8 4.9 %collective-permute-done.3 = bf16[512,256]{1,0:T(8,128)(2,1)S(1)} collective-permute-done((bf16[512,256]{1,0:T(8,128)(2,1)S(1)}, bf16[512,256]{1,0:T(8,128)(2,1)S(1)}, u32[]{:S(2)}, u32[]{:S(2)}) %collective-permute-start.3) | collective-permute-done | bytes 262176 | tf_op jit(solution)/shard_map/ppermute | solution.py:102
  29.2 0.7 bitcast_dynamic-update-slice_fusion.9
  30.0 1.0 collective-permute-start.8
  31.0 0.7 bitcast_dynamic-update-slice_fusion.8
  31.7 0.8 bitcast_dynamic-update-slice_fusion.7
  32.5 0.7 bitcast_dynamic-update-slice_fusion.6
  33.2 0.7 bitcast_dynamic-update-slice_fusion.5
  33.9 0.7 bitcast_dynamic-update-slice_fusion.4
  34.7 2.4 %collective-permute-done.8 = bf16[512,256]{1,0:T(8,128)(2,1)S(1)} collective-permute-done((bf16[512,256]{1,0:T(8,128)(2,1)S(1)}, bf16[512,256]{1,0:T(8,128)(2,1)S(1)}, u32[]{:S(2)}, u32[]{:S(2)}) %collective-permute-start.8) | collective-permute-done | bytes 262176 | tf_op jit(solution)/shard_map/ppermute | solution.py:102
  37.1 0.8 collective-permute-start.11
  37.9 0.7 bitcast_dynamic-update-slice_fusion.3
  38.6 0.7 collective-permute-start.10
  39.3 0.8 bitcast_dynamic-update-slice_fusion.2
  40.6 1.6 %add_convert_fusion.14 = bf16[256,1024]{1,0:T(8,128)(2,1)S(1)} fusion(f32[256,1024]{1,0:T(8,128)S(1)} %fusion.62, bf16[512,1024]{1,0:T(8,128)(2,1)S(1)} %copy-done.3, pred[]{:T(512)S(6)} %ge.12, pred[]{:T(512)S(6)} %eq.32, bf16[512,1024]{1,0:T(8,128)(2,1)} %collective-permute-done.12, bf16[512,256]{1,0:T(8,128)(2,1)S(1)} %get-tuple-element.71, ...), kind=kOutput, calls=%fused_computation.38 | convolution fusion | flops 270270464 | bytes 3932164 | tf_op jit(solution)/shard_map/dot_general | solution.py:141
  43.6 1.8 %add_convert_fusion.12 = bf16[256,1024]{1,0:T(8,128)(2,1)S(1)} fusion(f32[256,1024]{1,0:T(8,128)S(1)} %fusion.52, bf16[512,1024]{1,0:T(8,128)(2,1)S(1)} %copy-done.3, pred[]{:T(512)S(6)} %ge.12, pred[]{:T(512)S(6)} %eq.32, bf16[512,1024]{1,0:T(8,128)(2,1)} %collective-permute-done.12, bf16[512,256]{1,0:T(8,128)(2,1)S(1)} %get-tuple-element.73, ...), kind=kOutput, calls=%fused_computation.36 | convolution fusion | flops 270270464 | bytes 3932164 | tf_op jit(solution)/shard_map/dot_general | solution.py:141
  46.5 1.6 %add_convert_fusion = bf16[512,1024]{1,0:T(8,128)(2,1)S(1)} fusion(bf16[512,1024]{1,0:T(8,128)(2,1)} %param.11, bf16[4096,1024]{1,0:T(8,128)(2,1)S(1)} %bitcast.108, s32[]{:T(128)S(6)} %select_n.547), kind=kLoop, calls=%fused_computation.6 | loop fusion | flops 2097152 | bytes 3145732 | tf_op jit(solution)/shard_map/convert_element_type | solution.py:228
  48.1 3.6 %collective-permute-done.10 = bf16[512,512]{1,0:T(8,128)(2,1)S(1)} collective-permute-done((bf16[512,512]{1,0:T(8,128)(2,1)S(1)}, bf16[512,512]{1,0:T(8,128)(2,1)S(1)}, u32[]{:S(2)}, u32[]{:S(2)}) %collective-permute-start.10) | collective-permute-done | bytes 524320 | tf_op jit(solution)/shard_map/ppermute | solution.py:102
  51.7 0.8 bitcast_dynamic-update-slice_fusion.1
  52.6 0.8 bitcast_dynamic-update-slice_fusion
  53.4 1.8 %fusion.16 = f32[512,1024]{1,0:T(8,128)S(1)} fusion(bf16[512,1024]{1,0:T(8,128)(2,1)S(1)} %add_convert_fusion, bf16[4,1024,512]{2,1,0:T(8,128)(2,1)} %bitcast_dynamic-update-slice_fusion, s32[]{:T(128)S(6)} %select_n.508), kind=kOutput, calls=%fused_computation.51 | convolution fusion | flops 536870912 | bytes 3670020 | tf_op jit(solution)/shard_map/dot_general | solution.py:231
  55.2 1.6 %collective-permute-start.17 = (bf16[256,1024]{1,0:T(8,128)(2,1)S(1)}, bf16[256,1024]{1,0:T(8,128)(2,1)S(1)}, u32[]{:S(2)}, u32[]{:S(2)}) collective-permute-start(bf16[256,1024]{1,0:T(8,128)(2,1)S(1)} %add_convert_fusion.12), channel_id=1, source_target_pairs={{0,2},{2,4},{4,6},{3,1},{5,3},{7,5},{6,7},{1,0},{8,10},{10,12},{12... | collective-permute-start | bytes 1572872 | tf_op jit(solution)/shard_map/ppermute | solution.py:163
  56.8 2.2 %dynamic-slice_bitcast_fusion = (bf16[512,512]{1,0:T(8,128)(2,1)S(1)}, bf16[512,512]{1,0:T(8,128)(2,1)S(1)}, bf16[512,512]{1,0:T(8,128)(2,1)S(1)}, bf16[512,512]...) fusion(bf16[4,1024,512]{2,1,0:T(8,128)(2,1)} %bitcast_dynamic-update-slice_fusion, ...), kind=kLoop, calls=%fused_computation.55 | loop fusion | bytes 6291468 | tf_op jit(solution)/shard_map/squeeze | solution.py:213
  59.0 0.7 fusion.99
  59.7 0.7 add_select_fusion.3
  60.5 2.0 %collective-permute-start.15 = (bf16[256,1024]{1,0:T(8,128)(2,1)S(1)}, bf16[256,1024]{1,0:T(8,128)(2,1)S(1)}, u32[]{:S(2)}, u32[]{:S(2)}) collective-permute-start(bf16[256,1024]{1,0:T(8,128)(2,1)S(1)} %add_convert_fusion.14), channel_id=1, source_target_pairs={{0,2},{2,4},{4,6},{3,1},{5,3},{7,5},{6,7},{1,0},{8,10},{10,12},{12... | collective-permute-start | bytes 1572872 | tf_op jit(solution)/shard_map/ppermute | solution.py:163
  62.5 1.8 %fusion.12 = f32[512,1024]{1,0:T(8,128)S(1)} fusion(bf16[512,1024]{1,0:T(8,128)(2,1)S(1)} %collective-permute-done.13, bf16[4,1024,512]{2,1,0:T(8,128)(2,1)} %bitcast_dynamic-update-slice_fusion, s32[]{:T(128)S(6)} %select_n.555), kind=kOutput, calls=%fused_computation.47 | convolution fusion | flops 536870912 | bytes 3670020 | tf_op jit(solution)/shard_map/dot_general | solution.py:141
  64.3 1.8 %add_select_fusion.2 = f32[512,1024]{1,0:T(8,128)S(1)} fusion(f32[512,1024]{1,0:T(8,128)S(1)} %fusion.12, bf16[512,1024]{1,0:T(8,128)(2,1)S(1)} %copy-done.3, pred[]{:T(512)S(6)} %ge.29, bf16[4,1024,512]{2,1,0:T(8,128)(2,1)} %bitcast_dynamic-update-slice_fusion, s32[]{:T(128)S(6)} %select_n.555), kind=kOutput, calls=%fused_computation.4 | convolution fusion | flops 537919488 | bytes 5767173 | tf_op jit(solution)/shard_map/dot_general | solution.py:141
  66.1 1.8 %fusion.6 = f32[512,1024]{1,0:T(8,128)S(1)} fusion(bf16[512,1024]{1,0:T(8,128)(2,1)S(1)} %collective-permute-done.13, bf16[4,1024,512]{2,1,0:T(8,128)(2,1)} %bitcast_dynamic-update-slice_fusion, s32[]{:T(128)S(6)} %select_n.508), kind=kOutput, calls=%fused_computation.41 | convolution fusion | flops 536870912 | bytes 3670020 | tf_op jit(solution)/shard_map/dot_general | solution.py:141
  67.9 11.7 %collective-permute-done.15 = bf16[256,1024]{1,0:T(8,128)(2,1)S(1)} collective-permute-done((bf16[256,1024]{1,0:T(8,128)(2,1)S(1)}, bf16[256,1024]{1,0:T(8,128)(2,1)S(1)}, u32[]{:S(2)}, u32[]{:S(2)}) %collective-permute-start.15) | collective-permute-done | bytes 524320 | tf_op jit(solution)/shard_map/ppermute | solution.py:163
  80.9 0.6 add_convert_fusion.6
  81.6 1.9 %collective-permute-start.21 = (bf16[256,1024]{1,0:T(8,128)(2,1)S(1)}, bf16[256,1024]{1,0:T(8,128)(2,1)S(1)}, u32[]{:S(2)}, u32[]{:S(2)}) collective-permute-start(bf16[256,1024]{1,0:T(8,128)(2,1)S(1)} %add_convert_fusion.9), channel_id=1, source_target_pairs={{0,2},{2,4},{4,6},{3,1},{5,3},{7,5},{6,7},{1,0},{8,10},{10,12},{12... | collective-permute-start | bytes 1572872 | tf_op jit(solution)/shard_map/ppermute | solution.py:163
  83.5 0.7 fusion.100
  84.3 0.9 add_select_fusion.1
  85.7 1.8 %fusion.9 = f32[512,1024]{1,0:T(8,128)S(1)} fusion(bf16[512,1024]{1,0:T(8,128)(2,1)S(1)} %collective-permute-done.13, bf16[4,1024,512]{2,1,0:T(8,128)(2,1)} %bitcast_dynamic-update-slice_fusion, s32[]{:T(128)S(6)} %select_n.574), kind=kOutput, calls=%fused_computation.44 | convolution fusion | flops 536870912 | bytes 3670020 | tf_op jit(solution)/shard_map/dot_general | solution.py:141
  87.5 1.8 %add_select_fusion = f32[512,1024]{1,0:T(8,128)S(1)} fusion(f32[512,1024]{1,0:T(8,128)S(1)} %fusion.9, bf16[512,1024]{1,0:T(8,128)(2,1)S(1)} %copy-done.3, pred[]{:T(512)S(6)} %ge.31, bf16[4,1024,512]{2,1,0:T(8,128)(2,1)} %bitcast_dynamic-update-slice_fusion, s32[]{:T(128)S(6)} %select_n.574), kind=kOutput, calls=%fused_computation.2 | convolution fusion | flops 537919488 | bytes 5767173 | tf_op jit(solution)/shard_map/dot_general | solution.py:141
  90.2 11.7 %collective-permute-done.19 = bf16[256,1024]{1,0:T(8,128)(2,1)S(1)} collective-permute-done((bf16[256,1024]{1,0:T(8,128)(2,1)S(1)}, bf16[256,1024]{1,0:T(8,128)(2,1)S(1)}, u32[]{:S(2)}, u32[]{:S(2)}) %collective-permute-start.19) | collective-permute-done | bytes 524320 | tf_op jit(solution)/shard_map/ppermute | solution.py:163
  102.4 3.7 %collective-permute-done.22 = bf16[256,1024]{1,0:T(8,128)(2,1)S(1)} collective-permute-done((bf16[256,1024]{1,0:T(8,128)(2,1)S(1)}, bf16[256,1024]{1,0:T(8,128)(2,1)S(1)}, u32[]{:S(2)}, u32[]{:S(2)}) %collective-permute-start.22) | collective-permute-done | bytes 524320 | tf_op jit(solution)/shard_map/ppermute | solution.py:163
  106.4 2.7 %add_convert_fusion.1 = (bf16[256,1024]{1,0:T(8,128)(2,1)S(1)}, bf16[256,1024]{1,0:T(8,128)(2,1)S(1)}, bf16[256,1024]{1,0:T(8,128)(2,1)S(1)}, bf16[256,1024]{1,0:T(8,128)(2,1)S(1)}) fusion(bf16[256,1024]{1,0:T(8,128)(2,1)S(1)} %collective-permute-done.21, bf16[4096,1024]{1,0:T(8,128)(2,1)S(1)} %bitcast.108, s32[]{:T(128)S(6)} %select_n.590, pred[]{:T(512)S(6)} %ge.30, ...), kind=kLoop, calls=%fused_computation.25 | loop fusion | flops 5242880 | bytes 8388626 | tf_op jit(solution)/shard_map/convert_element_type | solution.py:228
  110.9 2.1 %add_add_fusion.1 = f32[512,1024]{1,0:T(8,128)S(1)} fusion(f32[512,1024]{1,0:T(8,128)S(1)} %fusion.30, f32[512,1024]{1,0:T(8,128)S(1)} %fusion.32, f32[512,1024]{1,0:T(8,128)S(1)} %fusion.34, f32[512,1024]{1,0:T(8,128)S(1)} %fusion.36, f32[512,1024]{1,0:T(8,128)S(1)} %fusion.38, f32[512,1024]{1,0:T(8,128)S(1)} %fusion.40, ...), kind=kOutput, calls=%fused_computation.1 | convolution fusion | flops 540016640 | bytes 16252932 | tf_op jit(solution)/shard_map/dot_general | solution.py:231
  113.0 1.2 collective-permute-start.23
  114.1 1.8 %convolution_add_fusion.own = f32[512,1024]{1,0:T(8,128)S(1)} fusion(f32[512,1024]{1,0:T(8,128)S(1)} %fusion.6, bf16[512,1024]{1,0:T(8,128)(2,1)S(1)} %copy-done.3, bf16[4,1024,512]{2,1,0:T(8,128)(2,1)} %bitcast_dynamic-update-slice_fusion, s32[]{:T(128)S(6)} %select_n.508), kind=kOutput, calls=%fused_computation.7 | convolution fusion | flops 537395200 | bytes 5767172 | tf_op jit(solution)/shard_map/dot_general | solution.py:141
  116.8 2.2 %collective-permute-start.28 = (bf16[256,1024]{1,0:T(8,128)(2,1)S(1)}, bf16[256,1024]{1,0:T(8,128)(2,1)S(1)}, u32[]{:S(2)}, u32[]{:S(2)}) collective-permute-start(bf16[256,1024]{1,0:T(8,128)(2,1)S(1)} %fusion.4), channel_id=1, source_target_pairs={{0,2},{2,4},{4,6},{3,1},{5,3},{7,5},{6,7},{1,0},{8,10},{10,12},{12... | collective-permute-start | bytes 1572872 | tf_op jit(solution)/shard_map/ppermute | solution.py:163
  119.9 2.0 %collective-permute-start.24 = (bf16[128,1024]{1,0:T(8,128)(2,1)S(1)}, bf16[128,1024]{1,0:T(8,128)(2,1)S(1)}, u32[]{:S(2)}, u32[]{:S(2)}) collective-permute-start(bf16[128,1024]{1,0:T(8,128)(2,1)S(1)} %add_convert_fusion.16), channel_id=1, source_target_pairs={{0,2},{2,4},{4,6},{3,1},{5,3},{7,5},{6,7},{1,0},{8,10},{10,12},{12... | collective-permute-start | bytes 786440 | tf_op jit(solution)/shard_map/ppermute | solution.py:163
  122.0 9.3 %collective-permute-done.28.first = bf16[256,1024]{1,0:T(8,128)(2,1)S(1)} collective-permute-done((bf16[256,1024]{1,0:T(8,128)(2,1)S(1)}, bf16[256,1024]{1,0:T(8,128)(2,1)S(1)}, u32[]{:S(2)}, u32[]{:S(2)}) %collective-permute-start.28) | collective-permute-done | bytes 524320 | tf_op jit(solution)/shard_map/ppermute | solution.py:163
  131.3 2.5 %collective-permute-start.26 = (bf16[128,1024]{1,0:T(8,128)(2,1)S(1)}, bf16[128,1024]{1,0:T(8,128)(2,1)S(1)}, u32[]{:S(2)}, u32[]{:S(2)}) collective-permute-start(bf16[128,1024]{1,0:T(8,128)(2,1)S(1)} %add_convert_fusion.18), channel_id=1, source_target_pairs={{0,2},{2,4},{4,6},{3,1},{5,3},{7,5},{6,7},{1,0},{8,10},{10,12},{12... | collective-permute-start | bytes 786440 | tf_op jit(solution)/shard_map/ppermute | solution.py:163
  134.3 2.8 %shard_map.119 = (f32[512,1024]{1,0:T(8,128)}, f32[512,1024]{1,0:T(8,128)}, f32[512,1024]{1,0:T(8,128)}, f32[8,512]{1,0:T(8,128)}) custom-call(f32[1,1024]{1,0:T(1,128)S(1)} %bitcast.104, bf16[128,128]{1,0:T(8,128)(2,1)S(1)} %fusion.86.table, f32[1,2]{1,0:T(1,128)S(1)} %maximum_bitcast_fusion.kept, f32[512,1024]{1,0:T(8,128)S(1)} %convolution_add_fusion.own, ...), custom_call_target="tpu_custom_call" | custom-call | tf_op jit(solution)/shard_map/pallas_call | solution.py:64
  137.1 4.5 %collective-permute-done.26.first = bf16[128,1024]{1,0:T(8,128)(2,1)S(1)} collective-permute-done((bf16[128,1024]{1,0:T(8,128)(2,1)S(1)}, bf16[128,1024]{1,0:T(8,128)(2,1)S(1)}, u32[]{:S(2)}, u32[]{:S(2)}) %collective-permute-start.26) | collective-permute-done | bytes 262176 | tf_op jit(solution)/shard_map/ppermute | solution.py:163
  141.6 0.7 collective-permute-done.27.second
  142.3 1.8 %shard_map.120 = (f32[512,1024]{1,0:T(8,128)}, f32[512,1024]{1,0:T(8,128)}, f32[512,1024]{1,0:T(8,128)}, f32[8,512]{1,0:T(8,128)}) custom-call(f32[1,1024]{1,0:T(1,128)S(1)} %bitcast.105, bf16[128,128]{1,0:T(8,128)(2,1)S(1)} %fusion.86.table, ...), custom_call_target="tpu_custom_call", output_to_operand_aliasing={{0}: (9, {}), {1}: (10, {}), {2}: (11, {}), {3}: (12, {})} | custom-call | tf_op jit(solution)/shard_map/pallas_call | solution.py:64
  144.2 1.8 %shard_map.121 = (f32[512,1024]{1,0:T(8,128)}, f32[512,1024]{1,0:T(8,128)}, f32[512,1024]{1,0:T(8,128)}, f32[8,512]{1,0:T(8,128)}) custom-call(f32[1,1024]{1,0:T(1,128)S(1)} %bitcast.106, bf16[128,128]{1,0:T(8,128)(2,1)S(1)} %fusion.86.table, ...), custom_call_target="tpu_custom_call", output_to_operand_aliasing={{0}: (9, {}), {1}: (10, {}), {2}: (11, {}), {3}: (12, {})} | custom-call | tf_op jit(solution)/shard_map/pallas_call | solution.py:64
  146.0 1.8 %add_add_fusion = f32[512,1024]{1,0:T(8,128)} fusion(f32[512,1024]{1,0:T(8,128)S(1)} %convolution_add_fusion.1, f32[512,1024]{1,0:T(8,128)S(1)} %collective-permute-done.23, bf16[256,1024]{1,0:T(8,128)(2,1)S(1)} %get-tuple-element.137, bf16[512,512]{1,0:T(8,128)(2,1)S(1)} %get-tuple-element.147), kind=kOutput, calls=%fused_computation | convolution fusion | flops 269484032 | bytes 7077888 | tf_op jit(solution)/shard_map/dot_general | solution.py:231
  (85 shorter events, 14.9 us)
Async XLA Ops:
  1.9 9.9 %collective-permute-start = (bf16[512,256]{1,0:T(8,128)(2,1)S(1)}, bf16[512,256]{1,0:T(8,128)(2,1)S(1)}, u32[]{:S(2)}, u32[]{:S(2)}) collective-permute-start(bf16[512,256]{1,0:T(8,128)(2,1)S(1)} %get-tuple-element.72), channel_id=1, source_target_pairs={{0,1},{1,0},{2,3},{3,2},{4,5},{5,4},{6,7},{7,6},{8,9},{9,8},{10,11... | collective-permute-start | bytes 786440 | tf_op jit(solution)/shard_map/ppermute | solution.py:160
  2.5 38.0 %collective-permute-start.12 = (bf16[512,1024]{1,0:T(8,128)(2,1)}, bf16[512,1024]{1,0:T(8,128)(2,1)}, u32[]{:S(2)}, u32[]{:S(2)}) collective-permute-start(bf16[512,1024]{1,0:T(8,128)(2,1)} %param.11), channel_id=1, source_target_pairs={{0,2},{2,4},{4,6},{3,1},{5,3},{7,5},{6,7},{1,0},{8,10},{10,12},{12... | collective-permute-start | bytes 3145736 | tf_op jit(solution)/shard_map/ppermute | solution.py:163
  5.1 6.4 %collective-permute-start.1 = (bf16[512,256]{1,0:T(8,128)(2,1)S(1)}, bf16[512,256]{1,0:T(8,128)(2,1)S(1)}, u32[]{:S(2)}, u32[]{:S(2)}) collective-permute-start(bf16[512,256]{1,0:T(8,128)(2,1)S(1)} %get-tuple-element.71), channel_id=1, source_target_pairs={{0,8},{1,17},{2,10},{3,19},{4,12},{5,21},{6,14},{7,23},{8,0},{9,25... | collective-permute-start | bytes 786440 | tf_op jit(solution)/shard_map/ppermute | solution.py:102
  6.6 6.6 %collective-permute-start.5 = (bf16[512,256]{1,0:T(8,128)(2,1)S(1)}, bf16[512,256]{1,0:T(8,128)(2,1)S(1)}, u32[]{:S(2)}, u32[]{:S(2)}) collective-permute-start(bf16[512,256]{1,0:T(8,128)(2,1)S(1)} %get-tuple-element.74), channel_id=1, source_target_pairs={{0,1},{1,0},{2,3},{3,2},{4,5},{5,4},{6,7},{7,6},{8,9},{9,8},{10,11... | collective-permute-start | bytes 786440 | tf_op jit(solution)/shard_map/ppermute | solution.py:160
  6.6 7.7 %collective-permute-start.6 = (bf16[512,256]{1,0:T(8,128)(2,1)S(1)}, bf16[512,256]{1,0:T(8,128)(2,1)S(1)}, u32[]{:S(2)}, u32[]{:S(2)}) collective-permute-start(bf16[512,256]{1,0:T(8,128)(2,1)S(1)} %get-tuple-element.73), channel_id=1, source_target_pairs={{0,8},{1,17},{2,10},{3,19},{4,12},{5,21},{6,14},{7,23},{8,0},{9,25... | collective-permute-start | bytes 786440 | tf_op jit(solution)/shard_map/ppermute | solution.py:102
  7.1 3.0 %copy-start.4 = (s32[1024]{0:T(1024)S(1)}, s32[1024]{0:T(1024)}, u32[]{:S(2)}) copy-start(s32[1024]{0:T(1024)} %param.12) | copy-start | bytes 12292
  7.1 4.7 %copy-start.3 = (bf16[512,1024]{1,0:T(8,128)(2,1)S(1)}, bf16[512,1024]{1,0:T(8,128)(2,1)}, u32[]{:S(2)}) copy-start(bf16[512,1024]{1,0:T(8,128)(2,1)} %param.9) | copy-start | bytes 3145732
  11.5 31.1 %collective-permute-start.14 = (bf16[512,1024]{1,0:T(8,128)(2,1)}, bf16[512,1024]{1,0:T(8,128)(2,1)S(1)}, u32[]{:S(2)}, u32[]{:S(2)}) collective-permute-start(bf16[512,1024]{1,0:T(8,128)(2,1)} %param.11), channel_id=1, source_target_pairs={{1,3},{3,5},{5,7},{2,0},{4,2},{6,4},{7,6},{0,1},{9,11},{11,13},{13... | collective-permute-start | bytes 3145736 | tf_op jit(solution)/shard_map/ppermute | solution.py:163
  11.8 28.2 %collective-permute-start.13 = (bf16[512,1024]{1,0:T(8,128)(2,1)S(1)}, bf16[512,1024]{1,0:T(8,128)(2,1)S(1)}, u32[]{:S(2)}, u32[]{:S(2)}) collective-permute-start(bf16[512,1024]{1,0:T(8,128)(2,1)S(1)} %copy-done.3), channel_id=1, source_target_pairs={{0,1},{1,0},{2,3},{3,2},{4,5},{5,4},{6,7},{7,6},{8,9},{9,8},{10,11... | collective-permute-start | bytes 3145736 | tf_op jit(solution)/shard_map/ppermute | solution.py:160
  13.2 6.4 %collective-permute-start.2 = (bf16[512,256]{1,0:T(8,128)(2,1)S(1)}, bf16[512,256]{1,0:T(8,128)(2,1)S(1)}, u32[]{:S(2)}, u32[]{:S(2)}) collective-permute-start(bf16[512,256]{1,0:T(8,128)(2,1)S(1)} %collective-permute-done), channel_id=1, source_target_pairs={{0,16},{1,9},{2,18},{3,11},{4,20},{5,13},{6,22},{7,15},{8,24},{9,1... | collective-permute-start | bytes 786440 | tf_op jit(solution)/shard_map/ppermute | solution.py:102
  14.3 8.1 %collective-permute-start.7 = (bf16[512,256]{1,0:T(8,128)(2,1)S(1)}, bf16[512,256]{1,0:T(8,128)(2,1)S(1)}, u32[]{:S(2)}, u32[]{:S(2)}) collective-permute-start(bf16[512,256]{1,0:T(8,128)(2,1)S(1)} %collective-permute-done.5), channel_id=1, source_target_pairs={{0,16},{1,9},{2,18},{3,11},{4,20},{5,13},{6,22},{7,15},{8,24},{9,1... | collective-permute-start | bytes 786440 | tf_op jit(solution)/shard_map/ppermute | solution.py:102
  19.6 10.4 %collective-permute-start.4 = (bf16[512,256]{1,0:T(8,128)(2,1)S(1)}, bf16[512,256]{1,0:T(8,128)(2,1)S(1)}, u32[]{:S(2)}, u32[]{:S(2)}) collective-permute-start(bf16[512,256]{1,0:T(8,128)(2,1)S(1)} %broadcast_select_fusion.2), channel_id=1, source_target_pairs={{0,16},{1,9},{2,18},{3,11},{4,20},{5,13},{6,22},{7,15},{8,24},{9,1... | collective-permute-start | bytes 786440 | tf_op jit(solution)/shard_map/ppermute | solution.py:102
  22.4 6.4 %collective-permute-start.3 = (bf16[512,256]{1,0:T(8,128)(2,1)S(1)}, bf16[512,256]{1,0:T(8,128)(2,1)S(1)}, u32[]{:S(2)}, u32[]{:S(2)}) collective-permute-start(bf16[512,256]{1,0:T(8,128)(2,1)S(1)} %broadcast_select_fusion.3), channel_id=1, source_target_pairs={{0,8},{1,17},{2,10},{3,19},{4,12},{5,21},{6,14},{7,23},{8,0},{9,25... | collective-permute-start | bytes 786440 | tf_op jit(solution)/shard_map/ppermute | solution.py:102
  28.7 9.9 %collective-permute-start.9 = (bf16[512,256]{1,0:T(8,128)(2,1)S(1)}, bf16[512,256]{1,0:T(8,128)(2,1)S(1)}, u32[]{:S(2)}, u32[]{:S(2)}) collective-permute-start(bf16[512,256]{1,0:T(8,128)(2,1)S(1)} %broadcast_select_fusion), channel_id=1, source_target_pairs={{0,16},{1,9},{2,18},{3,11},{4,20},{5,13},{6,22},{7,15},{8,24},{9,1... | collective-permute-start | bytes 786440 | tf_op jit(solution)/shard_map/ppermute | solution.py:102
  30.0 7.1 %collective-permute-start.8 = (bf16[512,256]{1,0:T(8,128)(2,1)S(1)}, bf16[512,256]{1,0:T(8,128)(2,1)S(1)}, u32[]{:S(2)}, u32[]{:S(2)}) collective-permute-start(bf16[512,256]{1,0:T(8,128)(2,1)S(1)} %broadcast_select_fusion.1), channel_id=1, source_target_pairs={{0,8},{1,17},{2,10},{3,19},{4,12},{5,21},{6,14},{7,23},{8,0},{9,25... | collective-permute-start | bytes 786440 | tf_op jit(solution)/shard_map/ppermute | solution.py:102
  37.1 15.5 %collective-permute-start.11 = (bf16[512,512]{1,0:T(8,128)(2,1)S(1)}, bf16[512,512]{1,0:T(8,128)(2,1)S(1)}, u32[]{:S(2)}, u32[]{:S(2)}) collective-permute-start(bf16[512,512]{1,0:T(8,128)(2,1)S(1)} %maximum_select_fusion.1), channel_id=1, source_target_pairs={{0,16},{1,9},{2,18},{3,11},{4,20},{5,13},{6,22},{7,15},{8,24},{9,1... | collective-permute-start | bytes 1572872 | tf_op jit(solution)/shard_map/ppermute | solution.py:102
  38.6 13.1 %collective-permute-start.10 = (bf16[512,512]{1,0:T(8,128)(2,1)S(1)}, bf16[512,512]{1,0:T(8,128)(2,1)S(1)}, u32[]{:S(2)}, u32[]{:S(2)}) collective-permute-start(bf16[512,512]{1,0:T(8,128)(2,1)S(1)} %maximum_select_fusion), channel_id=1, source_target_pairs={{0,8},{1,17},{2,10},{3,19},{4,12},{5,21},{6,14},{7,23},{8,0},{9,25... | collective-permute-start | bytes 1572872 | tf_op jit(solution)/shard_map/ppermute | solution.py:102
  42.6 3.8 %slice-start = ((s8[8388608]{0:T(1024)(128)(4,1)}), s8[4194304]{0:T(1024)(128)(4,1)S(1)}, s32[]{:S(2)}) async-start(s8[8388608]{0:T(1024)(128)(4,1)} %bitcast.107), calls=%async_computation | async-start | bytes 8388608
  43.6 2.8 %slice-start.1 = ((s8[8388608]{0:T(1024)(128)(4,1)}), s8[4194304]{0:T(1024)(128)(4,1)S(1)}, s32[]{:S(2)}) async-start(s8[8388608]{0:T(1024)(128)(4,1)} %bitcast.107), calls=%async_computation.1 | async-start | bytes 8388608
  55.2 25.4 %collective-permute-start.17 = (bf16[256,1024]{1,0:T(8,128)(2,1)S(1)}, bf16[256,1024]{1,0:T(8,128)(2,1)S(1)}, u32[]{:S(2)}, u32[]{:S(2)}) collective-permute-start(bf16[256,1024]{1,0:T(8,128)(2,1)S(1)} %add_convert_fusion.12), channel_id=1, source_target_pairs={{0,2},{2,4},{4,6},{3,1},{5,3},{7,5},{6,7},{1,0},{8,10},{10,12},{12... | collective-permute-start | bytes 1572872 | tf_op jit(solution)/shard_map/ppermute | solution.py:163
  56.8 24.0 %collective-permute-start.18 = (bf16[256,1024]{1,0:T(8,128)(2,1)S(1)}, bf16[256,1024]{1,0:T(8,128)(2,1)S(1)}, u32[]{:S(2)}, u32[]{:S(2)}) collective-permute-start(bf16[256,1024]{1,0:T(8,128)(2,1)S(1)} %add_convert_fusion.11), channel_id=1, source_target_pairs={{1,3},{3,5},{5,7},{2,0},{4,2},{6,4},{7,6},{0,1},{9,11},{11,13},{13... | collective-permute-start | bytes 1572872 | tf_op jit(solution)/shard_map/ppermute | solution.py:163
  60.5 19.2 %collective-permute-start.15 = (bf16[256,1024]{1,0:T(8,128)(2,1)S(1)}, bf16[256,1024]{1,0:T(8,128)(2,1)S(1)}, u32[]{:S(2)}, u32[]{:S(2)}) collective-permute-start(bf16[256,1024]{1,0:T(8,128)(2,1)S(1)} %add_convert_fusion.14), channel_id=1, source_target_pairs={{0,2},{2,4},{4,6},{3,1},{5,3},{7,5},{6,7},{1,0},{8,10},{10,12},{12... | collective-permute-start | bytes 1572872 | tf_op jit(solution)/shard_map/ppermute | solution.py:163
  66.1 14.3 %collective-permute-start.16 = (bf16[256,1024]{1,0:T(8,128)(2,1)S(1)}, bf16[256,1024]{1,0:T(8,128)(2,1)S(1)}, u32[]{:S(2)}, u32[]{:S(2)}) collective-permute-start(bf16[256,1024]{1,0:T(8,128)(2,1)S(1)} %add_convert_fusion.13), channel_id=1, source_target_pairs={{1,3},{3,5},{5,7},{2,0},{4,2},{6,4},{7,6},{0,1},{9,11},{11,13},{13... | collective-permute-start | bytes 1572872 | tf_op jit(solution)/shard_map/ppermute | solution.py:163
  81.6 20.8 %collective-permute-start.21 = (bf16[256,1024]{1,0:T(8,128)(2,1)S(1)}, bf16[256,1024]{1,0:T(8,128)(2,1)S(1)}, u32[]{:S(2)}, u32[]{:S(2)}) collective-permute-start(bf16[256,1024]{1,0:T(8,128)(2,1)S(1)} %add_convert_fusion.9), channel_id=1, source_target_pairs={{0,2},{2,4},{4,6},{3,1},{5,3},{7,5},{6,7},{1,0},{8,10},{10,12},{12... | collective-permute-start | bytes 1572872 | tf_op jit(solution)/shard_map/ppermute | solution.py:163
  85.2 16.8 %collective-permute-start.19 = (bf16[256,1024]{1,0:T(8,128)(2,1)S(1)}, bf16[256,1024]{1,0:T(8,128)(2,1)S(1)}, u32[]{:S(2)}, u32[]{:S(2)}) collective-permute-start(bf16[256,1024]{1,0:T(8,128)(2,1)S(1)} %fusion.5), channel_id=1, source_target_pairs={{0,2},{2,4},{4,6},{3,1},{5,3},{7,5},{6,7},{1,0},{8,10},{10,12},{12... | collective-permute-start | bytes 1572872 | tf_op jit(solution)/shard_map/ppermute | solution.py:163
  89.3 12.9 %collective-permute-start.20 = (bf16[256,1024]{1,0:T(8,128)(2,1)S(1)}, bf16[256,1024]{1,0:T(8,128)(2,1)S(1)}, u32[]{:S(2)}, u32[]{:S(2)}) collective-permute-start(bf16[256,1024]{1,0:T(8,128)(2,1)S(1)} %add_convert_fusion.10), channel_id=1, source_target_pairs={{1,3},{3,5},{5,7},{2,0},{4,2},{6,4},{7,6},{0,1},{9,11},{11,13},{13... | collective-permute-start | bytes 1572872 | tf_op jit(solution)/shard_map/ppermute | solution.py:163
  89.3 16.8 %collective-permute-start.22 = (bf16[256,1024]{1,0:T(8,128)(2,1)S(1)}, bf16[256,1024]{1,0:T(8,128)(2,1)S(1)}, u32[]{:S(2)}, u32[]{:S(2)}) collective-permute-start(bf16[256,1024]{1,0:T(8,128)(2,1)S(1)} %add_convert_fusion.8), channel_id=1, source_target_pairs={{1,3},{3,5},{5,7},{2,0},{4,2},{6,4},{7,6},{0,1},{9,11},{11,13},{13... | collective-permute-start | bytes 1572872 | tf_op jit(solution)/shard_map/ppermute | solution.py:163
  113.0 33.1 %collective-permute-start.23 = (f32[512,1024]{1,0:T(8,128)S(1)}, f32[512,1024]{1,0:T(8,128)S(1)}, u32[]{:S(2)}, u32[]{:S(2)}) collective-permute-start(f32[512,1024]{1,0:T(8,128)S(1)} %add_add_fusion.1), channel_id=1, source_target_pairs={{0,1},{1,0},{2,3},{3,2},{4,5},{5,4},{6,7},{7,6},{8,9},{9,8},{10,11... | collective-permute-start | bytes 6291464 | tf_op jit(solution)/shard_map/ppermute | solution.py:160
  116.8 14.5 %collective-permute-start.28 = (bf16[256,1024]{1,0:T(8,128)(2,1)S(1)}, bf16[256,1024]{1,0:T(8,128)(2,1)S(1)}, u32[]{:S(2)}, u32[]{:S(2)}) collective-permute-start(bf16[256,1024]{1,0:T(8,128)(2,1)S(1)} %fusion.4), channel_id=1, source_target_pairs={{0,2},{2,4},{4,6},{3,1},{5,3},{7,5},{6,7},{1,0},{8,10},{10,12},{12... | collective-permute-start | bytes 1572872 | tf_op jit(solution)/shard_map/ppermute | solution.py:163
  119.0 14.8 %collective-permute-start.29 = (bf16[256,1024]{1,0:T(8,128)(2,1)S(1)}, bf16[256,1024]{1,0:T(8,128)(2,1)S(1)}, u32[]{:S(2)}, u32[]{:S(2)}) collective-permute-start(bf16[256,1024]{1,0:T(8,128)(2,1)S(1)} %add_convert_fusion.5), channel_id=1, source_target_pairs={{1,3},{3,5},{5,7},{2,0},{4,2},{6,4},{7,6},{0,1},{9,11},{11,13},{13... | collective-permute-start | bytes 1572872 | tf_op jit(solution)/shard_map/ppermute | solution.py:163
  119.4 14.8 %copy-start.2 = (f32[512,1024]{1,0:T(8,128)S(1)}, f32[512,1024]{1,0:T(8,128)}, u32[]{:S(2)}) copy-start(f32[512,1024]{1,0:T(8,128)} %variance.5) | copy-start | bytes 6291460
  119.9 14.4 %copy-start = (f32[512,1024]{1,0:T(8,128)S(1)}, f32[512,1024]{1,0:T(8,128)}, u32[]{:S(2)}) copy-start(f32[512,1024]{1,0:T(8,128)} %master.5) | copy-start | bytes 6291460
  119.9 14.3 %copy-start.1 = (f32[512,1024]{1,0:T(8,128)S(1)}, f32[512,1024]{1,0:T(8,128)}, u32[]{:S(2)}) copy-start(f32[512,1024]{1,0:T(8,128)} %moment.5) | copy-start | bytes 6291460
  119.9 24.3 %collective-permute-start.24 = (bf16[128,1024]{1,0:T(8,128)(2,1)S(1)}, bf16[128,1024]{1,0:T(8,128)(2,1)S(1)}, u32[]{:S(2)}, u32[]{:S(2)}) collective-permute-start(bf16[128,1024]{1,0:T(8,128)(2,1)S(1)} %add_convert_fusion.16), channel_id=1, source_target_pairs={{0,2},{2,4},{4,6},{3,1},{5,3},{7,5},{6,7},{1,0},{8,10},{10,12},{12... | collective-permute-start | bytes 786440 | tf_op jit(solution)/shard_map/ppermute | solution.py:163
  122.0 22.2 %collective-permute-start.25 = (bf16[128,1024]{1,0:T(8,128)(2,1)S(1)}, bf16[128,1024]{1,0:T(8,128)(2,1)S(1)}, u32[]{:S(2)}, u32[]{:S(2)}) collective-permute-start(bf16[128,1024]{1,0:T(8,128)(2,1)S(1)} %add_convert_fusion.15), channel_id=1, source_target_pairs={{1,3},{3,5},{5,7},{2,0},{4,2},{6,4},{7,6},{0,1},{9,11},{11,13},{13... | collective-permute-start | bytes 786440 | tf_op jit(solution)/shard_map/ppermute | solution.py:163
  131.3 10.3 %collective-permute-start.26 = (bf16[128,1024]{1,0:T(8,128)(2,1)S(1)}, bf16[128,1024]{1,0:T(8,128)(2,1)S(1)}, u32[]{:S(2)}, u32[]{:S(2)}) collective-permute-start(bf16[128,1024]{1,0:T(8,128)(2,1)S(1)} %add_convert_fusion.18), channel_id=1, source_target_pairs={{0,2},{2,4},{4,6},{3,1},{5,3},{7,5},{6,7},{1,0},{8,10},{10,12},{12... | collective-permute-start | bytes 786440 | tf_op jit(solution)/shard_map/ppermute | solution.py:163
  133.8 8.5 %collective-permute-start.27 = (bf16[128,1024]{1,0:T(8,128)(2,1)S(1)}, bf16[128,1024]{1,0:T(8,128)(2,1)S(1)}, u32[]{:S(2)}, u32[]{:S(2)}) collective-permute-start(bf16[128,1024]{1,0:T(8,128)(2,1)S(1)} %add_convert_fusion.17), channel_id=1, source_target_pairs={{1,3},{3,5},{5,7},{2,0},{4,2},{6,4},{7,6},{0,1},{9,11},{11,13},{13... | collective-permute-start | bytes 786440 | tf_op jit(solution)/shard_map/ppermute | solution.py:163

commit v3 on v2

--- a/solution.py
+++ b/solution.py
@@ -226,17 +226,12 @@
                 cached = lax.dynamic_slice(cache, (first, 0), (height, width))
                 weight = cached.astype(jnp.float32) + delta.astype(jnp.float32)
                 weights.append(lax.optimization_barrier(weight.astype(jnp.bfloat16)))
-            return [
-                [
-                    jnp.dot(
-                        tokens_for(chip_index, which)[:, part * height :][:, :height],
-                        weight,
-                        preferred_element_type=jnp.float32,
-                    )
-                    for part, weight in enumerate(weights)
-                ]
-                for which in (0, 1)
-            ]
+            found = [[], []]
+            for which in (0, 1):
+                for part, weight in enumerate(weights):
+                    given = tokens_for(chip_index, which)[:, part * height :][:, :height]
+                    found[which].append(jnp.dot(given, weight, preferred_element_type=jnp.float32))
+            return found
 
         def pieces_of(turn):
             found = [(k, 0, size) for k in range(parts)]
@@ -292,6 +287,11 @@
 
         mine, other = products(chip, [weight_delta], caches[1])
         mine, other = mine[0], other[0]
+        for line in (0, 1):
+            history[line][0] = [
+                lax.optimization_barrier(jnp.where(places[line] == 0, jnp.bfloat16(0), value))
+                for value in history[line][0]
+            ]
         order = sorted(range(1, chips), key=lambda t: max(t, chips - t))
         later = []
         for number, turn in enumerate(order, 1):

time: 148 us -> 147 us (level)
  starting transfers between devices: 26.9 us -> 31.7 us
  waiting for transfers between devices: 59.2 us -> 54.5 us
  other arithmetic: 6.87 us -> 4.71 us
    ppermute x10, starting transfers between devices: 8.07 us -> 12.1 us  [across(): return lax.ppermute(value, ('outer', 'inner'), pairs)]
    ppermute x10, waiting for transfers between devices: 16.9 us -> 13.1 us  [across(): return lax.ppermute(value, ('outer', 'inner'), pairs)]
    convert_element_type x3, other arithmetic: 4.98 us -> 2.65 us  [products(): weights.append(lax.optimization_barrier(weight.astype(jnp.bfloat16)))]
  transfers between devices with their start and end apart: 30 -> 30, of which waited for: 14 -> 13; matrix products, arithmetic and copies ran while one was open for 27% -> 28% of each run, Pallas kernels for 4% -> 4%
where the time goes in v3:
time: 147 us
  waiting for transfers between devices  54.5 us (37%)
  starting transfers between devices  31.7 us (22%)
  matrix products  30.7 us (21%)
  local copies, waits for them, and re-layouts  17.1 us (12%)
  Pallas kernels  6.5 us (4%)
  other arithmetic  4.71 us (3%)
    ppermute x16, waiting for transfers between devices, along(): return lax.ppermute(value, 'inner', line_pairs[line])  41.4 us
    dot_general x18, matrix products, contract(): lax.dot_general(left, right, (((0,), (0,)), ((), ())), preferred_element_...  20.2 us
    ppermute x16, starting transfers between devices, along(): return lax.ppermute(value, 'inner', line_pairs[line])  16.8 us
    ppermute x10, waiting for transfers between devices, across(): return lax.ppermute(value, ('outer', 'inner'), pairs)  13.1 us
    ppermute x10, starting transfers between devices, across(): return lax.ppermute(value, ('outer', 'inner'), pairs)  12.1 us
    dynamic_update_slice x14, local copies, waits for them, and re-layouts, body(): lax.dynamic_update_slice(held, piece, (owner, which * count, 0, part * si...  10.5 us
    dot_general x14, matrix products, products(): jnp.dot(given, weight, preferred_element_type=jnp.float32)  10.5 us
    pallas_call x3, Pallas kernels, finish(): pl.pallas_call(functools.partial(finish_kernel, start), grid=(size // til...  6.5 us
  transfers between devices with their start and end apart: 30, of which 13 were waited for; matrix products, arithmetic and copies ran while one was open for 28% of the time, Pallas kernels for 4%

profile of v3, /device:TPU:0, one launch (start us, length us, event | category | flops | bytes accessed | tf_op | source)
XLA Modules:
  0.0 146.6 jit_solution(11378258318121092285)
XLA Ops:
  0.6 3.1 %collective-permute-start.12 = (bf16[512,1024]{1,0:T(8,128)(2,1)}, bf16[512,1024]{1,0:T(8,128)(2,1)}, u32[]{:S(2)}, u32[]{:S(2)}) collective-permute-start(bf16[512,1024]{1,0:T(8,128)(2,1)} %param.11), channel_id=1, source_target_pairs={{0,2},{2,4},{4,6},{3,1},{5,3},{7,5},{6,7},{1,0},{8,10},{10,12},{12... | collective-permute-start | bytes 3145736 | tf_op jit(solution)/shard_map/ppermute | solution.py:163
  3.7 1.3 constant_dynamic-slice_fusion
  5.0 1.6 %collective-permute-start.1 = (bf16[512,256]{1,0:T(8,128)(2,1)S(1)}, bf16[512,256]{1,0:T(8,128)(2,1)S(1)}, u32[]{:S(2)}, u32[]{:S(2)}) collective-permute-start(bf16[512,256]{1,0:T(8,128)(2,1)S(1)} %get-tuple-element.71), channel_id=1, source_target_pairs={{0,8},{1,17},{2,10},{3,19},{4,12},{5,21},{6,14},{7,23},{8,0},{9,25... | collective-permute-start | bytes 786440 | tf_op jit(solution)/shard_map/ppermute | solution.py:102
  6.8 1.5 %collective-permute-start.6 = (bf16[512,256]{1,0:T(8,128)(2,1)S(1)}, bf16[512,256]{1,0:T(8,128)(2,1)S(1)}, u32[]{:S(2)}, u32[]{:S(2)}) collective-permute-start(bf16[512,256]{1,0:T(8,128)(2,1)S(1)} %get-tuple-element.73), channel_id=1, source_target_pairs={{0,8},{1,17},{2,10},{3,19},{4,12},{5,21},{6,14},{7,23},{8,0},{9,25... | collective-permute-start | bytes 786440 | tf_op jit(solution)/shard_map/ppermute | solution.py:102
  8.3 2.3 %reshape.100 = bf16[4,1024,512]{2,1,0:T(8,128)(2,1)} broadcast(bf16[]{:T(256)} %constant.187.clone.1), dimensions={} | broadcast | bytes 4194306 | tf_op jit(solution)/shard_map/reshape | solution.py:209
  10.6 0.7 bitcast_dynamic-update-slice_fusion.13
  11.8 1.4 collective-permute-start.13
  13.2 0.9 collective-permute-start.2
  14.3 1.5 %collective-permute-start.7 = (bf16[512,256]{1,0:T(8,128)(2,1)S(1)}, bf16[512,256]{1,0:T(8,128)(2,1)S(1)}, u32[]{:S(2)}, u32[]{:S(2)}) collective-permute-start(bf16[512,256]{1,0:T(8,128)(2,1)S(1)} %collective-permute-done.5), channel_id=1, source_target_pairs={{0,16},{1,9},{2,18},{3,11},{4,20},{5,13},{6,22},{7,15},{8,24},{9,1... | collective-permute-start | bytes 786440 | tf_op jit(solution)/shard_map/ppermute | solution.py:102
  16.6 0.7 bitcast_dynamic-update-slice_fusion.11
  17.4 2.1 %collective-permute-done.2 = bf16[512,256]{1,0:T(8,128)(2,1)S(1)} collective-permute-done((bf16[512,256]{1,0:T(8,128)(2,1)S(1)}, bf16[512,256]{1,0:T(8,128)(2,1)S(1)}, u32[]{:S(2)}, u32[]{:S(2)}) %collective-permute-start.2) | collective-permute-done | bytes 262176 | tf_op jit(solution)/shard_map/ppermute | solution.py:102
  19.6 0.9 collective-permute-start.4
  20.5 1.9 %collective-permute-done.7 = bf16[512,256]{1,0:T(8,128)(2,1)S(1)} collective-permute-done((bf16[512,256]{1,0:T(8,128)(2,1)S(1)}, bf16[512,256]{1,0:T(8,128)(2,1)S(1)}, u32[]{:S(2)}, u32[]{:S(2)}) %collective-permute-start.7) | collective-permute-done | bytes 262176 | tf_op jit(solution)/shard_map/ppermute | solution.py:102
  22.4 0.9 collective-permute-start.3
  23.3 0.7 bitcast_dynamic-update-slice_fusion.10
  24.2 4.6 %collective-permute-done.3 = bf16[512,256]{1,0:T(8,128)(2,1)S(1)} collective-permute-done((bf16[512,256]{1,0:T(8,128)(2,1)S(1)}, bf16[512,256]{1,0:T(8,128)(2,1)S(1)}, u32[]{:S(2)}, u32[]{:S(2)}) %collective-permute-start.3) | collective-permute-done | bytes 262176 | tf_op jit(solution)/shard_map/ppermute | solution.py:102
  28.7 0.9 collective-permute-start.9
  30.4 1.5 %collective-permute-start.8 = (bf16[512,256]{1,0:T(8,128)(2,1)S(1)}, bf16[512,256]{1,0:T(8,128)(2,1)S(1)}, u32[]{:S(2)}, u32[]{:S(2)}) collective-permute-start(bf16[512,256]{1,0:T(8,128)(2,1)S(1)} %broadcast_select_fusion.3), channel_id=1, source_target_pairs={{0,8},{1,17},{2,10},{3,19},{4,12},{5,21},{6,14},{7,23},{8,0},{9,25... | collective-permute-start | bytes 786440 | tf_op jit(solution)/shard_map/ppermute | solution.py:102
  31.9 0.7 bitcast_dynamic-update-slice_fusion.8
  32.6 0.8 bitcast_dynamic-update-slice_fusion.7
  33.4 0.7 bitcast_dynamic-update-slice_fusion.6
  34.1 0.7 bitcast_dynamic-update-slice_fusion.5
  35.6 1.5 %collective-permute-done.8 = bf16[512,256]{1,0:T(8,128)(2,1)S(1)} collective-permute-done((bf16[512,256]{1,0:T(8,128)(2,1)S(1)}, bf16[512,256]{1,0:T(8,128)(2,1)S(1)}, u32[]{:S(2)}, u32[]{:S(2)}) %collective-permute-start.8) | collective-permute-done | bytes 262176 | tf_op jit(solution)/shard_map/ppermute | solution.py:102
  37.1 0.9 collective-permute-start.11
  38.0 0.7 bitcast_dynamic-update-slice_fusion.3
  38.7 1.5 %collective-permute-start.10 = (bf16[512,512]{1,0:T(8,128)(2,1)S(1)}, bf16[512,512]{1,0:T(8,128)(2,1)S(1)}, u32[]{:S(2)}, u32[]{:S(2)}) collective-permute-start(bf16[512,512]{1,0:T(8,128)(2,1)S(1)} %maximum_select_fusion), channel_id=1, source_target_pairs={{0,8},{1,17},{2,10},{3,19},{4,12},{5,21},{6,14},{7,23},{8,0},{9,25... | collective-permute-start | bytes 1572872 | tf_op jit(solution)/shard_map/ppermute | solution.py:102
  40.2 0.7 bitcast_dynamic-update-slice_fusion.2
  41.4 1.6 %add_convert_fusion.14 = bf16[256,1024]{1,0:T(8,128)(2,1)S(1)} fusion(bf16[512,1024]{1,0:T(8,128)(2,1)} %collective-permute-done.12, f32[256,1024]{1,0:T(8,128)S(1)} %fusion.62, bf16[512,1024]{1,0:T(8,128)(2,1)S(1)} %copy-done.3, pred[]{:T(512)S(6)} %ge.12, pred[]{:T(512)S(6)} %eq.32, bf16[512,256]{1,0:T(8,128)(2,1)S(1)} %get-tuple-element.71, ...), kind=kOutput, calls=%fused_computation.38 | convolution fusion | flops 270270464 | bytes 3932164 | tf_op jit(solution)/shard_map/dot_general | solution.py:141
  44.5 1.8 %add_convert_fusion.12 = bf16[256,1024]{1,0:T(8,128)(2,1)S(1)} fusion(bf16[512,1024]{1,0:T(8,128)(2,1)} %collective-permute-done.12, f32[256,1024]{1,0:T(8,128)S(1)} %fusion.52, bf16[512,1024]{1,0:T(8,128)(2,1)S(1)} %copy-done.3, pred[]{:T(512)S(6)} %ge.12, pred[]{:T(512)S(6)} %eq.32, bf16[512,256]{1,0:T(8,128)(2,1)S(1)} %get-tuple-element.73, ...), kind=kOutput, calls=%fused_computation.36 | convolution fusion | flops 270270464 | bytes 3932164 | tf_op jit(solution)/shard_map/dot_general | solution.py:141
  47.4 0.8 copy-done.4
  48.6 3.0 %collective-permute-done.10 = bf16[512,512]{1,0:T(8,128)(2,1)S(1)} collective-permute-done((bf16[512,512]{1,0:T(8,128)(2,1)S(1)}, bf16[512,512]{1,0:T(8,128)(2,1)S(1)}, u32[]{:S(2)}, u32[]{:S(2)}) %collective-permute-start.10) | collective-permute-done | bytes 524320 | tf_op jit(solution)/shard_map/ppermute | solution.py:102
  51.6 0.8 bitcast_dynamic-update-slice_fusion.1
  52.4 0.8 bitcast_dynamic-update-slice_fusion
  53.2 1.8 %fusion.16 = f32[512,1024]{1,0:T(8,128)S(1)} fusion(bf16[512,1024]{1,0:T(8,128)(2,1)S(1)} %add_convert_fusion, bf16[4,1024,512]{2,1,0:T(8,128)(2,1)} %bitcast_dynamic-update-slice_fusion, s32[]{:T(128)S(6)} %select_n.522), kind=kOutput, calls=%fused_computation.61 | convolution fusion | flops 536870912 | bytes 3670020 | tf_op jit(solution)/shard_map/dot_general | solution.py:233
  55.0 1.6 %collective-permute-start.17 = (bf16[256,1024]{1,0:T(8,128)(2,1)S(1)}, bf16[256,1024]{1,0:T(8,128)(2,1)S(1)}, u32[]{:S(2)}, u32[]{:S(2)}) collective-permute-start(bf16[256,1024]{1,0:T(8,128)(2,1)S(1)} %add_convert_fusion.12), channel_id=1, source_target_pairs={{0,2},{2,4},{4,6},{3,1},{5,3},{7,5},{6,7},{1,0},{8,10},{10,12},{12... | collective-permute-start | bytes 1572872 | tf_op jit(solution)/shard_map/ppermute | solution.py:163
  56.6 2.2 %dynamic-slice_bitcast_fusion = (bf16[512,512]{1,0:T(8,128)(2,1)S(1)}, bf16[512,512]{1,0:T(8,128)(2,1)S(1)}, bf16[512,512]{1,0:T(8,128)(2,1)S(1)}, bf16[512,512]...) fusion(bf16[4,1024,512]{2,1,0:T(8,128)(2,1)} %bitcast_dynamic-update-slice_fusion, ...), kind=kLoop, calls=%fused_computation.65 | loop fusion | bytes 6291468 | tf_op jit(solution)/shard_map/squeeze | solution.py:213
  58.8 0.7 fusion.99
  59.6 0.7 add_select_fusion.3
  60.3 2.0 %collective-permute-start.15 = (bf16[256,1024]{1,0:T(8,128)(2,1)S(1)}, bf16[256,1024]{1,0:T(8,128)(2,1)S(1)}, u32[]{:S(2)}, u32[]{:S(2)}) collective-permute-start(bf16[256,1024]{1,0:T(8,128)(2,1)S(1)} %add_convert_fusion.14), channel_id=1, source_target_pairs={{0,2},{2,4},{4,6},{3,1},{5,3},{7,5},{6,7},{1,0},{8,10},{10,12},{12... | collective-permute-start | bytes 1572872 | tf_op jit(solution)/shard_map/ppermute | solution.py:163
  62.3 1.8 %fusion.12 = f32[512,1024]{1,0:T(8,128)S(1)} fusion(bf16[512,1024]{1,0:T(8,128)(2,1)S(1)} %collective-permute-done.13, bf16[4,1024,512]{2,1,0:T(8,128)(2,1)} %bitcast_dynamic-update-slice_fusion, s32[]{:T(128)S(6)} %select_n.569), kind=kOutput, calls=%fused_computation.57 | convolution fusion | flops 536870912 | bytes 3670020 | tf_op jit(solution)/shard_map/dot_general | solution.py:141
  64.1 1.8 %add_select_fusion.2 = f32[512,1024]{1,0:T(8,128)S(1)} fusion(f32[512,1024]{1,0:T(8,128)S(1)} %fusion.12, bf16[512,1024]{1,0:T(8,128)(2,1)S(1)} %copy-done.3, pred[]{:T(512)S(6)} %ge.29, bf16[4,1024,512]{2,1,0:T(8,128)(2,1)} %bitcast_dynamic-update-slice_fusion, s32[]{:T(128)S(6)} %select_n.569), kind=kOutput, calls=%fused_computation.4 | convolution fusion | flops 537919488 | bytes 5767173 | tf_op jit(solution)/shard_map/dot_general | solution.py:141
  66.1 1.8 %fusion.6 = f32[512,1024]{1,0:T(8,128)S(1)} fusion(bf16[512,1024]{1,0:T(8,128)(2,1)S(1)} %collective-permute-done.13, bf16[4,1024,512]{2,1,0:T(8,128)(2,1)} %bitcast_dynamic-update-slice_fusion, s32[]{:T(128)S(6)} %select_n.522), kind=kOutput, calls=%fused_computation.51 | convolution fusion | flops 536870912 | bytes 3670020 | tf_op jit(solution)/shard_map/dot_general | solution.py:141
  67.9 11.5 %collective-permute-done.15 = bf16[256,1024]{1,0:T(8,128)(2,1)S(1)} collective-permute-done((bf16[256,1024]{1,0:T(8,128)(2,1)S(1)}, bf16[256,1024]{1,0:T(8,128)(2,1)S(1)}, u32[]{:S(2)}, u32[]{:S(2)}) %collective-permute-start.15) | collective-permute-done | bytes 524320 | tf_op jit(solution)/shard_map/ppermute | solution.py:163
  81.4 2.0 %collective-permute-start.21 = (bf16[256,1024]{1,0:T(8,128)(2,1)S(1)}, bf16[256,1024]{1,0:T(8,128)(2,1)S(1)}, u32[]{:S(2)}, u32[]{:S(2)}) collective-permute-start(bf16[256,1024]{1,0:T(8,128)(2,1)S(1)} %add_convert_fusion.9), channel_id=1, source_target_pairs={{0,2},{2,4},{4,6},{3,1},{5,3},{7,5},{6,7},{1,0},{8,10},{10,12},{12... | collective-permute-start | bytes 1572872 | tf_op jit(solution)/shard_map/ppermute | solution.py:163
  83.4 0.7 fusion.100
  84.1 0.9 add_select_fusion.1
  85.1 1.3 collective-permute-start.19
  86.3 1.8 %fusion.9 = f32[512,1024]{1,0:T(8,128)S(1)} fusion(bf16[512,1024]{1,0:T(8,128)(2,1)S(1)} %collective-permute-done.13, bf16[4,1024,512]{2,1,0:T(8,128)(2,1)} %bitcast_dynamic-update-slice_fusion, s32[]{:T(128)S(6)} %select_n.588), kind=kOutput, calls=%fused_computation.54 | convolution fusion | flops 536870912 | bytes 3670020 | tf_op jit(solution)/shard_map/dot_general | solution.py:141
  88.1 1.8 %add_select_fusion = f32[512,1024]{1,0:T(8,128)S(1)} fusion(f32[512,1024]{1,0:T(8,128)S(1)} %fusion.9, bf16[512,1024]{1,0:T(8,128)(2,1)S(1)} %copy-done.3, pred[]{:T(512)S(6)} %ge.31, bf16[4,1024,512]{2,1,0:T(8,128)(2,1)} %bitcast_dynamic-update-slice_fusion, s32[]{:T(128)S(6)} %select_n.588), kind=kOutput, calls=%fused_computation.2 | convolution fusion | flops 537919488 | bytes 5767173 | tf_op jit(solution)/shard_map/dot_general | solution.py:141
  90.9 10.9 %collective-permute-done.19 = bf16[256,1024]{1,0:T(8,128)(2,1)S(1)} collective-permute-done((bf16[256,1024]{1,0:T(8,128)(2,1)S(1)}, bf16[256,1024]{1,0:T(8,128)(2,1)S(1)}, u32[]{:S(2)}, u32[]{:S(2)}) %collective-permute-start.19) | collective-permute-done | bytes 524320 | tf_op jit(solution)/shard_map/ppermute | solution.py:163
  102.2 3.7 %collective-permute-done.22 = bf16[256,1024]{1,0:T(8,128)(2,1)S(1)} collective-permute-done((bf16[256,1024]{1,0:T(8,128)(2,1)S(1)}, bf16[256,1024]{1,0:T(8,128)(2,1)S(1)}, u32[]{:S(2)}, u32[]{:S(2)}) %collective-permute-start.22) | collective-permute-done | bytes 524320 | tf_op jit(solution)/shard_map/ppermute | solution.py:163
  106.2 1.6 %add_convert_fusion.1 = (bf16[256,1024]{1,0:T(8,128)(2,1)S(1)}, bf16[256,1024]{1,0:T(8,128)(2,1)S(1)}, bf16[256,1024]{1,0:T(8,128)(2,1)S(1)}, bf16[256,1024]{1,0:T(8,128)(2,1)S(1)}) fusion(bf16[256,1024]{1,0:T(8,128)(2,1)S(1)} %collective-permute-done.21, bf16[512,1024]{1,0:T(8,128)(2,1)S(1)} %broadcast_select_fusion, bf16[4096,1024]{1,0:T(8,128)(2,1)S(1)} %bitcast.108, ...), kind=kLoop, calls=%fused_computation.25 | loop fusion | flops 5242880 | bytes 8388626 | tf_op jit(solution)/shard_map/convert_element_type | solution.py:228
  109.6 2.1 %add_add_fusion.1 = f32[512,1024]{1,0:T(8,128)S(1)} fusion(f32[512,1024]{1,0:T(8,128)S(1)} %fusion.30, f32[512,1024]{1,0:T(8,128)S(1)} %fusion.32, f32[512,1024]{1,0:T(8,128)S(1)} %fusion.34, f32[512,1024]{1,0:T(8,128)S(1)} %fusion.36, f32[512,1024]{1,0:T(8,128)S(1)} %fusion.38, f32[512,1024]{1,0:T(8,128)S(1)} %fusion.40, ...), kind=kOutput, calls=%fused_computation.1 | convolution fusion | flops 540016640 | bytes 16252932 | tf_op jit(solution)/shard_map/dot_general | solution.py:233
  111.7 1.2 collective-permute-start.23
  112.9 1.8 %convolution_add_fusion.own = f32[512,1024]{1,0:T(8,128)S(1)} fusion(f32[512,1024]{1,0:T(8,128)S(1)} %fusion.6, bf16[512,1024]{1,0:T(8,128)(2,1)S(1)} %copy-done.3, bf16[4,1024,512]{2,1,0:T(8,128)(2,1)} %bitcast_dynamic-update-slice_fusion, s32[]{:T(128)S(6)} %select_n.522), kind=kOutput, calls=%fused_computation.7 | convolution fusion | flops 537395200 | bytes 5767172 | tf_op jit(solution)/shard_map/dot_general | solution.py:141
  115.6 2.2 %collective-permute-start.28 = (bf16[256,1024]{1,0:T(8,128)(2,1)S(1)}, bf16[256,1024]{1,0:T(8,128)(2,1)S(1)}, u32[]{:S(2)}, u32[]{:S(2)}) collective-permute-start(bf16[256,1024]{1,0:T(8,128)(2,1)S(1)} %fusion.4), channel_id=1, source_target_pairs={{0,2},{2,4},{4,6},{3,1},{5,3},{7,5},{6,7},{1,0},{8,10},{10,12},{12... | collective-permute-start | bytes 1572872 | tf_op jit(solution)/shard_map/ppermute | solution.py:163
  118.7 2.0 %collective-permute-start.24 = (bf16[128,1024]{1,0:T(8,128)(2,1)S(1)}, bf16[128,1024]{1,0:T(8,128)(2,1)S(1)}, u32[]{:S(2)}, u32[]{:S(2)}) collective-permute-start(bf16[128,1024]{1,0:T(8,128)(2,1)S(1)} %add_convert_fusion.16), channel_id=1, source_target_pairs={{0,2},{2,4},{4,6},{3,1},{5,3},{7,5},{6,7},{1,0},{8,10},{10,12},{12... | collective-permute-start | bytes 786440 | tf_op jit(solution)/shard_map/ppermute | solution.py:163
  120.7 9.3 %collective-permute-done.28.first = bf16[256,1024]{1,0:T(8,128)(2,1)S(1)} collective-permute-done((bf16[256,1024]{1,0:T(8,128)(2,1)S(1)}, bf16[256,1024]{1,0:T(8,128)(2,1)S(1)}, u32[]{:S(2)}, u32[]{:S(2)}) %collective-permute-start.28) | collective-permute-done | bytes 524320 | tf_op jit(solution)/shard_map/ppermute | solution.py:163
  130.1 2.5 %collective-permute-start.26 = (bf16[128,1024]{1,0:T(8,128)(2,1)S(1)}, bf16[128,1024]{1,0:T(8,128)(2,1)S(1)}, u32[]{:S(2)}, u32[]{:S(2)}) collective-permute-start(bf16[128,1024]{1,0:T(8,128)(2,1)S(1)} %add_convert_fusion.18), channel_id=1, source_target_pairs={{0,2},{2,4},{4,6},{3,1},{5,3},{7,5},{6,7},{1,0},{8,10},{10,12},{12... | collective-permute-start | bytes 786440 | tf_op jit(solution)/shard_map/ppermute | solution.py:163
  133.0 2.8 %shard_map.119 = (f32[512,1024]{1,0:T(8,128)}, f32[512,1024]{1,0:T(8,128)}, f32[512,1024]{1,0:T(8,128)}, f32[8,512]{1,0:T(8,128)}) custom-call(f32[1,1024]{1,0:T(1,128)S(1)} %bitcast.104, bf16[128,128]{1,0:T(8,128)(2,1)S(1)} %fusion.86.table, f32[1,2]{1,0:T(1,128)S(1)} %maximum_bitcast_fusion.kept, f32[512,1024]{1,0:T(8,128)S(1)} %convolution_add_fusion.own, ...), custom_call_target="tpu_custom_call" | custom-call | tf_op jit(solution)/shard_map/pallas_call | solution.py:64
  135.8 4.6 %collective-permute-done.26.first = bf16[128,1024]{1,0:T(8,128)(2,1)S(1)} collective-permute-done((bf16[128,1024]{1,0:T(8,128)(2,1)S(1)}, bf16[128,1024]{1,0:T(8,128)(2,1)S(1)}, u32[]{:S(2)}, u32[]{:S(2)}) %collective-permute-start.26) | collective-permute-done | bytes 262176 | tf_op jit(solution)/shard_map/ppermute | solution.py:163
  141.1 1.8 %shard_map.120 = (f32[512,1024]{1,0:T(8,128)}, f32[512,1024]{1,0:T(8,128)}, f32[512,1024]{1,0:T(8,128)}, f32[8,512]{1,0:T(8,128)}) custom-call(f32[1,1024]{1,0:T(1,128)S(1)} %bitcast.105, bf16[128,128]{1,0:T(8,128)(2,1)S(1)} %fusion.86.table, ...), custom_call_target="tpu_custom_call", output_to_operand_aliasing={{0}: (9, {}), {1}: (10, {}), {2}: (11, {}), {3}: (12, {})} | custom-call | tf_op jit(solution)/shard_map/pallas_call | solution.py:64
  143.0 1.9 %shard_map.121 = (f32[512,1024]{1,0:T(8,128)}, f32[512,1024]{1,0:T(8,128)}, f32[512,1024]{1,0:T(8,128)}, f32[8,512]{1,0:T(8,128)}) custom-call(f32[1,1024]{1,0:T(1,128)S(1)} %bitcast.106, bf16[128,128]{1,0:T(8,128)(2,1)S(1)} %fusion.86.table, ...), custom_call_target="tpu_custom_call", output_to_operand_aliasing={{0}: (9, {}), {1}: (10, {}), {2}: (11, {}), {3}: (12, {})} | custom-call | tf_op jit(solution)/shard_map/pallas_call | solution.py:64
  144.8 1.8 %add_add_fusion = f32[512,1024]{1,0:T(8,128)} fusion(f32[512,1024]{1,0:T(8,128)S(1)} %convolution_add_fusion.1, f32[512,1024]{1,0:T(8,128)S(1)} %collective-permute-done.23, bf16[256,1024]{1,0:T(8,128)(2,1)S(1)} %get-tuple-element.137, bf16[512,512]{1,0:T(8,128)(2,1)S(1)} %get-tuple-element.147), kind=kOutput, calls=%fused_computation | convolution fusion | flops 269484032 | bytes 7077888 | tf_op jit(solution)/shard_map/dot_general | solution.py:233
  (89 shorter events, 15.1 us)
Async XLA Ops:
  0.6 40.8 %collective-permute-start.12 = (bf16[512,1024]{1,0:T(8,128)(2,1)}, bf16[512,1024]{1,0:T(8,128)(2,1)}, u32[]{:S(2)}, u32[]{:S(2)}) collective-permute-start(bf16[512,1024]{1,0:T(8,128)(2,1)} %param.11), channel_id=1, source_target_pairs={{0,2},{2,4},{4,6},{3,1},{5,3},{7,5},{6,7},{1,0},{8,10},{10,12},{12... | collective-permute-start | bytes 3145736 | tf_op jit(solution)/shard_map/ppermute | solution.py:163
  5.0 6.8 %collective-permute-start = (bf16[512,256]{1,0:T(8,128)(2,1)S(1)}, bf16[512,256]{1,0:T(8,128)(2,1)S(1)}, u32[]{:S(2)}, u32[]{:S(2)}) collective-permute-start(bf16[512,256]{1,0:T(8,128)(2,1)S(1)} %get-tuple-element.72), channel_id=1, source_target_pairs={{0,1},{1,0},{2,3},{3,2},{4,5},{5,4},{6,7},{7,6},{8,9},{9,8},{10,11... | collective-permute-start | bytes 786440 | tf_op jit(solution)/shard_map/ppermute | solution.py:160
  5.0 6.6 %collective-permute-start.1 = (bf16[512,256]{1,0:T(8,128)(2,1)S(1)}, bf16[512,256]{1,0:T(8,128)(2,1)S(1)}, u32[]{:S(2)}, u32[]{:S(2)}) collective-permute-start(bf16[512,256]{1,0:T(8,128)(2,1)S(1)} %get-tuple-element.71), channel_id=1, source_target_pairs={{0,8},{1,17},{2,10},{3,19},{4,12},{5,21},{6,14},{7,23},{8,0},{9,25... | collective-permute-start | bytes 786440 | tf_op jit(solution)/shard_map/ppermute | solution.py:102
  6.6 6.6 %collective-permute-start.5 = (bf16[512,256]{1,0:T(8,128)(2,1)S(1)}, bf16[512,256]{1,0:T(8,128)(2,1)S(1)}, u32[]{:S(2)}, u32[]{:S(2)}) collective-permute-start(bf16[512,256]{1,0:T(8,128)(2,1)S(1)} %get-tuple-element.74), channel_id=1, source_target_pairs={{0,1},{1,0},{2,3},{3,2},{4,5},{5,4},{6,7},{7,6},{8,9},{9,8},{10,11... | collective-permute-start | bytes 786440 | tf_op jit(solution)/shard_map/ppermute | solution.py:160
  6.8 7.5 %collective-permute-start.6 = (bf16[512,256]{1,0:T(8,128)(2,1)S(1)}, bf16[512,256]{1,0:T(8,128)(2,1)S(1)}, u32[]{:S(2)}, u32[]{:S(2)}) collective-permute-start(bf16[512,256]{1,0:T(8,128)(2,1)S(1)} %get-tuple-element.73), channel_id=1, source_target_pairs={{0,8},{1,17},{2,10},{3,19},{4,12},{5,21},{6,14},{7,23},{8,0},{9,25... | collective-permute-start | bytes 786440 | tf_op jit(solution)/shard_map/ppermute | solution.py:102
  8.3 3.0 %copy-start.5 = (s32[1024]{0:T(1024)S(1)}, s32[1024]{0:T(1024)}, u32[]{:S(2)}) copy-start(s32[1024]{0:T(1024)} %param.12) | copy-start | bytes 12292
  8.3 3.5 %copy-start.3 = (bf16[512,1024]{1,0:T(8,128)(2,1)S(1)}, bf16[512,1024]{1,0:T(8,128)(2,1)}, u32[]{:S(2)}) copy-start(bf16[512,1024]{1,0:T(8,128)(2,1)} %param.9) | copy-start | bytes 3145732
  11.7 31.8 %collective-permute-start.14 = (bf16[512,1024]{1,0:T(8,128)(2,1)}, bf16[512,1024]{1,0:T(8,128)(2,1)S(1)}, u32[]{:S(2)}, u32[]{:S(2)}) collective-permute-start(bf16[512,1024]{1,0:T(8,128)(2,1)} %param.11), channel_id=1, source_target_pairs={{1,3},{3,5},{5,7},{2,0},{4,2},{6,4},{7,6},{0,1},{9,11},{11,13},{13... | collective-permute-start | bytes 3145736 | tf_op jit(solution)/shard_map/ppermute | solution.py:163
  11.8 29.1 %collective-permute-start.13 = (bf16[512,1024]{1,0:T(8,128)(2,1)S(1)}, bf16[512,1024]{1,0:T(8,128)(2,1)S(1)}, u32[]{:S(2)}, u32[]{:S(2)}) collective-permute-start(bf16[512,1024]{1,0:T(8,128)(2,1)S(1)} %copy-done.3), channel_id=1, source_target_pairs={{0,1},{1,0},{2,3},{3,2},{4,5},{5,4},{6,7},{7,6},{8,9},{9,8},{10,11... | collective-permute-start | bytes 3145736 | tf_op jit(solution)/shard_map/ppermute | solution.py:160
  13.2 6.4 %collective-permute-start.2 = (bf16[512,256]{1,0:T(8,128)(2,1)S(1)}, bf16[512,256]{1,0:T(8,128)(2,1)S(1)}, u32[]{:S(2)}, u32[]{:S(2)}) collective-permute-start(bf16[512,256]{1,0:T(8,128)(2,1)S(1)} %collective-permute-done), channel_id=1, source_target_pairs={{0,16},{1,9},{2,18},{3,11},{4,20},{5,13},{6,22},{7,15},{8,24},{9,1... | collective-permute-start | bytes 786440 | tf_op jit(solution)/shard_map/ppermute | solution.py:102
  14.3 8.1 %collective-permute-start.7 = (bf16[512,256]{1,0:T(8,128)(2,1)S(1)}, bf16[512,256]{1,0:T(8,128)(2,1)S(1)}, u32[]{:S(2)}, u32[]{:S(2)}) collective-permute-start(bf16[512,256]{1,0:T(8,128)(2,1)S(1)} %collective-permute-done.5), channel_id=1, source_target_pairs={{0,16},{1,9},{2,18},{3,11},{4,20},{5,13},{6,22},{7,15},{8,24},{9,1... | collective-permute-start | bytes 786440 | tf_op jit(solution)/shard_map/ppermute | solution.py:102
  19.6 10.8 %collective-permute-start.4 = (bf16[512,256]{1,0:T(8,128)(2,1)S(1)}, bf16[512,256]{1,0:T(8,128)(2,1)S(1)}, u32[]{:S(2)}, u32[]{:S(2)}) collective-permute-start(bf16[512,256]{1,0:T(8,128)(2,1)S(1)} %broadcast_select_fusion.4), channel_id=1, source_target_pairs={{0,16},{1,9},{2,18},{3,11},{4,20},{5,13},{6,22},{7,15},{8,24},{9,1... | collective-permute-start | bytes 786440 | tf_op jit(solution)/shard_map/ppermute | solution.py:102
  22.4 6.4 %collective-permute-start.3 = (bf16[512,256]{1,0:T(8,128)(2,1)S(1)}, bf16[512,256]{1,0:T(8,128)(2,1)S(1)}, u32[]{:S(2)}, u32[]{:S(2)}) collective-permute-start(bf16[512,256]{1,0:T(8,128)(2,1)S(1)} %broadcast_select_fusion.5), channel_id=1, source_target_pairs={{0,8},{1,17},{2,10},{3,19},{4,12},{5,21},{6,14},{7,23},{8,0},{9,25... | collective-permute-start | bytes 786440 | tf_op jit(solution)/shard_map/ppermute | solution.py:102
  28.7 10.0 %collective-permute-start.9 = (bf16[512,256]{1,0:T(8,128)(2,1)S(1)}, bf16[512,256]{1,0:T(8,128)(2,1)S(1)}, u32[]{:S(2)}, u32[]{:S(2)}) collective-permute-start(bf16[512,256]{1,0:T(8,128)(2,1)S(1)} %broadcast_select_fusion.2), channel_id=1, source_target_pairs={{0,16},{1,9},{2,18},{3,11},{4,20},{5,13},{6,22},{7,15},{8,24},{9,1... | collective-permute-start | bytes 786440 | tf_op jit(solution)/shard_map/ppermute | solution.py:102
  30.4 6.7 %collective-permute-start.8 = (bf16[512,256]{1,0:T(8,128)(2,1)S(1)}, bf16[512,256]{1,0:T(8,128)(2,1)S(1)}, u32[]{:S(2)}, u32[]{:S(2)}) collective-permute-start(bf16[512,256]{1,0:T(8,128)(2,1)S(1)} %broadcast_select_fusion.3), channel_id=1, source_target_pairs={{0,8},{1,17},{2,10},{3,19},{4,12},{5,21},{6,14},{7,23},{8,0},{9,25... | collective-permute-start | bytes 786440 | tf_op jit(solution)/shard_map/ppermute | solution.py:102
  37.1 15.3 %collective-permute-start.11 = (bf16[512,512]{1,0:T(8,128)(2,1)S(1)}, bf16[512,512]{1,0:T(8,128)(2,1)S(1)}, u32[]{:S(2)}, u32[]{:S(2)}) collective-permute-start(bf16[512,512]{1,0:T(8,128)(2,1)S(1)} %maximum_select_fusion.1), channel_id=1, source_target_pairs={{0,16},{1,9},{2,18},{3,11},{4,20},{5,13},{6,22},{7,15},{8,24},{9,1... | collective-permute-start | bytes 1572872 | tf_op jit(solution)/shard_map/ppermute | solution.py:102
  38.7 12.8 %collective-permute-start.10 = (bf16[512,512]{1,0:T(8,128)(2,1)S(1)}, bf16[512,512]{1,0:T(8,128)(2,1)S(1)}, u32[]{:S(2)}, u32[]{:S(2)}) collective-permute-start(bf16[512,512]{1,0:T(8,128)(2,1)S(1)} %maximum_select_fusion), channel_id=1, source_target_pairs={{0,8},{1,17},{2,10},{3,19},{4,12},{5,21},{6,14},{7,23},{8,0},{9,25... | collective-permute-start | bytes 1572872 | tf_op jit(solution)/shard_map/ppermute | solution.py:102
  43.5 3.9 %slice-start = ((s8[8388608]{0:T(1024)(128)(4,1)}), s8[4194304]{0:T(1024)(128)(4,1)S(1)}, s32[]{:S(2)}) async-start(s8[8388608]{0:T(1024)(128)(4,1)} %bitcast.107), calls=%async_computation | async-start | bytes 8388608
  44.5 2.9 %slice-start.1 = ((s8[8388608]{0:T(1024)(128)(4,1)}), s8[4194304]{0:T(1024)(128)(4,1)S(1)}, s32[]{:S(2)}) async-start(s8[8388608]{0:T(1024)(128)(4,1)} %bitcast.107), calls=%async_computation.1 | async-start | bytes 8388608
  46.8 1.4 copy-start.4
  55.0 25.4 %collective-permute-start.17 = (bf16[256,1024]{1,0:T(8,128)(2,1)S(1)}, bf16[256,1024]{1,0:T(8,128)(2,1)S(1)}, u32[]{:S(2)}, u32[]{:S(2)}) collective-permute-start(bf16[256,1024]{1,0:T(8,128)(2,1)S(1)} %add_convert_fusion.12), channel_id=1, source_target_pairs={{0,2},{2,4},{4,6},{3,1},{5,3},{7,5},{6,7},{1,0},{8,10},{10,12},{12... | collective-permute-start | bytes 1572872 | tf_op jit(solution)/shard_map/ppermute | solution.py:163
  56.6 24.0 %collective-permute-start.18 = (bf16[256,1024]{1,0:T(8,128)(2,1)S(1)}, bf16[256,1024]{1,0:T(8,128)(2,1)S(1)}, u32[]{:S(2)}, u32[]{:S(2)}) collective-permute-start(bf16[256,1024]{1,0:T(8,128)(2,1)S(1)} %add_convert_fusion.11), channel_id=1, source_target_pairs={{1,3},{3,5},{5,7},{2,0},{4,2},{6,4},{7,6},{0,1},{9,11},{11,13},{13... | collective-permute-start | bytes 1572872 | tf_op jit(solution)/shard_map/ppermute | solution.py:163
  60.3 19.2 %collective-permute-start.15 = (bf16[256,1024]{1,0:T(8,128)(2,1)S(1)}, bf16[256,1024]{1,0:T(8,128)(2,1)S(1)}, u32[]{:S(2)}, u32[]{:S(2)}) collective-permute-start(bf16[256,1024]{1,0:T(8,128)(2,1)S(1)} %add_convert_fusion.14), channel_id=1, source_target_pairs={{0,2},{2,4},{4,6},{3,1},{5,3},{7,5},{6,7},{1,0},{8,10},{10,12},{12... | collective-permute-start | bytes 1572872 | tf_op jit(solution)/shard_map/ppermute | solution.py:163
  65.9 14.3 %collective-permute-start.16 = (bf16[256,1024]{1,0:T(8,128)(2,1)S(1)}, bf16[256,1024]{1,0:T(8,128)(2,1)S(1)}, u32[]{:S(2)}, u32[]{:S(2)}) collective-permute-start(bf16[256,1024]{1,0:T(8,128)(2,1)S(1)} %add_convert_fusion.13), channel_id=1, source_target_pairs={{1,3},{3,5},{5,7},{2,0},{4,2},{6,4},{7,6},{0,1},{9,11},{11,13},{13... | collective-permute-start | bytes 1572872 | tf_op jit(solution)/shard_map/ppermute | solution.py:163
  81.4 20.7 %collective-permute-start.21 = (bf16[256,1024]{1,0:T(8,128)(2,1)S(1)}, bf16[256,1024]{1,0:T(8,128)(2,1)S(1)}, u32[]{:S(2)}, u32[]{:S(2)}) collective-permute-start(bf16[256,1024]{1,0:T(8,128)(2,1)S(1)} %add_convert_fusion.9), channel_id=1, source_target_pairs={{0,2},{2,4},{4,6},{3,1},{5,3},{7,5},{6,7},{1,0},{8,10},{10,12},{12... | collective-permute-start | bytes 1572872 | tf_op jit(solution)/shard_map/ppermute | solution.py:163
  85.1 16.7 %collective-permute-start.19 = (bf16[256,1024]{1,0:T(8,128)(2,1)S(1)}, bf16[256,1024]{1,0:T(8,128)(2,1)S(1)}, u32[]{:S(2)}, u32[]{:S(2)}) collective-permute-start(bf16[256,1024]{1,0:T(8,128)(2,1)S(1)} %fusion.5), channel_id=1, source_target_pairs={{0,2},{2,4},{4,6},{3,1},{5,3},{7,5},{6,7},{1,0},{8,10},{10,12},{12... | collective-permute-start | bytes 1572872 | tf_op jit(solution)/shard_map/ppermute | solution.py:163
  89.9 12.1 %collective-permute-start.20 = (bf16[256,1024]{1,0:T(8,128)(2,1)S(1)}, bf16[256,1024]{1,0:T(8,128)(2,1)S(1)}, u32[]{:S(2)}, u32[]{:S(2)}) collective-permute-start(bf16[256,1024]{1,0:T(8,128)(2,1)S(1)} %add_convert_fusion.10), channel_id=1, source_target_pairs={{1,3},{3,5},{5,7},{2,0},{4,2},{6,4},{7,6},{0,1},{9,11},{11,13},{13... | collective-permute-start | bytes 1572872 | tf_op jit(solution)/shard_map/ppermute | solution.py:163
  89.9 16.0 %collective-permute-start.22 = (bf16[256,1024]{1,0:T(8,128)(2,1)S(1)}, bf16[256,1024]{1,0:T(8,128)(2,1)S(1)}, u32[]{:S(2)}, u32[]{:S(2)}) collective-permute-start(bf16[256,1024]{1,0:T(8,128)(2,1)S(1)} %add_convert_fusion.8), channel_id=1, source_target_pairs={{1,3},{3,5},{5,7},{2,0},{4,2},{6,4},{7,6},{0,1},{9,11},{11,13},{13... | collective-permute-start | bytes 1572872 | tf_op jit(solution)/shard_map/ppermute | solution.py:163
  111.7 33.1 %collective-permute-start.23 = (f32[512,1024]{1,0:T(8,128)S(1)}, f32[512,1024]{1,0:T(8,128)S(1)}, u32[]{:S(2)}, u32[]{:S(2)}) collective-permute-start(f32[512,1024]{1,0:T(8,128)S(1)} %add_add_fusion.1), channel_id=1, source_target_pairs={{0,1},{1,0},{2,3},{3,2},{4,5},{5,4},{6,7},{7,6},{8,9},{9,8},{10,11... | collective-permute-start | bytes 6291464 | tf_op jit(solution)/shard_map/ppermute | solution.py:160
  115.6 14.5 %collective-permute-start.28 = (bf16[256,1024]{1,0:T(8,128)(2,1)S(1)}, bf16[256,1024]{1,0:T(8,128)(2,1)S(1)}, u32[]{:S(2)}, u32[]{:S(2)}) collective-permute-start(bf16[256,1024]{1,0:T(8,128)(2,1)S(1)} %fusion.4), channel_id=1, source_target_pairs={{0,2},{2,4},{4,6},{3,1},{5,3},{7,5},{6,7},{1,0},{8,10},{10,12},{12... | collective-permute-start | bytes 1572872 | tf_op jit(solution)/shard_map/ppermute | solution.py:163
  117.8 14.8 %collective-permute-start.29 = (bf16[256,1024]{1,0:T(8,128)(2,1)S(1)}, bf16[256,1024]{1,0:T(8,128)(2,1)S(1)}, u32[]{:S(2)}, u32[]{:S(2)}) collective-permute-start(bf16[256,1024]{1,0:T(8,128)(2,1)S(1)} %add_convert_fusion.5), channel_id=1, source_target_pairs={{1,3},{3,5},{5,7},{2,0},{4,2},{6,4},{7,6},{0,1},{9,11},{11,13},{13... | collective-permute-start | bytes 1572872 | tf_op jit(solution)/shard_map/ppermute | solution.py:163
  118.2 14.8 %copy-start.2 = (f32[512,1024]{1,0:T(8,128)S(1)}, f32[512,1024]{1,0:T(8,128)}, u32[]{:S(2)}) copy-start(f32[512,1024]{1,0:T(8,128)} %variance.5) | copy-start | bytes 6291460
  118.7 14.4 %copy-start = (f32[512,1024]{1,0:T(8,128)S(1)}, f32[512,1024]{1,0:T(8,128)}, u32[]{:S(2)}) copy-start(f32[512,1024]{1,0:T(8,128)} %master.5) | copy-start | bytes 6291460
  118.7 14.3 %copy-start.1 = (f32[512,1024]{1,0:T(8,128)S(1)}, f32[512,1024]{1,0:T(8,128)}, u32[]{:S(2)}) copy-start(f32[512,1024]{1,0:T(8,128)} %moment.5) | copy-start | bytes 6291460
  118.7 24.3 %collective-permute-start.24 = (bf16[128,1024]{1,0:T(8,128)(2,1)S(1)}, bf16[128,1024]{1,0:T(8,128)(2,1)S(1)}, u32[]{:S(2)}, u32[]{:S(2)}) collective-permute-start(bf16[128,1024]{1,0:T(8,128)(2,1)S(1)} %add_convert_fusion.16), channel_id=1, source_target_pairs={{0,2},{2,4},{4,6},{3,1},{5,3},{7,5},{6,7},{1,0},{8,10},{10,12},{12... | collective-permute-start | bytes 786440 | tf_op jit(solution)/shard_map/ppermute | solution.py:163
  120.7 22.2 %collective-permute-start.25 = (bf16[128,1024]{1,0:T(8,128)(2,1)S(1)}, bf16[128,1024]{1,0:T(8,128)(2,1)S(1)}, u32[]{:S(2)}, u32[]{:S(2)}) collective-permute-start(bf16[128,1024]{1,0:T(8,128)(2,1)S(1)} %add_convert_fusion.15), channel_id=1, source_target_pairs={{1,3},{3,5},{5,7},{2,0},{4,2},{6,4},{7,6},{0,1},{9,11},{11,13},{13... | collective-permute-start | bytes 786440 | tf_op jit(solution)/shard_map/ppermute | solution.py:163
  130.1 10.3 %collective-permute-start.26 = (bf16[128,1024]{1,0:T(8,128)(2,1)S(1)}, bf16[128,1024]{1,0:T(8,128)(2,1)S(1)}, u32[]{:S(2)}, u32[]{:S(2)}) collective-permute-start(bf16[128,1024]{1,0:T(8,128)(2,1)S(1)} %add_convert_fusion.18), channel_id=1, source_target_pairs={{0,2},{2,4},{4,6},{3,1},{5,3},{7,5},{6,7},{1,0},{8,10},{10,12},{12... | collective-permute-start | bytes 786440 | tf_op jit(solution)/shard_map/ppermute | solution.py:163
  132.6 8.5 %collective-permute-start.27 = (bf16[128,1024]{1,0:T(8,128)(2,1)S(1)}, bf16[128,1024]{1,0:T(8,128)(2,1)S(1)}, u32[]{:S(2)}, u32[]{:S(2)}) collective-permute-start(bf16[128,1024]{1,0:T(8,128)(2,1)S(1)} %add_convert_fusion.17), channel_id=1, source_target_pairs={{1,3},{3,5},{5,7},{2,0},{4,2},{6,4},{7,6},{0,1},{9,11},{11,13},{13... | collective-permute-start | bytes 786440 | tf_op jit(solution)/shard_map/ppermute | solution.py:163
